TPU v7x, 32 devices: a whole 2x2x4 slice. The times are simulated.
32 devices in a mesh: gx: 4 (over z), gy: 8 (over y, x, core).
Axes of the slice: x: 2, y: 2, z: 4, core: 2. Of those that a mesh axis runs over, the one named last changes fastest.
Arguments:
- tprime: float32 [256, 256, 128], P('gx', 'gy'), may hold values from -5 to 5
- vapor: float32 [256, 256, 128], P('gx', 'gy'), may hold values from -0.2 to 0.2
- wind_u: float32 [256, 256, 128], P('gx', 'gy'), may hold values from -2.5 to 2.5
- wind_v: float32 [256, 256, 128], P('gx', 'gy'), may hold values from -2.5 to 2.5
- wind_w: float32 [256, 256, 128], P('gx', 'gy'), may hold values from -2.5 to 2.5
- radius: float32 [32768, 128], P(('gx', 'gy')), may hold values from 4 to 20
- min_radius: float32 [32768, 128], P(('gx', 'gy')), may hold values from 1 to 4
- multiplicity: float32 [32768, 128], P(('gx', 'gy')), may hold values from 0.5 to 2
- drop_counts: int32 [32768], P(('gx', 'gy')), may hold values from 0 to 128, as said below
- cell_index: int32 [32768], P(('gx', 'gy')), may hold values from 0 to 262143
- move_list: int32 [32768], P(('gx', 'gy')), may hold values from -1 to 1023, as said below
Outputs:
- temperature_out: float32 [256, 256, 128], P('gx', 'gy')
- vapor_out: float32 [256, 256, 128], P('gx', 'gy')
- radius_out: float32 [16384, 128], P(('gx', 'gy'))
- multiplicity_out: float32 [16384, 128], P(('gx', 'gy'))
Inputs may be any that keep to these rules, and one draw needn't show every extreme that they name: `move_list`: each entry is -1 for an empty home slot, else o * 32 + k: the block goes to owner o as the k-th block from its device to o. Within one device no value repeats, every owner receives exactly 512 blocks, some device holds 1024 live blocks and uses k = 31. `drop_counts`: 0 exactly in the home slots whose move_list entry is -1, else 1 to 128.
All inputs are finite; a program needn't handle non-finite values.
Results may differ from a plain program's by a relative error of at most 0.0003.
Values sent between devices are 32-bit elements; how exact they have to be, the bound alone decides.
No kernel may reach another device: no remote copies, remote signals or barrier semaphores. Data moves between devices by JAX's collectives and lax.ppermute only.
A program may use at most 64 MiB of HBM per device.

v0:
```python
import jax
import jax.numpy as jnp
from jax import lax
from jax.experimental import pallas as pl
from jax.experimental.pallas import tpu as pltpu
from jax.sharding import PartitionSpec as P

SUBSTEPS = 6
BLK_DEV = 512
LAN = 128
SUB = 8
NV = 16
collect = 1e-07
time_step = 2.0
advect_step = 0.6
clausius = 0.07; growth = 200.0 / 3.0; solute = 0.05; condense = 5e-07; latent = 10.0
SMEM=lambda: pl.BlockSpec(memory_space=pltpu.SMEM)
VM=lambda: pl.BlockSpec(memory_space=pltpu.VMEM)

def row_loop(n, unroll, fn):
    def group(g,_):
        base=pl.multiple_of(g*unroll,unroll)
        for u in range(unroll):
            fn(base+u)
        return 0
    lax.fori_loop(0,n//unroll,group,0)

def place_kernel(move,count,mult,out,buf):
    n=mult.shape[0]
    buf[...]=jnp.zeros_like(buf)
    lane=lax.broadcasted_iota(jnp.int32,(1,LAN),1)
    def one(b):
        slot=move[b]
        dst=jnp.where(slot>=0,slot,n)
        buf[pl.ds(dst,1),:]=jnp.where(lane<count[b],mult[pl.ds(b,1),:],0.0)
    row_loop(n,8,one)
    out[...]=buf[:n,:]

def place(move,count,mult):
    n=mult.shape[0]
    return pl.pallas_call(place_kernel,out_shape=jax.ShapeDtypeStruct(mult.shape,jnp.float32),
        in_specs=[SMEM(),SMEM(),VM()],out_specs=VM(),
        scratch_shapes=[pltpu.VMEM((n+SUB,LAN),jnp.float32)],name="place")(move,count,mult)

def home_kernel(move,cell,count,level,radius,floor,mult,tp,vp,send,ht,hv,ct,cv,rows_t,rows_v,buf):
    n=radius.shape[0]
    def fetch(b):
        c=lax.shift_right_logical(cell[b],7)
        rows_t[pl.ds(b,1),:]=tp[pl.ds(c,1),:]
        rows_v[pl.ds(b,1),:]=vp[pl.ds(c,1),:]
    row_loop(n,8,fetch)
    depth=lax.broadcasted_iota(jnp.int32,(LAN,LAN),0)
    def tile(t,_):
        sl=pl.ds(pl.multiple_of(t*LAN,LAN),LAN)
        here=depth==level[pl.ds(t,1),:]
        temp0=jnp.sum(jnp.where(here,jnp.transpose(rows_t[sl,:]),0.0),axis=0,keepdims=True)
        wet0=jnp.sum(jnp.where(here,jnp.transpose(rows_v[sl,:]),0.0),axis=0,keepdims=True)
        r=jnp.transpose(radius[sl,:]); fl=jnp.transpose(floor[sl,:])
        m=jnp.where(depth<count[pl.ds(t,1),:],jnp.transpose(mult[sl,:]),0.0)
        r2=r*r; f2=fl*fl; g3=(growth*solute)*(f2*fl)
        inv=lax.rsqrt(r2); mass=r2*(r2*inv)
        temp=temp0; wet=wet0
        for k in range(SUBSTEPS):
            sat=(1.0+wet)*jnp.exp(-clausius*temp)-1.0
            grown=jnp.maximum(r2+(growth*sat+g3*(inv*inv*inv)),f2)
            inv=lax.rsqrt(grown)
            new=grown*(grown*inv)
            condensed=jnp.sum(m*(new-mass),axis=0,keepdims=True)
            wet=wet-condense*condensed
            temp=temp+latent*condense*condensed
            r2=grown; mass=new
        ht[pl.ds(t,1),:]=temp-temp0; hv[pl.ds(t,1),:]=wet-wet0
        ct[pl.ds(t,1),:]=temp0; cv[pl.ds(t,1),:]=wet0
        rows_t[sl,:]=jnp.transpose(r2)
        return 0
    lax.fori_loop(0,n//LAN,tile,0)
    buf[...]=jnp.zeros_like(buf)
    def put(b):
        slot=move[b]
        dst=jnp.where(slot>=0,slot,n)
        buf[pl.ds(dst,1),:]=rows_t[pl.ds(b,1),:]
    row_loop(n,8,put)
    send[...]=buf[:n,:]

def home(move,cell,count,radius,floor,mult,tp,vp):
    n=radius.shape[0]; g=n//LAN
    levels=tp.shape[-1]
    tab=jax.ShapeDtypeStruct((g,LAN),jnp.float32)
    return pl.pallas_call(home_kernel,
        out_shape=(jax.ShapeDtypeStruct(radius.shape,jnp.float32),tab,tab,tab,tab),
        in_specs=[SMEM(),SMEM()]+[VM()]*7,out_specs=(VM(),)*5,
        scratch_shapes=[pltpu.VMEM((n,LAN),jnp.float32),pltpu.VMEM((n,LAN),jnp.float32),pltpu.VMEM((n+SUB,LAN),jnp.float32)],
        name="home")(move,cell,count.reshape(g,LAN),(cell%levels).reshape(g,LAN),radius,floor,mult,
                     tp.reshape(-1,levels),vp.reshape(-1,levels))

def scatter_kernel(cell,cellv,ht,hv,ct,cv,tp,vp,ot,ov,vt,vv,acct,accv):
    g=cellv.shape[0]; n=g*LAN
    spread=lambda ref,t: jnp.transpose(jnp.broadcast_to(ref[pl.ds(t,1),:],(LAN,LAN)))
    acct[...]=jnp.zeros_like(acct); accv[...]=jnp.zeros_like(accv)
    def source(t,_):
        c=spread(cellv,t); a=spread(ht,t); b=spread(hv,t)
        for o in range(g):
            mine=cellv[o:o+1,:]
            st=jnp.zeros((SUB,LAN),jnp.float32); sv=st
            for k in range(LAN//SUB):
                same=c[k*SUB:(k+1)*SUB,:]==mine
                st=st+jnp.where(same,a[k*SUB:(k+1)*SUB,:],0.0)
                sv=sv+jnp.where(same,b[k*SUB:(k+1)*SUB,:],0.0)
            acct[o*SUB:(o+1)*SUB,:]+=st
            accv[o*SUB:(o+1)*SUB,:]+=sv
        return 0
    lax.fori_loop(0,g,source,0)
    def rows(t,_):
        sl=pl.ds(pl.multiple_of(t*LAN,LAN),LAN)
        s8=pl.ds(pl.multiple_of(t*SUB,SUB),SUB)
        nt=ct[pl.ds(t,1),:]+jnp.sum(acct[s8,:],axis=0,keepdims=True)
        nv=cv[pl.ds(t,1),:]+jnp.sum(accv[s8,:],axis=0,keepdims=True)
        vt[sl,:]=jnp.transpose(jnp.broadcast_to(nt,(LAN,LAN)))
        vv[sl,:]=jnp.transpose(jnp.broadcast_to(nv,(LAN,LAN)))
        return 0
    lax.fori_loop(0,g,rows,0)
    ot[...]=tp[...]; ov[...]=vp[...]
    lane=lax.broadcasted_iota(jnp.int32,(1,LAN),1)
    def put(b):
        x=cell[b]
        c=lax.shift_right_logical(x,7); hit=lane==(x&127)
        pltpu.store(ot.at[pl.ds(c,1),:],vt[pl.ds(b,1),:],mask=hit)
        pltpu.store(ov.at[pl.ds(c,1),:],vv[pl.ds(b,1),:],mask=hit)
    row_loop(n,8,put)

def scatter(cell,ht,hv,ct,cv,tp,vp):
    g=ht.shape[0]; n=g*LAN
    t2=tp.reshape(-1,LAN); v2=vp.reshape(-1,LAN)
    o=jax.ShapeDtypeStruct(t2.shape,jnp.float32)
    a,b=pl.pallas_call(scatter_kernel,out_shape=(o,o),in_specs=[SMEM()]+[VM()]*7,out_specs=(VM(),VM()),
        scratch_shapes=[pltpu.VMEM((n,LAN),jnp.float32)]*2+[pltpu.VMEM((g*SUB,LAN),jnp.float32)]*2,
        name="scatter")(cell,cell.reshape(g,LAN).astype(jnp.float32),ht,hv,ct,cv,t2,v2)
    return a.reshape(tp.shape),b.reshape(vp.shape)


def batcher(n):
    out=[]
    p=1
    while p<n:
        k=p
        while k>=1:
            for j in range(k%p, n-k, 2*k):
                for i in range(0, min(k, n-j-k)):
                    if (i+j)//(p*2)==(i+j+k)//(p*2):
                        out.append((i+j,i+j+k))
            k//=2
        p*=2
    return out
NET16=batcher(16)

def swap(keys, pays, a, b):
    c = keys[a] > keys[b]
    keys[a], keys[b] = jnp.where(c, keys[b], keys[a]), jnp.where(c, keys[a], keys[b])
    for p in pays:
        p[a], p[b] = jnp.where(c, p[b], p[a]), jnp.where(c, p[a], p[b])

def swap_min(keys, a, b):
    keys[a], keys[b] = jnp.minimum(keys[a], keys[b]), jnp.maximum(keys[a], keys[b])

def partner(x, j, upper):
    if j == 4:
        return pltpu.roll(x, 4, 0)
    return jnp.where(upper, pltpu.roll(x, j, 0), pltpu.roll(x, 8 - j, 0))

def sort128(keys, pays, row, flip):
    bit=[(row & 1) != 0, (row & 2) != 0, (row & 4) != 0]
    def flipped(mask):
        for v in range(NV):
            keys[v] = jnp.where(mask, flip(keys[v]), keys[v])
    flipped(bit[0])
    for a,b in NET16:
        swap(keys,pays,a,b) if pays else swap_min(keys,a,b)
    for lvl in range(3):
        nxt = bit[lvl+1] if lvl < 2 else None
        flipped(jnp.logical_xor(bit[lvl], nxt) if nxt is not None else bit[lvl])
        for s in range(lvl,-1,-1):
            j=1<<s; up=bit[s]
            for v in range(NV):
                pk=partner(keys[v],j,up)
                if pays:
                    c=jnp.logical_xor(keys[v]>pk, up)
                    keys[v]=jnp.where(c,pk,keys[v])
                    for p in pays:
                        p[v]=jnp.where(c,partner(p[v],j,up),p[v])
                else:
                    keys[v]=jnp.where(up, jnp.maximum(keys[v],pk), jnp.minimum(keys[v],pk))
        for d in (8,4,2,1):
            for a in range(NV):
                if a & d == 0:
                    swap(keys,pays,a,a|d) if pays else swap_min(keys,a,a|d)

def before(parts, row):
    run=None; excl=[]
    for x in parts:
        excl.append(run)
        run = x if run is None else run + x
    x=run
    for j in (1,2,4):
        x = x + jnp.where(row >= j, pltpu.roll(x, j, 0), 0.0)
    ahead = jnp.where(row >= 1, pltpu.roll(x, 1, 0), 0.0)
    total = jnp.sum(run, axis=0, keepdims=True)
    return [ahead if e is None else ahead + e for e in excl], total

def collect_tile(r2t, mt):
    row = lax.broadcasted_iota(jnp.int32,(SUB,LAN),0)
    keys=[]; m=[]
    for v in range(NV):
        q = row*16+v
        x = r2t[v*8:(v+1)*8,:]
        keys.append((x*16384.0).astype(jnp.int32)*128+q)
        m.append(mt[v*8:(v+1)*8,:])
    sort128(keys,[m],row,lambda k: -1-k)
    q=[k & 127 for k in keys]
    r2=[(lax.shift_right_logical(k,7)).astype(jnp.float32)*(1.0/16384.0) + (0.5/16384.0) for k in keys]
    rad=[jnp.sqrt(x) for x in r2]
    r3=[a*b for a,b in zip(r2,rad)]
    r4=[a*a for a in r2]
    m1=[a*b for a,b in zip(m,rad)]
    m3=[a*b for a,b in zip(m,r3)]
    m4=[a*b for a,b in zip(m,r4)]
    m6=[a*b for a,b in zip(m3,r3)]
    m7=[a*b for a,b in zip(m3,r4)]
    p0,t0=before(m,row); p1,t1=before(m1,row)
    p3,t3=before(m3,row); p4,t4=before(m4,row)
    p6,_=before(m6,row); p7,_=before(m7,row)
    outs_r=[]; outs_m=[]; key2=[]
    for v in range(NV):
        gain = collect*((r4[v]*p3[v]-p7[v]) + 2.0*(r3[v]*p4[v]-rad[v]*p6[v]))
        loss = collect*(((t4-p4[v]) - r4[v]*(t0-p0[v])) + 2.0*(rad[v]*(t3-p3[v]) - r3[v]*(t1-p1[v])))
        x = r3[v] + time_step*gain
        y = jnp.exp(jnp.log(x)*(1.0/3.0))
        y = y - (y*y*y - x)/(3.0*y*y)
        outs_r.append(jnp.where(m[v]>0.0, y, 0.0))
        outs_m.append(m[v]*jnp.exp(-time_step*loss))
        key2.append((q[v]*128 + (row + v*8)).astype(jnp.float32))
    sort128(key2,[],row,lambda k: -k)
    rank=[(key2[v]-(row*16+v).astype(jnp.float32)*128.0) for v in range(NV)]
    cat=lambda l: jnp.concatenate(l,axis=0)
    return cat(outs_r),cat(outs_m),cat(rank)


def receive_kernel(src, mults, r2s, ro_ref, mo_ref, mrow, rrow):
    blocks = ro_ref.shape[0]

    def pull(b):
        s = src[b]
        mrow[pl.ds(b, 1), :] = mults[pl.ds(s, 1), :]
        rrow[pl.ds(b, 1), :] = r2s[pl.ds(s, 1), :]

    row_loop(blocks, 8, pull)

    def tile(t, _):
        sl = pl.ds(pl.multiple_of(t * LAN, LAN), LAN)
        a, b, rank = collect_tile(jnp.transpose(rrow[sl, :]), jnp.transpose(mrow[sl, :]))
        rank = jnp.transpose(rank).astype(jnp.int32)
        ro_ref[sl, :] = jnp.take_along_axis(jnp.transpose(a), rank, axis=1)
        mo_ref[sl, :] = jnp.take_along_axis(jnp.transpose(b), rank, axis=1)
        return 0

    lax.fori_loop(0, blocks // LAN, tile, 0)


def receive(src, mults, r2s):
    out = jax.ShapeDtypeStruct((BLK_DEV, LAN), jnp.float32)
    return pl.pallas_call(
        receive_kernel,
        out_shape=(out, out),
        in_specs=[SMEM(), VM(), VM()],
        out_specs=(VM(), VM()),
        scratch_shapes=[pltpu.VMEM((BLK_DEV, LAN), jnp.float32)] * 2,
        name="receive",
    )(src, mults, r2s)


def sources(mults):
    taken = mults[:, 0] > 0.0
    position = jnp.cumsum(taken.astype(jnp.int32)) - 1
    hit = (position[None, :] == jnp.arange(BLK_DEV, dtype=jnp.int32)[:, None]) & taken[None, :]
    return jnp.sum(jnp.where(hit, jnp.arange(mults.shape[0], dtype=jnp.int32)[None, :], 0), axis=1)


def exchange(rows, devices):
    moved = lax.all_to_all(
        rows.reshape((devices, -1) + rows.shape[1:]), ("gx", "gy"), 0, 0, tiled=True
    )
    return moved.reshape(rows.shape)


def with_halo(array, sides, width):
    for axis, dim in sides:
        size, length = (lax.axis_size(axis), array.shape[dim])
        up = [(i, (i + 1) % size) for i in range(size)]
        down = [(j, i) for i, j in up]
        last = lax.slice_in_dim(array, length - width, length, axis=dim)
        first = lax.slice_in_dim(array, 0, width, axis=dim)
        before_ = lax.ppermute(last, axis, up)
        after_ = lax.ppermute(first, axis, down)
        array = jnp.concatenate([before_, array, after_], axis=dim)
    return array


def tendency(padded, along_x, along_y, along_z):
    middle_y = padded[:, :, 1:-1]
    flux_x = along_x * (0.5 * (middle_y[:, :-1] + middle_y[:, 1:]))
    middle_x = padded[:, 1:-1]
    flux_y = along_y * (0.5 * (middle_x[:, :, :-1] + middle_x[:, :, 1:]))
    core = padded[:, 1:-1, 1:-1]
    flux_z = along_z * (0.5 * (core[..., :-1] + core[..., 1:]))
    edge = jnp.zeros(core.shape[:-1] + (1,), core.dtype)
    flux_z = jnp.concatenate([edge, flux_z, edge], axis=-1)
    return (
        -(flux_x[:, 1:] - flux_x[:, :-1])
        - (flux_y[:, :, 1:] - flux_y[:, :, :-1])
        - (flux_z[..., 1:] - flux_z[..., :-1])
    )


def body(
    tprime,
    vapor,
    wind_u,
    wind_v,
    wind_w,
    radius,
    min_radius,
    multiplicity,
    drop_counts,
    cell_index,
    move_list,
):
    devices = lax.axis_size("gx") * lax.axis_size("gy")
    mults = exchange(place(move_list, drop_counts, multiplicity), devices)
    sent, ht, hv, ct, cv = home(
        move_list, cell_index, drop_counts, radius, min_radius, multiplicity, tprime, vapor
    )
    r2s = exchange(sent, devices)
    heated_t, heated_v = scatter(cell_index, ht, hv, ct, cv, tprime, vapor)
    radius_out, multiplicity_out = receive(sources(mults), mults, r2s)
    winds = with_halo(jnp.stack([wind_u, wind_v]), (("gx", 1), ("gy", 2)), 1)
    along_x = 0.5 * (winds[0, :-1, 1:-1] + winds[0, 1:, 1:-1])
    along_y = 0.5 * (winds[1, 1:-1, :-1] + winds[1, 1:-1, 1:])
    along_z = 0.5 * (wind_w[..., :-1] + wind_w[..., 1:])
    start = jnp.stack([heated_t, heated_v])
    section = start
    for weight in (1.0 / 3.0, 0.5, 1.0):
        section = start + advect_step * weight * tendency(
            with_halo(section, (("gx", 1), ("gy", 2)), 1), along_x, along_y, along_z
        )
    return (section[0], section[1], radius_out, multiplicity_out)


def solution(mesh):
    tile = P("gx", "gy", None)
    rows = P(("gx", "gy"), None)
    flat = P(("gx", "gy"))
    return jax.shard_map(
        body,
        mesh=mesh,
        in_specs=(tile,) * 5 + (rows,) * 3 + (flat,) * 3,
        out_specs=(tile, tile, rows, rows),
        check_vma=False,
    )
```

profile of v0, /device:TPU:0, one launch (start us, length us, event | category | flops | bytes accessed | tf_op | source)
XLA Modules:
  0.0 113.5 jit_solution(9546467756106981755)
XLA Ops:
  0.6 1.4 %fusion.40 = (s32[8,128]{1,0:T(8,128)}, f32[8,128]{1,0:T(8,128)}) fusion(s32[1024]{0:T(1024)} %cell.3), kind=kLoop, calls=%fused_computation.118 | loop fusion | flops 12288 | bytes 12288 | tf_op jit(solution)/shard_map/reshape | solution.py:93
  2.0 10.8 %home.1 = (f32[1024,128]{1,0:T(8,128)}, f32[8,128]{1,0:T(8,128)}, f32[8,128]{1,0:T(8,128)}, f32[8,128]{1,0:T(8,128)}, f32[8,128]{1,0:T(8,128)}) custom-call(s32[1024]{0:T(1024)} %move.3, s32[1024]{0:T(1024)} %cell.3, s32[8,128]{1,0:T(8,128)} %bitcast.56, s32[8,128]{1,0:T(8,128)} %get-tuple-element.42.level, f32[1024,128]{1,0:T(8,128)} %radius.1, ...), custom_call_target="tpu_custom_call" | custom-call | tf_op jit(solution)/shard_map/home/pallas_call | solution.py:89
  12.9 7.8 %scatter.1 = (f32[2048,128]{1,0:T(8,128)}, f32[2048,128]{1,0:T(8,128)}) custom-call(s32[1024]{0:T(1024)} %cell.3, f32[8,128]{1,0:T(8,128)} %get-tuple-element.43.cellv, f32[8,128]{1,0:T(8,128)} %get-tuple-element.13.ht, f32[8,128]{1,0:T(8,128)} %get-tuple-element.14.hv, f32[8,128]{1,0:T(8,128)} %get-tuple-element.15.ct, f32[8,128]{1,0:T(8,128)} %get-tuple-element.16.cv, ...), custom_call_target="tpu_custom_call" | custom-call | tf_op jit(solution)/shard_map/scatter/pallas_call | solution.py:135
  20.6 0.8 fusion.37
  21.4 5.1 %collective-permute-start.1 = (f32[2,1,32,128]{3,2,1,0:T(8,128)S(1)}, f32[2,1,32,128]{3,2,1,0:T(8,128)S(1)}, u32[]{:S(2)}, u32[]{:S(2)}) collective-permute-start(f32[2,1,32,128]{3,2,1,0:T(8,128)S(1)} %get-tuple-element.41), channel_id=1, source_target_pairs={{8,0},{16,8},{24,16},{0,24},{9,1},{17,9},{25,17},{1,25},{10,2},{18... | collective-permute-start | bytes 98312 | tf_op jit(solution)/shard_map/ppermute | solution.py:302
  26.5 3.9 %collective-permute-start.3 = (f32[2,1,32,128]{3,2,1,0:T(8,128)S(1)}, f32[2,1,32,128]{3,2,1,0:T(8,128)S(1)}, u32[]{:S(2)}, u32[]{:S(2)}) collective-permute-start(f32[2,1,32,128]{3,2,1,0:T(8,128)S(1)} %get-tuple-element.39), channel_id=1, source_target_pairs={{8,0},{16,8},{24,16},{0,24},{9,1},{17,9},{25,17},{1,25},{10,2},{18... | collective-permute-start | bytes 98312 | tf_op jit(solution)/shard_map/ppermute | solution.py:302
  30.4 4.0 %place.1 = f32[1024,128]{1,0:T(8,128)} custom-call(s32[1024]{0:T(1024)} %move.3, s32[1024]{0:T(1024)} %count.1, f32[1024,128]{1,0:T(8,128)} %mult.3), custom_call_target="tpu_custom_call" | custom-call | tf_op jit(solution)/shard_map/place/pallas_call | solution.py:41
  34.4 6.2 %all-to-all-start = ((f32[32,32,128]{2,1,0:T(8,128)}), f32[32,32,128]{2,1,0:T(8,128)}, u32[]{:S(2)}, u32[]{:S(2)}) async-start(f32[32,32,128]{2,1,0:T(8,128)} %bitcast.54), calls=%async_computation | async-start | bytes 1048576 | tf_op jit(solution)/shard_map/all_to_all | solution.py:288
  40.6 1.9 %add_multiply_fusion = f32[64,32,127]{2,1,0:T(8,128)S(1)} fusion(f32[64,32,128]{2,1,0:T(8,128)} %param.15), kind=kLoop, calls=%fused_computation.93 | loop fusion | flops 520192 | bytes 3121152 | tf_op jit(solution)/shard_map/mul | solution.py:313
  42.5 0.6 fusion.11
  43.3 2.4 %collective-permute-start.5 = (f32[2,66,1,128]{3,2,1,0:T(1,128)S(1)}, f32[2,66,1,128]{3,2,1,0:T(1,128)S(1)}, u32[]{:S(2)}, u32[]{:S(2)}) collective-permute-start(f32[2,66,1,128]{3,2,1,0:T(1,128)S(1)} %get-tuple-element.31), channel_id=1, source_target_pairs={{1,0},{2,1},{3,2},{4,3},{5,4},{6,5},{7,6},{0,7},{9,8},{10,9},{11,1... | collective-permute-start | bytes 202760 | tf_op jit(solution)/shard_map/ppermute | solution.py:302
  45.8 2.7 %collective-permute-start.7 = (f32[2,66,1,128]{3,2,1,0:T(1,128)S(1)}, f32[2,66,1,128]{3,2,1,0:T(1,128)S(1)}, u32[]{:S(2)}, u32[]{:S(2)}) collective-permute-start(f32[2,66,1,128]{3,2,1,0:T(1,128)S(1)} %get-tuple-element.29), channel_id=1, source_target_pairs={{1,0},{2,1},{3,2},{4,3},{5,4},{6,5},{7,6},{0,7},{9,8},{10,9},{11,1... | collective-permute-start | bytes 202760 | tf_op jit(solution)/shard_map/ppermute | solution.py:302
  48.5 0.1 fusion.36
  48.6 0.4 fusion.6
  49.0 1.5 %collective-permute-done.7 = f32[2,66,1,128]{3,2,1,0:T(1,128)S(1)} collective-permute-done((f32[2,66,1,128]{3,2,1,0:T(1,128)S(1)}, f32[2,66,1,128]{3,2,1,0:T(1,128)S(1)}, u32[]{:S(2)}, u32[]{:S(2)}) %collective-permute-start.7) | collective-permute-done | bytes 67616 | tf_op jit(solution)/shard_map/ppermute | solution.py:302
  50.5 3.2 %collective-permute-done.6 = f32[2,66,1,128]{3,2,1,0:T(1,128)S(1)} collective-permute-done((f32[2,66,1,128]{3,2,1,0:T(1,128)S(1)}, f32[2,66,1,128]{3,2,1,0:T(1,128)S(1)}, u32[]{:S(2)}, u32[]{:S(2)}) %collective-permute-start.6) | collective-permute-done | bytes 67616 | tf_op jit(solution)/shard_map/ppermute | solution.py:301
  53.7 0.2 fusion.33
  53.9 1.6 %fusion.5 = f32[2,64,33,128]{3,2,1,0:T(8,128)S(1)} fusion(f32[2,66,1,128]{3,2,1,0:T(1,128)S(1)} %collective-permute-done.5, f32[2,1,32,128]{3,2,1,0:T(8,128)S(1)} %collective-permute-done.1, f32[2,1,32,128]{3,2,1,0:T(8,128)S(1)} %collective-permute-done, f32[1,64,32,128]{3,2,1,0:T(8,128)S(1)} %bitcast.38, f32[1,64,32,128]{3,2,1,0:T(8,128)S(1)} %bitcast.30, ...), kind=kLoop, calls=%fused_computation.27 | loop fusion | flops 5406720 | bytes 5541888 | tf_op jit(solution)/shard_map/mul | solution.py:311
  55.6 1.3 %fusion.28 = f32[2,64,32,128]{3,2,1,0:T(8,128)S(1)} fusion(f32[2,64,33,128]{3,2,1,0:T(8,128)S(1)} %fusion.5, f32[2,65,32,128]{3,2,1,0:T(8,128)S(1)} %fusion.6, f32[2,64,32,127]{3,2,1,0:T(8,128)S(1)} %fusion.11, f32[1,64,32,128]{3,2,1,0:T(8,128)S(1)} %bitcast.39, f32[1,64,32,128]{3,2,1,0:T(8,128)S(1)} %bitcast.31), kind=kLoop, calls=%fused_computation.67 | loop fusion | flops 4718592 | bytes 14663680 | tf_op jit(solution)/shard_map/add | solution.py:351
  56.9 2.8 %collective-permute-start.9 = (f32[2,1,32,128]{3,2,1,0:T(8,128)S(1)}, f32[2,1,32,128]{3,2,1,0:T(8,128)S(1)}, u32[]{:S(2)}, u32[]{:S(2)}) collective-permute-start(f32[2,1,32,128]{3,2,1,0:T(8,128)S(1)} %get-tuple-element.37), channel_id=1, source_target_pairs={{8,0},{16,8},{24,16},{0,24},{9,1},{17,9},{25,17},{1,25},{10,2},{18... | collective-permute-start | bytes 98312 | tf_op jit(solution)/shard_map/ppermute | solution.py:302
  59.7 0.6 fusion.19
  60.4 0.9 collective-permute-done.9
  61.3 4.1 %collective-permute-done.8 = f32[2,1,32,128]{3,2,1,0:T(8,128)S(1)} collective-permute-done((f32[2,1,32,128]{3,2,1,0:T(8,128)S(1)}, f32[2,1,32,128]{3,2,1,0:T(8,128)S(1)}, u32[]{:S(2)}, u32[]{:S(2)}) %collective-permute-start.8) | collective-permute-done | bytes 32800 | tf_op jit(solution)/shard_map/ppermute | solution.py:301
  65.6 0.5 collective-permute-start.10
  66.1 0.4 fusion.7
  66.5 1.5 %collective-permute-done.11 = f32[2,66,1,128]{3,2,1,0:T(1,128)S(1)} collective-permute-done((f32[2,66,1,128]{3,2,1,0:T(1,128)S(1)}, f32[2,66,1,128]{3,2,1,0:T(1,128)S(1)}, u32[]{:S(2)}, u32[]{:S(2)}) %collective-permute-start.11) | collective-permute-done | bytes 67616 | tf_op jit(solution)/shard_map/ppermute | solution.py:302
  67.9 2.3 %collective-permute-done.10 = f32[2,66,1,128]{3,2,1,0:T(1,128)S(1)} collective-permute-done((f32[2,66,1,128]{3,2,1,0:T(1,128)S(1)}, f32[2,66,1,128]{3,2,1,0:T(1,128)S(1)}, u32[]{:S(2)}, u32[]{:S(2)}) %collective-permute-start.10) | collective-permute-done | bytes 67616 | tf_op jit(solution)/shard_map/ppermute | solution.py:301
  70.3 1.6 %fusion.3 = f32[2,64,33,128]{3,2,1,0:T(8,128)S(1)} fusion(f32[2,66,1,128]{3,2,1,0:T(1,128)S(1)} %collective-permute-done.11, f32[2,1,32,128]{3,2,1,0:T(8,128)S(1)} %collective-permute-done.9, f32[2,64,32,128]{3,2,1,0:T(8,128)S(1)} %fusion.28, f32[2,1,32,128]{3,2,1,0:T(8,128)S(1)} %collective-permute-done.8, ...), kind=kLoop, calls=%fused_computation.19 | loop fusion | flops 4325376 | bytes 5541888 | tf_op jit(solution)/shard_map/mul | solution.py:311
  71.8 1.3 %fusion.23 = f32[2,64,32,128]{3,2,1,0:T(8,128)S(1)} fusion(f32[2,64,33,128]{3,2,1,0:T(8,128)S(1)} %fusion.3, f32[2,65,32,128]{3,2,1,0:T(8,128)S(1)} %fusion.7, f32[2,64,32,127]{3,2,1,0:T(8,128)S(1)} %fusion.19, f32[1,64,32,128]{3,2,1,0:T(8,128)S(1)} %bitcast.40, f32[1,64,32,128]{3,2,1,0:T(8,128)S(1)} %bitcast.32), kind=kLoop, calls=%fused_computation.60 | loop fusion | flops 4718592 | bytes 14663680 | tf_op jit(solution)/shard_map/add | solution.py:351
  73.2 2.0 %collective-permute-start.12 = (f32[2,1,32,128]{3,2,1,0:T(8,128)S(1)}, f32[2,1,32,128]{3,2,1,0:T(8,128)S(1)}, u32[]{:S(2)}, u32[]{:S(2)}) collective-permute-start(f32[2,1,32,128]{3,2,1,0:T(8,128)S(1)} %get-tuple-element.34), channel_id=1, source_target_pairs={{0,8},{8,16},{16,24},{24,0},{1,9},{9,17},{17,25},{25,1},{2,10},{10... | collective-permute-start | bytes 98312 | tf_op jit(solution)/shard_map/ppermute | solution.py:301
  75.2 0.6 fusion.13
  75.8 1.2 %collective-permute-done.13 = f32[2,1,32,128]{3,2,1,0:T(8,128)S(1)} collective-permute-done((f32[2,1,32,128]{3,2,1,0:T(8,128)S(1)}, f32[2,1,32,128]{3,2,1,0:T(8,128)S(1)}, u32[]{:S(2)}, u32[]{:S(2)}) %collective-permute-start.13) | collective-permute-done | bytes 32800 | tf_op jit(solution)/shard_map/ppermute | solution.py:302
  77.1 1.9 %collective-permute-done.12 = f32[2,1,32,128]{3,2,1,0:T(8,128)S(1)} collective-permute-done((f32[2,1,32,128]{3,2,1,0:T(8,128)S(1)}, f32[2,1,32,128]{3,2,1,0:T(8,128)S(1)}, u32[]{:S(2)}, u32[]{:S(2)}) %collective-permute-start.12) | collective-permute-done | bytes 32800 | tf_op jit(solution)/shard_map/ppermute | solution.py:301
  79.1 0.5 collective-permute-start.14
  79.6 0.4 fusion.8
  80.0 1.5 %collective-permute-done.15 = f32[2,66,1,128]{3,2,1,0:T(1,128)S(1)} collective-permute-done((f32[2,66,1,128]{3,2,1,0:T(1,128)S(1)}, f32[2,66,1,128]{3,2,1,0:T(1,128)S(1)}, u32[]{:S(2)}, u32[]{:S(2)}) %collective-permute-start.15) | collective-permute-done | bytes 67616 | tf_op jit(solution)/shard_map/ppermute | solution.py:302
  81.5 2.5 %collective-permute-done.14 = f32[2,66,1,128]{3,2,1,0:T(1,128)S(1)} collective-permute-done((f32[2,66,1,128]{3,2,1,0:T(1,128)S(1)}, f32[2,66,1,128]{3,2,1,0:T(1,128)S(1)}, u32[]{:S(2)}, u32[]{:S(2)}) %collective-permute-start.14) | collective-permute-done | bytes 67616 | tf_op jit(solution)/shard_map/ppermute | solution.py:301
  84.0 1.6 %fusion.1 = f32[2,64,33,128]{3,2,1,0:T(8,128)S(1)} fusion(f32[2,66,1,128]{3,2,1,0:T(1,128)S(1)} %collective-permute-done.15, f32[2,1,32,128]{3,2,1,0:T(8,128)S(1)} %collective-permute-done.13, f32[2,64,32,128]{3,2,1,0:T(8,128)S(1)} %fusion.23, f32[2,1,32,128]{3,2,1,0:T(8,128)S(1)} %collective-permute-done.12, ...), kind=kLoop, calls=%fused_computation.11 | loop fusion | flops 4325376 | bytes 5541888 | tf_op jit(solution)/shard_map/mul | solution.py:311
  85.5 2.6 %fusion.17 = f32[2,64,32,128]{3,2,1,0:T(8,128)} fusion(f32[2,64,33,128]{3,2,1,0:T(8,128)S(1)} %fusion.1, f32[2,65,32,128]{3,2,1,0:T(8,128)S(1)} %fusion.8, f32[2,64,32,127]{3,2,1,0:T(8,128)S(1)} %fusion.13, f32[1,64,32,128]{3,2,1,0:T(8,128)S(1)} %bitcast.41, f32[1,64,32,128]{3,2,1,0:T(8,128)S(1)} %bitcast.33), kind=kLoop, calls=%fused_computation.51 | loop fusion | flops 4718592 | bytes 14663680 | tf_op jit(solution)/shard_map/add | solution.py:351
  88.1 2.6 %all-to-all-start.1 = ((f32[32,32,128]{2,1,0:T(8,128)}), f32[32,32,128]{2,1,0:T(8,128)S(1)}, u32[]{:S(2)}, u32[]{:S(2)}) async-start(f32[32,32,128]{2,1,0:T(8,128)} %bitcast.16), calls=%async_computation.1 | async-start | bytes 1048576 | tf_op jit(solution)/shard_map/all_to_all | solution.py:288
  90.7 3.0 %slice_bitcast_fusion = (f32[64,32,128]{2,1,0:T(8,128)}, f32[64,32,128]{2,1,0:T(8,128)}) fusion(f32[2,64,32,128]{3,2,1,0:T(8,128)} %fusion.17), kind=kLoop, calls=%fused_computation.91 | loop fusion | bytes 4194304 | tf_op jit(solution)/shard_map/squeeze | solution.py:354
  93.8 1.3 %fusion.41 = (pred[1024]{0:T(1024)(128)(4,1)S(1)}, pred[1024,1]{1,0:T(8,128)(4,1)S(1)}) fusion(f32[1024,128]{1,0:T(8,128)} %bitcast.14.mults), kind=kLoop, calls=%fused_computation.122 | loop fusion | flops 1024 | bytes 6144 | tf_op jit(solution)/shard_map/gt | solution.py:281
  95.0 0.2 convert_reduce_fusion
  95.2 0.3 reduce-window.9
  95.8 1.1 select_reduce_fusion.src
  96.9 9.4 %all-to-all-done.1 = f32[32,32,128]{2,1,0:T(8,128)S(1)} async-done(((f32[32,32,128]{2,1,0:T(8,128)}), f32[32,32,128]{2,1,0:T(8,128)S(1)}, u32[]{:S(2)}, u32[]{:S(2)}) %all-to-all-start.1) | async-done | bytes 524320 | tf_op jit(solution)/shard_map/all_to_all | solution.py:288
  106.4 0.8 copy-done.5
  107.2 6.3 %receive.1 = (f32[512,128]{1,0:T(8,128)}, f32[512,128]{1,0:T(8,128)}) custom-call(s32[512]{0:T(512)} %select_reduce_fusion.src, f32[1024,128]{1,0:T(8,128)} %bitcast.14.mults, f32[1024,128]{1,0:T(8,128)} %bitcast.55), custom_call_target="tpu_custom_call" | custom-call | tf_op jit(solution)/shard_map/receive/pallas_call | solution.py:270
  (37 shorter events, 0.9 us)
Async XLA Ops:
  12.8 13.7 %copy-start.2 = (f32[64,32,128]{2,1,0:T(8,128)S(1)}, f32[64,32,128]{2,1,0:T(8,128)}, u32[]{:S(2)}) copy-start(f32[64,32,128]{2,1,0:T(8,128)} %param.14) | copy-start | bytes 3145732
  12.8 13.7 %copy-start.3 = (f32[64,32,128]{2,1,0:T(8,128)S(1)}, f32[64,32,128]{2,1,0:T(8,128)}, u32[]{:S(2)}) copy-start(f32[64,32,128]{2,1,0:T(8,128)} %param.13) | copy-start | bytes 3145732
  21.4 21.8 %collective-permute-start.1 = (f32[2,1,32,128]{3,2,1,0:T(8,128)S(1)}, f32[2,1,32,128]{3,2,1,0:T(8,128)S(1)}, u32[]{:S(2)}, u32[]{:S(2)}) collective-permute-start(f32[2,1,32,128]{3,2,1,0:T(8,128)S(1)} %get-tuple-element.41), channel_id=1, source_target_pairs={{8,0},{16,8},{24,16},{0,24},{9,1},{17,9},{25,17},{1,25},{10,2},{18... | collective-permute-start | bytes 98312 | tf_op jit(solution)/shard_map/ppermute | solution.py:302
  26.5 16.7 %collective-permute-start = (f32[2,1,32,128]{3,2,1,0:T(8,128)S(1)}, f32[2,1,32,128]{3,2,1,0:T(8,128)S(1)}, u32[]{:S(2)}, u32[]{:S(2)}) collective-permute-start(f32[2,1,32,128]{3,2,1,0:T(8,128)S(1)} %get-tuple-element.40), channel_id=1, source_target_pairs={{0,8},{8,16},{16,24},{24,0},{1,9},{9,17},{17,25},{25,1},{2,10},{10... | collective-permute-start | bytes 98312 | tf_op jit(solution)/shard_map/ppermute | solution.py:301
  26.5 19.2 %collective-permute-start.3 = (f32[2,1,32,128]{3,2,1,0:T(8,128)S(1)}, f32[2,1,32,128]{3,2,1,0:T(8,128)S(1)}, u32[]{:S(2)}, u32[]{:S(2)}) collective-permute-start(f32[2,1,32,128]{3,2,1,0:T(8,128)S(1)} %get-tuple-element.39), channel_id=1, source_target_pairs={{8,0},{16,8},{24,16},{0,24},{9,1},{17,9},{25,17},{1,25},{10,2},{18... | collective-permute-start | bytes 98312 | tf_op jit(solution)/shard_map/ppermute | solution.py:302
  30.4 15.3 %collective-permute-start.2 = (f32[2,1,32,128]{3,2,1,0:T(8,128)S(1)}, f32[2,1,32,128]{3,2,1,0:T(8,128)S(1)}, u32[]{:S(2)}, u32[]{:S(2)}) collective-permute-start(f32[2,1,32,128]{3,2,1,0:T(8,128)S(1)} %get-tuple-element.38), channel_id=1, source_target_pairs={{0,8},{8,16},{16,24},{24,0},{1,9},{9,17},{17,25},{25,1},{2,10},{10... | collective-permute-start | bytes 98312 | tf_op jit(solution)/shard_map/ppermute | solution.py:301
  34.4 8.1 %copy-start = (f32[2048,128]{1,0:T(8,128)S(1)}, f32[2048,128]{1,0:T(8,128)}, u32[]{:S(2)}) copy-start(f32[2048,128]{1,0:T(8,128)} %get-tuple-element.17) | copy-start | bytes 3145732
  34.4 8.1 %copy-start.1 = (f32[2048,128]{1,0:T(8,128)S(1)}, f32[2048,128]{1,0:T(8,128)}, u32[]{:S(2)}) copy-start(f32[2048,128]{1,0:T(8,128)} %get-tuple-element.18) | copy-start | bytes 3145732
  34.4 53.7 %all-to-all-start = ((f32[32,32,128]{2,1,0:T(8,128)}), f32[32,32,128]{2,1,0:T(8,128)}, u32[]{:S(2)}, u32[]{:S(2)}) async-start(f32[32,32,128]{2,1,0:T(8,128)} %bitcast.54), calls=%async_computation | async-start | bytes 1048576 | tf_op jit(solution)/shard_map/all_to_all | solution.py:288
  43.2 2.5 %copy-start.4 = (f32[64,32,128]{2,1,0:T(8,128)S(1)}, f32[64,32,128]{2,1,0:T(8,128)}, u32[]{:S(2)}) copy-start(f32[64,32,128]{2,1,0:T(8,128)} %param.13) | copy-start | bytes 3145732
  43.3 10.6 %collective-permute-start.5 = (f32[2,66,1,128]{3,2,1,0:T(1,128)S(1)}, f32[2,66,1,128]{3,2,1,0:T(1,128)S(1)}, u32[]{:S(2)}, u32[]{:S(2)}) collective-permute-start(f32[2,66,1,128]{3,2,1,0:T(1,128)S(1)} %get-tuple-element.31), channel_id=1, source_target_pairs={{1,0},{2,1},{3,2},{4,3},{5,4},{6,5},{7,6},{0,7},{9,8},{10,9},{11,1... | collective-permute-start | bytes 202760 | tf_op jit(solution)/shard_map/ppermute | solution.py:302
  45.7 8.3 %collective-permute-start.4 = (f32[2,66,1,128]{3,2,1,0:T(1,128)S(1)}, f32[2,66,1,128]{3,2,1,0:T(1,128)S(1)}, u32[]{:S(2)}, u32[]{:S(2)}) collective-permute-start(f32[2,66,1,128]{3,2,1,0:T(1,128)S(1)} %get-tuple-element.30), channel_id=1, source_target_pairs={{0,1},{1,2},{2,3},{3,4},{4,5},{5,6},{6,7},{7,0},{8,9},{9,10},{10,1... | collective-permute-start | bytes 202760 | tf_op jit(solution)/shard_map/ppermute | solution.py:301
  45.8 4.7 %collective-permute-start.7 = (f32[2,66,1,128]{3,2,1,0:T(1,128)S(1)}, f32[2,66,1,128]{3,2,1,0:T(1,128)S(1)}, u32[]{:S(2)}, u32[]{:S(2)}) collective-permute-start(f32[2,66,1,128]{3,2,1,0:T(1,128)S(1)} %get-tuple-element.29), channel_id=1, source_target_pairs={{1,0},{2,1},{3,2},{4,3},{5,4},{6,5},{7,6},{0,7},{9,8},{10,9},{11,1... | collective-permute-start | bytes 202760 | tf_op jit(solution)/shard_map/ppermute | solution.py:302
  48.5 5.2 %collective-permute-start.6 = (f32[2,66,1,128]{3,2,1,0:T(1,128)S(1)}, f32[2,66,1,128]{3,2,1,0:T(1,128)S(1)}, u32[]{:S(2)}, u32[]{:S(2)}) collective-permute-start(f32[2,66,1,128]{3,2,1,0:T(1,128)S(1)} %get-tuple-element.28), channel_id=1, source_target_pairs={{0,1},{1,2},{2,3},{3,4},{4,5},{5,6},{6,7},{7,0},{8,9},{9,10},{10,1... | collective-permute-start | bytes 202760 | tf_op jit(solution)/shard_map/ppermute | solution.py:301
  56.9 4.4 %collective-permute-start.9 = (f32[2,1,32,128]{3,2,1,0:T(8,128)S(1)}, f32[2,1,32,128]{3,2,1,0:T(8,128)S(1)}, u32[]{:S(2)}, u32[]{:S(2)}) collective-permute-start(f32[2,1,32,128]{3,2,1,0:T(8,128)S(1)} %get-tuple-element.37), channel_id=1, source_target_pairs={{8,0},{16,8},{24,16},{0,24},{9,1},{17,9},{25,17},{1,25},{10,2},{18... | collective-permute-start | bytes 98312 | tf_op jit(solution)/shard_map/ppermute | solution.py:302
  59.7 5.7 %collective-permute-start.8 = (f32[2,1,32,128]{3,2,1,0:T(8,128)S(1)}, f32[2,1,32,128]{3,2,1,0:T(8,128)S(1)}, u32[]{:S(2)}, u32[]{:S(2)}) collective-permute-start(f32[2,1,32,128]{3,2,1,0:T(8,128)S(1)} %get-tuple-element.36), channel_id=1, source_target_pairs={{0,8},{8,16},{16,24},{24,0},{1,9},{9,17},{17,25},{25,1},{2,10},{10... | collective-permute-start | bytes 98312 | tf_op jit(solution)/shard_map/ppermute | solution.py:301
  65.5 2.4 %collective-permute-start.11 = (f32[2,66,1,128]{3,2,1,0:T(1,128)S(1)}, f32[2,66,1,128]{3,2,1,0:T(1,128)S(1)}, u32[]{:S(2)}, u32[]{:S(2)}) collective-permute-start(f32[2,66,1,128]{3,2,1,0:T(1,128)S(1)} %get-tuple-element.27), channel_id=1, source_target_pairs={{1,0},{2,1},{3,2},{4,3},{5,4},{6,5},{7,6},{0,7},{9,8},{10,9},{11,1... | collective-permute-start | bytes 202760 | tf_op jit(solution)/shard_map/ppermute | solution.py:302
  65.6 4.7 %collective-permute-start.10 = (f32[2,66,1,128]{3,2,1,0:T(1,128)S(1)}, f32[2,66,1,128]{3,2,1,0:T(1,128)S(1)}, u32[]{:S(2)}, u32[]{:S(2)}) collective-permute-start(f32[2,66,1,128]{3,2,1,0:T(1,128)S(1)} %get-tuple-element.26), channel_id=1, source_target_pairs={{0,1},{1,2},{2,3},{3,4},{4,5},{5,6},{6,7},{7,0},{8,9},{9,10},{10,1... | collective-permute-start | bytes 202760 | tf_op jit(solution)/shard_map/ppermute | solution.py:301
  73.1 4.0 %collective-permute-start.13 = (f32[2,1,32,128]{3,2,1,0:T(8,128)S(1)}, f32[2,1,32,128]{3,2,1,0:T(8,128)S(1)}, u32[]{:S(2)}, u32[]{:S(2)}) collective-permute-start(f32[2,1,32,128]{3,2,1,0:T(8,128)S(1)} %get-tuple-element.35), channel_id=1, source_target_pairs={{8,0},{16,8},{24,16},{0,24},{9,1},{17,9},{25,17},{1,25},{10,2},{18... | collective-permute-start | bytes 98312 | tf_op jit(solution)/shard_map/ppermute | solution.py:302
  73.2 5.8 %collective-permute-start.12 = (f32[2,1,32,128]{3,2,1,0:T(8,128)S(1)}, f32[2,1,32,128]{3,2,1,0:T(8,128)S(1)}, u32[]{:S(2)}, u32[]{:S(2)}) collective-permute-start(f32[2,1,32,128]{3,2,1,0:T(8,128)S(1)} %get-tuple-element.34), channel_id=1, source_target_pairs={{0,8},{8,16},{16,24},{24,0},{1,9},{9,17},{17,25},{25,1},{2,10},{10... | collective-permute-start | bytes 98312 | tf_op jit(solution)/shard_map/ppermute | solution.py:301
  79.0 2.4 %collective-permute-start.15 = (f32[2,66,1,128]{3,2,1,0:T(1,128)S(1)}, f32[2,66,1,128]{3,2,1,0:T(1,128)S(1)}, u32[]{:S(2)}, u32[]{:S(2)}) collective-permute-start(f32[2,66,1,128]{3,2,1,0:T(1,128)S(1)} %get-tuple-element.25), channel_id=1, source_target_pairs={{1,0},{2,1},{3,2},{4,3},{5,4},{6,5},{7,6},{0,7},{9,8},{10,9},{11,1... | collective-permute-start | bytes 202760 | tf_op jit(solution)/shard_map/ppermute | solution.py:302
  79.1 4.8 %collective-permute-start.14 = (f32[2,66,1,128]{3,2,1,0:T(1,128)S(1)}, f32[2,66,1,128]{3,2,1,0:T(1,128)S(1)}, u32[]{:S(2)}, u32[]{:S(2)}) collective-permute-start(f32[2,66,1,128]{3,2,1,0:T(1,128)S(1)} %get-tuple-element.24), channel_id=1, source_target_pairs={{0,1},{1,2},{2,3},{3,4},{4,5},{5,6},{6,7},{7,0},{8,9},{9,10},{10,1... | collective-permute-start | bytes 202760 | tf_op jit(solution)/shard_map/ppermute | solution.py:301
  88.1 18.2 %all-to-all-start.1 = ((f32[32,32,128]{2,1,0:T(8,128)}), f32[32,32,128]{2,1,0:T(8,128)S(1)}, u32[]{:S(2)}, u32[]{:S(2)}) async-start(f32[32,32,128]{2,1,0:T(8,128)} %bitcast.16), calls=%async_computation.1 | async-start | bytes 1048576 | tf_op jit(solution)/shard_map/all_to_all | solution.py:288
  106.4 0.8 copy-start.5
where the time goes:
time: 114 us
  waiting for transfers between devices  30 us (26%)
  Pallas kernels  28.9 us (25%)
  starting transfers between devices  28.9 us (25%)
  other arithmetic  20.7 us (18%)
  local copies, waits for them, and re-layouts  4.06 us (4%)
    ppermute x8, starting transfers between devices, with_halo(): after_ = lax.ppermute(first, axis, down)  17 us
    ppermute x8, waiting for transfers between devices, with_halo(): before_ = lax.ppermute(last, axis, up)  14 us
    pallas_call x1, Pallas kernels, home(): pl.pallas_call(home_kernel, out_shape=(jax.ShapeDtypeStruct(radius.shape,...  10.8 us
    all_to_all x2, waiting for transfers between devices, exchange(): lax.all_to_all(rows.reshape((devices, -1) + rows.shape[1:]), ('gx', 'gy')...  9.44 us
    all_to_all x2, starting transfers between devices, exchange(): lax.all_to_all(rows.reshape((devices, -1) + rows.shape[1:]), ('gx', 'gy')...  8.8 us
    pallas_call x1, Pallas kernels, scatter(): pl.pallas_call(scatter_kernel, out_shape=(o, o), in_specs=[SMEM()] + [VM(...  7.76 us
    ppermute x8, waiting for transfers between devices, with_halo(): after_ = lax.ppermute(first, axis, down)  6.58 us
    pallas_call x1, Pallas kernels, receive(): pl.pallas_call(receive_kernel, out_shape=(out, out), in_specs=[SMEM(), VM...  6.34 us
  transfers between devices with their start and end apart: 18, of which 11 were waited for; matrix products, arithmetic and copies ran while one was open for 19% of the time, Pallas kernels for 4%

commit v1 on v0

--- a/solution.py
+++ b/solution.py
@@ -25,30 +25,27 @@
         return 0
     lax.fori_loop(0,n//unroll,group,0)
 
-def place_kernel(move,count,mult,out,buf):
+def place_kernel(slot,mult,out,buf):
     n=mult.shape[0]
     buf[...]=jnp.zeros_like(buf)
-    lane=lax.broadcasted_iota(jnp.int32,(1,LAN),1)
     def one(b):
-        slot=move[b]
-        dst=jnp.where(slot>=0,slot,n)
-        buf[pl.ds(dst,1),:]=jnp.where(lane<count[b],mult[pl.ds(b,1),:],0.0)
-    row_loop(n,8,one)
+        buf[pl.ds(slot[b],1),:]=mult[pl.ds(b,1),:]
+    row_loop(n,32,one)
     out[...]=buf[:n,:]
 
-def place(move,count,mult):
+def place(slot,mult):
     n=mult.shape[0]
     return pl.pallas_call(place_kernel,out_shape=jax.ShapeDtypeStruct(mult.shape,jnp.float32),
-        in_specs=[SMEM(),SMEM(),VM()],out_specs=VM(),
-        scratch_shapes=[pltpu.VMEM((n+SUB,LAN),jnp.float32)],name="place")(move,count,mult)
-
-def home_kernel(move,cell,count,level,radius,floor,mult,tp,vp,send,ht,hv,ct,cv,rows_t,rows_v,buf):
+        in_specs=[SMEM(),VM()],out_specs=VM(),
+        scratch_shapes=[pltpu.VMEM((n+SUB,LAN),jnp.float32)],name="place")(slot,mult)
+
+def home_kernel(slot,column,count,level,radius,floor,mult,tp,vp,send,ht,hv,ct,cv,rows_t,rows_v,buf):
     n=radius.shape[0]
     def fetch(b):
-        c=lax.shift_right_logical(cell[b],7)
+        c=column[b]
         rows_t[pl.ds(b,1),:]=tp[pl.ds(c,1),:]
         rows_v[pl.ds(b,1),:]=vp[pl.ds(c,1),:]
-    row_loop(n,8,fetch)
+    row_loop(n,32,fetch)
     depth=lax.broadcasted_iota(jnp.int32,(LAN,LAN),0)
     def tile(t,_):
         sl=pl.ds(pl.multiple_of(t*LAN,LAN),LAN)
@@ -56,7 +53,8 @@
         temp0=jnp.sum(jnp.where(here,jnp.transpose(rows_t[sl,:]),0.0),axis=0,keepdims=True)
         wet0=jnp.sum(jnp.where(here,jnp.transpose(rows_v[sl,:]),0.0),axis=0,keepdims=True)
         r=jnp.transpose(radius[sl,:]); fl=jnp.transpose(floor[sl,:])
-        m=jnp.where(depth<count[pl.ds(t,1),:],jnp.transpose(mult[sl,:]),0.0)
+        alive=depth<count[pl.ds(t,1),:]
+        m=jnp.where(alive,jnp.transpose(mult[sl,:]),0.0)
         r2=r*r; f2=fl*fl; g3=(growth*solute)*(f2*fl)
         inv=lax.rsqrt(r2); mass=r2*(r2*inv)
         temp=temp0; wet=wet0
@@ -71,18 +69,16 @@
             r2=grown; mass=new
         ht[pl.ds(t,1),:]=temp-temp0; hv[pl.ds(t,1),:]=wet-wet0
         ct[pl.ds(t,1),:]=temp0; cv[pl.ds(t,1),:]=wet0
-        rows_t[sl,:]=jnp.transpose(r2)
+        rows_t[sl,:]=jnp.transpose(jnp.where(alive,r2,0.0))
         return 0
     lax.fori_loop(0,n//LAN,tile,0)
     buf[...]=jnp.zeros_like(buf)
     def put(b):
-        slot=move[b]
-        dst=jnp.where(slot>=0,slot,n)
-        buf[pl.ds(dst,1),:]=rows_t[pl.ds(b,1),:]
-    row_loop(n,8,put)
+        buf[pl.ds(slot[b],1),:]=rows_t[pl.ds(b,1),:]
+    row_loop(n,32,put)
     send[...]=buf[:n,:]
 
-def home(move,cell,count,radius,floor,mult,tp,vp):
+def home(slot,column,level,count,radius,floor,mult,tp,vp):
     n=radius.shape[0]; g=n//LAN
     levels=tp.shape[-1]
     tab=jax.ShapeDtypeStruct((g,LAN),jnp.float32)
@@ -90,10 +86,10 @@
         out_shape=(jax.ShapeDtypeStruct(radius.shape,jnp.float32),tab,tab,tab,tab),
         in_specs=[SMEM(),SMEM()]+[VM()]*7,out_specs=(VM(),)*5,
         scratch_shapes=[pltpu.VMEM((n,LAN),jnp.float32),pltpu.VMEM((n,LAN),jnp.float32),pltpu.VMEM((n+SUB,LAN),jnp.float32)],
-        name="home")(move,cell,count.reshape(g,LAN),(cell%levels).reshape(g,LAN),radius,floor,mult,
+        name="home")(slot,column,count.reshape(g,LAN),level.reshape(g,LAN),radius,floor,mult,
                      tp.reshape(-1,levels),vp.reshape(-1,levels))
 
-def scatter_kernel(cell,cellv,ht,hv,ct,cv,tp,vp,ot,ov,vt,vv,acct,accv):
+def scatter_kernel(column,level,cellv,ht,hv,ct,cv,tp,vp,ot,ov,vt,vv,acct,accv):
     g=cellv.shape[0]; n=g*LAN
     spread=lambda ref,t: jnp.transpose(jnp.broadcast_to(ref[pl.ds(t,1),:],(LAN,LAN)))
     acct[...]=jnp.zeros_like(acct); accv[...]=jnp.zeros_like(accv)
@@ -122,19 +118,18 @@
     ot[...]=tp[...]; ov[...]=vp[...]
     lane=lax.broadcasted_iota(jnp.int32,(1,LAN),1)
     def put(b):
-        x=cell[b]
-        c=lax.shift_right_logical(x,7); hit=lane==(x&127)
+        c=column[b]; hit=lane==level[b]
         pltpu.store(ot.at[pl.ds(c,1),:],vt[pl.ds(b,1),:],mask=hit)
         pltpu.store(ov.at[pl.ds(c,1),:],vv[pl.ds(b,1),:],mask=hit)
-    row_loop(n,8,put)
-
-def scatter(cell,ht,hv,ct,cv,tp,vp):
+    row_loop(n,32,put)
+
+def scatter(column,level,cell,ht,hv,ct,cv,tp,vp):
     g=ht.shape[0]; n=g*LAN
     t2=tp.reshape(-1,LAN); v2=vp.reshape(-1,LAN)
     o=jax.ShapeDtypeStruct(t2.shape,jnp.float32)
-    a,b=pl.pallas_call(scatter_kernel,out_shape=(o,o),in_specs=[SMEM()]+[VM()]*7,out_specs=(VM(),VM()),
+    a,b=pl.pallas_call(scatter_kernel,out_shape=(o,o),in_specs=[SMEM()]*2+[VM()]*7,out_specs=(VM(),VM()),
         scratch_shapes=[pltpu.VMEM((n,LAN),jnp.float32)]*2+[pltpu.VMEM((g*SUB,LAN),jnp.float32)]*2,
-        name="scatter")(cell,cell.reshape(g,LAN).astype(jnp.float32),ht,hv,ct,cv,t2,v2)
+        name="scatter")(column,level,cell.reshape(g,LAN).astype(jnp.float32),ht,hv,ct,cv,t2,v2)
     return a.reshape(tp.shape),b.reshape(vp.shape)
 
 
@@ -244,6 +239,108 @@
     return cat(outs_r),cat(outs_m),cat(rank)
 
 
+W=3
+UNROLL=8
+
+def advect_kernel(tc,vc,uc,vw,wc,xlo,xhi,ylo,yhi,ot,ov,f,ax,ay,az,ad,s1,s2,sem):
+    nx,ny,_=tc.shape
+    nt=ny//SUB+1
+    copies=[pltpu.make_async_copy(c,f.at[i,pl.ds(W,nx),pl.ds(0,ny)],sem.at[i]) for i,c in enumerate((tc,vc,uc,vw,wc))]
+    for c in copies: c.start()
+    def sides(x,_):
+        for i in range(5):
+            f[i,x,ny:ny+W,:]=yhi[i,x]
+            f[i,x,ny+SUB-W:ny+SUB,:]=ylo[i,x]
+        return 0
+    lax.fori_loop(0,nx+2*W,sides,0)
+    for i in range(5):
+        f[i,0:W,0:ny,:]=xlo[i]
+        f[i,W+nx:W+nx+W,0:ny,:]=xhi[i]
+    for c in copies: c.wait()
+    scale=0.25*advect_step
+    lane=lax.broadcasted_iota(jnp.int32,(SUB,LAN),1)
+    first=lane==0; last=lane==LAN-1
+    row=lax.broadcasted_iota(jnp.int32,(SUB,LAN),0)
+    bottom=row==SUB-1; top=row==0
+    rows=lambda t: pl.ds(t*SUB,SUB)
+    near=pair_matrix()
+    def ahead(tl):
+        r=[pltpu.roll(x,SUB-1,0) for x in tl]
+        return [jnp.where(bottom,r[(t+1)%nt],r[t]) for t in range(nt)]
+    def behind(tl):
+        r=[pltpu.roll(x,1,0) for x in tl]
+        return [jnp.where(top,r[t-1],r[t]) for t in range(nt)]
+    def pairs(tl):
+        x=jnp.concatenate(tl,axis=0)
+        hi=x.astype(jnp.bfloat16)
+        lo=(x-hi.astype(jnp.float32)).astype(jnp.bfloat16)
+        y=jnp.dot(jnp.concatenate([hi,lo],axis=1),near,preferred_element_type=jnp.float32)
+        return [(y[k*SUB:(k+1)*SUB,:LAN],y[k*SUB:(k+1)*SUB,LAN:]) for k in range(len(tl))]
+    def coef(g,_):
+        x0=g*UNROLL
+        zs=pairs([f[4,x0+p,rows(t),:] for p in range(UNROLL) for t in range(nt)])
+        for p in range(UNROLL):
+            x=x0+p
+            xn=x+1
+            for t in range(nt):
+                ax[x,rows(t),:]=scale*(f[2,x,rows(t),:]+f[2,xn,rows(t),:])
+            v=[f[3,x,rows(t),:] for t in range(nt)]
+            for t,n in enumerate(ahead(v)):
+                ay[x,rows(t),:]=scale*(v[t]+n)
+            for t in range(nt):
+                up,dn=zs[p*nt+t]
+                az[x,rows(t),:]=jnp.where(last,0.0,scale*up)
+                ad[x,rows(t),:]=jnp.where(first,0.0,scale*dn)
+        return 0
+    lax.fori_loop(0,pl.cdiv(nx+2*W,UNROLL),coef,0)
+    def section(weight,src,dst,margin,count):
+        edge=tuple(ax[margin-1,rows(t),:]*(src[i,margin-1,rows(t),:]+src[i,margin,rows(t),:]) for i in range(2) for t in range(count))
+        def planes(g,prev):
+            x0=margin+g*UNROLL
+            f0={(i,p):[src[i,x0+p,rows(t),:] for t in range(nt)] for i in range(2) for p in range(UNROLL+1)}
+            zs=[pairs([f0[i,p][t] for p in range(UNROLL) for t in range(count)]) for i in range(2)]
+            for p in range(UNROLL):
+                x=x0+p; nxt=[]
+                for i in range(2):
+                    c=f0[i,p]; up=ahead(c)
+                    gy=[ay[x,rows(t),:]*(c[t]+up[t]) for t in range(nt)]
+                    dn=behind(gy)
+                    for t in range(count):
+                        gx=ax[x,rows(t),:]*(c[t]+f0[i,p+1][t])
+                        zu,zd=zs[i][p*count+t]
+                        d=(gx-prev[i*count+t])+(gy[t]-dn[t])+(az[x,rows(t),:]*zu-ad[x,rows(t),:]*zd)
+                        dst(i,x,t,f[i,x,rows(t),:]-weight*d)
+                        nxt.append(gx)
+                prev=tuple(nxt)
+            return prev
+        lax.fori_loop(0,pl.cdiv(nx+2*W-2*margin,UNROLL),planes,edge)
+    def put(buf):
+        def g(i,x,t,val): buf[i,x,rows(t),:]=val
+        return g
+    def out(i,x,t,val):
+        (ot,ov)[i][x-W,rows(t),:]=val
+    section(1.0/3.0,f,put(s1),1,nt)
+    section(0.5,s1,put(s2),2,nt)
+    section(1.0,s2,out,3,nt-1)
+
+def pair_matrix():
+    k=lax.broadcasted_iota(jnp.int32,(2*LAN,2*LAN),0)
+    n=lax.broadcasted_iota(jnp.int32,(2*LAN,2*LAN),1)
+    z=jnp.where(k>=LAN,k-LAN,k)
+    o=jnp.where(n>=LAN,n-LAN,n)
+    other=jnp.where(n>=LAN,o-1,o+1)
+    return jnp.where((z==o)|(z==other),1.0,0.0).astype(jnp.bfloat16)
+
+def advect(t,v,u,w2,w3,xlo,xhi,ylo,yhi):
+    nx,ny,nz=t.shape
+    o=jax.ShapeDtypeStruct(t.shape,jnp.float32)
+    ext=(pl.cdiv(nx+2*W,UNROLL)*UNROLL+SUB,ny+SUB,nz)
+    ANY=pl.BlockSpec(memory_space=pl.ANY); VM=pl.BlockSpec(memory_space=pltpu.VMEM)
+    return pl.pallas_call(advect_kernel,out_shape=(o,o),in_specs=[ANY]*5+[VM]*4,out_specs=(VM,VM),
+        scratch_shapes=[pltpu.VMEM((5,)+ext,jnp.float32)]+[pltpu.VMEM(ext,jnp.float32)]*4+[pltpu.VMEM((2,)+ext,jnp.float32)]*2+[pltpu.SemaphoreType.DMA((5,))],
+        name="advect")(t,v,u,w2,w3,xlo,xhi,ylo,yhi)
+
+
 def receive_kernel(src, mults, r2s, ro_ref, mo_ref, mrow, rrow):
     blocks = ro_ref.shape[0]
 
@@ -252,11 +349,12 @@
         mrow[pl.ds(b, 1), :] = mults[pl.ds(s, 1), :]
         rrow[pl.ds(b, 1), :] = r2s[pl.ds(s, 1), :]
 
-    row_loop(blocks, 8, pull)
+    row_loop(blocks, 32, pull)
 
     def tile(t, _):
         sl = pl.ds(pl.multiple_of(t * LAN, LAN), LAN)
-        a, b, rank = collect_tile(jnp.transpose(rrow[sl, :]), jnp.transpose(mrow[sl, :]))
+        r2 = jnp.transpose(rrow[sl, :])
+        a, b, rank = collect_tile(r2, jnp.where(r2 > 0.0, jnp.transpose(mrow[sl, :]), 0.0))
         rank = jnp.transpose(rank).astype(jnp.int32)
         ro_ref[sl, :] = jnp.take_along_axis(jnp.transpose(a), rank, axis=1)
         mo_ref[sl, :] = jnp.take_along_axis(jnp.transpose(b), rank, axis=1)
@@ -291,33 +389,30 @@
     return moved.reshape(rows.shape)
 
 
-def with_halo(array, sides, width):
-    for axis, dim in sides:
-        size, length = (lax.axis_size(axis), array.shape[dim])
-        up = [(i, (i + 1) % size) for i in range(size)]
-        down = [(j, i) for i, j in up]
-        last = lax.slice_in_dim(array, length - width, length, axis=dim)
-        first = lax.slice_in_dim(array, 0, width, axis=dim)
-        before_ = lax.ppermute(last, axis, up)
-        after_ = lax.ppermute(first, axis, down)
-        array = jnp.concatenate([before_, array, after_], axis=dim)
-    return array
-
-
-def tendency(padded, along_x, along_y, along_z):
-    middle_y = padded[:, :, 1:-1]
-    flux_x = along_x * (0.5 * (middle_y[:, :-1] + middle_y[:, 1:]))
-    middle_x = padded[:, 1:-1]
-    flux_y = along_y * (0.5 * (middle_x[:, :, :-1] + middle_x[:, :, 1:]))
-    core = padded[:, 1:-1, 1:-1]
-    flux_z = along_z * (0.5 * (core[..., :-1] + core[..., 1:]))
-    edge = jnp.zeros(core.shape[:-1] + (1,), core.dtype)
-    flux_z = jnp.concatenate([edge, flux_z, edge], axis=-1)
-    return (
-        -(flux_x[:, 1:] - flux_x[:, :-1])
-        - (flux_y[:, :, 1:] - flux_y[:, :, :-1])
-        - (flux_z[..., 1:] - flux_z[..., :-1])
-    )
+def shifts(axis):
+    size = lax.axis_size(axis)
+    up = [(i, (i + 1) % size) for i in range(size)]
+    return up, [(j, i) for i, j in up]
+
+
+def slabs(arrays, dim, start):
+    return jnp.stack([lax.slice_in_dim(a, start, start + W, axis=dim) for a in arrays])
+
+
+def halos(arrays):
+    nx, ny = arrays[0].shape[:2]
+    up, down = shifts("gx")
+    xlo = lax.ppermute(slabs(arrays, 0, nx - W), "gx", up)
+    xhi = lax.ppermute(slabs(arrays, 0, 0), "gx", down)
+    up, down = shifts("gy")
+
+    def side(start):
+        ends = [x[:, :, start : start + W] for x in (xlo, xhi)]
+        return jnp.concatenate([ends[0], slabs(arrays, 1, start), ends[1]], axis=1)
+
+    ylo = lax.ppermute(side(ny - W), "gy", up)
+    yhi = lax.ppermute(side(0), "gy", down)
+    return xlo, xhi, ylo, yhi
 
 
 def body(
@@ -334,24 +429,20 @@
     move_list,
 ):
     devices = lax.axis_size("gx") * lax.axis_size("gy")
-    mults = exchange(place(move_list, drop_counts, multiplicity), devices)
+    levels = tprime.shape[2]
+    slot = jnp.where(move_list >= 0, move_list, multiplicity.shape[0])
+    column = cell_index // levels
+    level = cell_index % levels
+    mults = exchange(place(slot, multiplicity), devices)
     sent, ht, hv, ct, cv = home(
-        move_list, cell_index, drop_counts, radius, min_radius, multiplicity, tprime, vapor
+        slot, column, level, drop_counts, radius, min_radius, multiplicity, tprime, vapor
     )
     r2s = exchange(sent, devices)
-    heated_t, heated_v = scatter(cell_index, ht, hv, ct, cv, tprime, vapor)
+    heated_t, heated_v = scatter(column, level, cell_index, ht, hv, ct, cv, tprime, vapor)
+    fields = (heated_t, heated_v, wind_u, wind_v, wind_w)
+    temperature_out, vapor_out = advect(*fields, *halos(fields))
     radius_out, multiplicity_out = receive(sources(mults), mults, r2s)
-    winds = with_halo(jnp.stack([wind_u, wind_v]), (("gx", 1), ("gy", 2)), 1)
-    along_x = 0.5 * (winds[0, :-1, 1:-1] + winds[0, 1:, 1:-1])
-    along_y = 0.5 * (winds[1, 1:-1, :-1] + winds[1, 1:-1, 1:])
-    along_z = 0.5 * (wind_w[..., :-1] + wind_w[..., 1:])
-    start = jnp.stack([heated_t, heated_v])
-    section = start
-    for weight in (1.0 / 3.0, 0.5, 1.0):
-        section = start + advect_step * weight * tendency(
-            with_halo(section, (("gx", 1), ("gy", 2)), 1), along_x, along_y, along_z
-        )
-    return (section[0], section[1], radius_out, multiplicity_out)
+    return (temperature_out, vapor_out, radius_out, multiplicity_out)
 
 
 def solution(mesh):

time: 114 us -> 94.4 us (0.83)
  other arithmetic: 20.7 us -> 3.61 us
  starting transfers between devices: 28.9 us -> 16.4 us
  Pallas kernels: 28.9 us -> 39.7 us
  waiting for transfers between devices: 30 us -> 19.6 us
  local copies, waits for them, and re-layouts: 4.06 us -> 13.6 us
    ppermute x16 -> x4, starting transfers between devices: 20.1 us -> 5.04 us  [the longest x1 3.66 us: halos(): xhi = lax.ppermute(slabs(arrays, 0, 0), 'gx', down)]
    pallas_call x1 -> x2, Pallas kernels: 7.76 us -> 21.6 us  [the longest x1 14.9 us: advect(): pl.pallas_call(advect_kernel, out_shape=(o, o), in_specs=[ANY] * 5 + [VM]...]
    mul x12 -> x0, other arithmetic: 10 us -> none  [the longest x4 4.96 us: tendency(): flux_y = along_y * (0.5 * (middle_x[:, :, :-1] + middle_x[:, :, 1:]))]
    all_to_all x2, waiting for transfers between devices: 9.44 us -> 0.01 us  [exchange(): lax.all_to_all(rows.reshape((devices, -1) + rows.shape[1:]), ('gx', 'gy')...]
    unnamed x12 -> x18, local copies, waits for them, and re-layouts: 0.83 us -> 7.55 us
    add x3 -> x0, other arithmetic: 5.16 us -> none  [body(): start + advect_step * weight * tendency(with_halo(section, (('gx', 1), ('...]
    squeeze x1 -> x0, local copies, waits for them, and re-layouts: 3.03 us -> none  [body(): return (section[0], section[1], radius_out, multiplicity_out)]
    all_to_all x2, starting transfers between devices: 8.8 us -> 11.3 us  [exchange(): lax.all_to_all(rows.reshape((devices, -1) + rows.shape[1:]), ('gx', 'gy')...]
  transfers between devices with their start and end apart: 18 -> 6, of which waited for: 11 -> 4; matrix products, arithmetic and copies ran while one was open for 19% -> 15% of each run, Pallas kernels for 4% -> 33%
where the time goes in v1:
time: 94.4 us; the launch traced here: 93.6 us
  Pallas kernels  39.7 us (42%)
  waiting for transfers between devices  19.6 us (21%)
  starting transfers between devices  16.4 us (17%)
  local copies, waits for them, and re-layouts  13.6 us (14%)
  other arithmetic  3.61 us (4%)
    pallas_call x1, Pallas kernels, advect(): pl.pallas_call(advect_kernel, out_shape=(o, o), in_specs=[ANY] * 5 + [VM]...  14.9 us
    ppermute x1, waiting for transfers between devices, halos(): yhi = lax.ppermute(side(0), 'gy', down)  12.1 us
    all_to_all x2, starting transfers between devices, exchange(): lax.all_to_all(rows.reshape((devices, -1) + rows.shape[1:]), ('gx', 'gy')...  11.3 us
    pallas_call x1, Pallas kernels, home(): pl.pallas_call(home_kernel, out_shape=(jax.ShapeDtypeStruct(radius.shape,...  9.1 us
    unnamed x18, local copies, waits for them, and re-layouts  7.55 us
    pallas_call x1, Pallas kernels, scatter(): pl.pallas_call(scatter_kernel, out_shape=(o, o), in_specs=[SMEM()] * 2 +...  6.7 us
    pallas_call x1, Pallas kernels, receive(): pl.pallas_call(receive_kernel, out_shape=(out, out), in_specs=[SMEM(), VM...  6.11 us
    ppermute x1, waiting for transfers between devices, halos(): xlo = lax.ppermute(slabs(arrays, 0, nx - W), 'gx', up)  5.32 us
  transfers between devices with their start and end apart: 6, of which 4 were waited for; matrix products, arithmetic and copies ran while one was open for 15% of the time, Pallas kernels for 33%

profile of v1, /device:TPU:0, one launch (start us, length us, event | category | flops | bytes accessed | tf_op | source)
XLA Modules:
  0.0 93.6 jit_solution(9666714068501946697)
XLA Ops:
  0.6 1.4 %fusion.7 = (s32[8,128]{1,0:T(8,128)}, s32[1024]{0:T(1024)}, f32[8,128]{1,0:T(8,128)}, s32[1024]{0:T(1024)}, s32[1024]{0:T(1024)}) fusion(s32[1024]{0:T(1024)} %param.20, s32[1024]{0:T(1024)} %param.21), kind=kLoop, calls=%fused_computation.43 | loop fusion | flops 22528 | bytes 28672 | tf_op jit(solution)/shard_map/reshape | solution.py:89
  2.0 2.9 %place.1 = f32[1024,128]{1,0:T(8,128)} custom-call(s32[1024]{0:T(1024)} %get-tuple-element.56.slot, f32[1024,128]{1,0:T(8,128)} %mult.3), custom_call_target="tpu_custom_call" | custom-call | tf_op jit(solution)/shard_map/place/pallas_call | solution.py:38
  4.9 7.3 %all-to-all-start = ((f32[32,32,128]{2,1,0:T(8,128)}), f32[32,32,128]{2,1,0:T(8,128)S(1)}, u32[]{:S(2)}, u32[]{:S(2)}) async-start(f32[32,32,128]{2,1,0:T(8,128)} %bitcast.66), calls=%async_computation | async-start | bytes 1048576 | tf_op jit(solution)/shard_map/all_to_all | solution.py:386
  12.2 9.1 %home.1 = (f32[1024,128]{1,0:T(8,128)}, f32[8,128]{1,0:T(8,128)}, f32[8,128]{1,0:T(8,128)}, f32[8,128]{1,0:T(8,128)}, f32[8,128]{1,0:T(8,128)}) custom-call(s32[1024]{0:T(1024)} %get-tuple-element.56.slot, s32[1024]{0:T(1024)} %get-tuple-element.53.column, s32[8,128]{1,0:T(8,128)} %bitcast.78, s32[8,128]{1,0:T(8,128)} %get-tuple-element.52.level, ...), custom_call_target="tpu_custom_call" | custom-call | tf_op jit(solution)/shard_map/home/pallas_call | solution.py:85
  21.3 6.7 %scatter.1 = (f32[2048,128]{1,0:T(8,128)}, f32[2048,128]{1,0:T(8,128)}) custom-call(s32[1024]{0:T(1024)} %get-tuple-element.53.column, s32[1024]{0:T(1024)} %get-tuple-element.55.level, f32[8,128]{1,0:T(8,128)} %get-tuple-element.54.cellv, f32[8,128]{1,0:T(8,128)} %get-tuple-element.15.ht, f32[8,128]{1,0:T(8,128)} %get-tuple-element.16.hv, ...), custom_call_target="tpu_custom_call" | custom-call | tf_op jit(solution)/shard_map/scatter/pallas_call | solution.py:130
  28.0 0.8 fusion.10
  28.8 0.8 fusion.9
  29.7 0.8 bitcast_dynamic-update-slice_fusion.8
  30.6 0.8 bitcast_dynamic-update-slice_fusion.7
  31.4 0.8 bitcast_dynamic-update-slice_fusion.6
  32.2 3.7 %collective-permute-start.1 = (f32[5,3,32,128]{3,2,1,0:T(8,128)S(1)}, f32[5,3,32,128]{3,2,1,0:T(8,128)S(1)}, u32[]{:S(2)}, u32[]{:S(2)}) collective-permute-start(f32[5,3,32,128]{3,2,1,0:T(8,128)S(1)} %get-tuple-element.38), channel_id=1, source_target_pairs={{8,0},{16,8},{24,16},{0,24},{9,1},{17,9},{25,17},{1,25},{10,2},{18... | collective-permute-start | bytes 737288 | tf_op jit(solution)/shard_map/ppermute | solution.py:406
  35.9 0.0 collective-permute-start
  35.9 1.1 %fusion.2 = (f32[5,64,3,128]{3,2,1,0:T(4,128)S(1)}, f32[5,64,3,128]{3,2,1,0:T(4,128)S(1)}) fusion(f32[64,32,128]{2,1,0:T(8,128)} %bitcast.68), kind=kLoop, calls=%fused_computation.10 | loop fusion | bytes 458752
  37.0 1.1 %fusion.1 = (f32[5,64,3,128]{3,2,1,0:T(4,128)S(1)}, f32[5,64,3,128]{3,2,1,0:T(4,128)S(1)}) fusion(f32[5,64,3,128]{3,2,1,0:T(4,128)S(1)} %get-tuple-element.36, f32[64,32,128]{2,1,0:T(8,128)} %bitcast.70, f32[5,64,3,128]{3,2,1,0:T(4,128)S(1)} %get-tuple-element.37), kind=kLoop, calls=%fused_computation.8 | loop fusion | bytes 458752
  38.1 1.1 %bitcast_dynamic-update-slice_fusion.2 = (f32[5,64,3,128]{3,2,1,0:T(4,128)S(1)}, f32[5,64,3,128]{3,2,1,0:T(4,128)S(1)}) fusion(f32[5,64,3,128]{3,2,1,0:T(4,128)S(1)} %get-tuple-element.34, f32[64,32,128]{2,1,0:T(8,128)} %uc.1, f32[5,64,3,128]{3,2,1,0:T(4,128)S(1)} %get-tuple-element.35), kind=kLoop, calls=%fused_computation.17 | loop fusion | bytes 458752
  39.2 1.1 %bitcast_dynamic-update-slice_fusion.1 = (f32[5,64,3,128]{3,2,1,0:T(4,128)S(1)}, f32[5,64,3,128]{3,2,1,0:T(4,128)S(1)}) fusion(f32[5,64,3,128]{3,2,1,0:T(4,128)S(1)} %get-tuple-element.32, f32[64,32,128]{2,1,0:T(8,128)} %vw.1, f32[5,64,3,128]{3,2,1,0:T(4,128)S(1)} %get-tuple-element.33), kind=kLoop, calls=%fused_computation.16 | loop fusion | bytes 458752
  40.3 1.1 %bitcast_dynamic-update-slice_fusion = (f32[5,64,3,128]{3,2,1,0:T(4,128)S(1)}, f32[5,64,3,128]{3,2,1,0:T(4,128)S(1)}) fusion(f32[5,64,3,128]{3,2,1,0:T(4,128)S(1)} %get-tuple-element.30, f32[64,32,128]{2,1,0:T(8,128)} %wc.1, f32[5,64,3,128]{3,2,1,0:T(4,128)S(1)} %get-tuple-element.31), kind=kLoop, calls=%fused_computation.15 | loop fusion | bytes 458752 | tf_op jit(solution)/shard_map/stack | solution.py:399
  41.4 0.9 collective-permute-done.1.xhi
  42.3 0.0 copy-start.2
  42.3 5.3 %collective-permute-done.xlo = f32[5,3,32,128]{3,2,1,0:T(8,128)S(1)} collective-permute-done((f32[5,3,32,128]{3,2,1,0:T(8,128)S(1)}, f32[5,3,32,128]{3,2,1,0:T(8,128)S(1)}, u32[]{:S(2)}, u32[]{:S(2)}) %collective-permute-start) | collective-permute-done | bytes 245792 | tf_op jit(solution)/shard_map/ppermute | solution.py:405
  47.6 0.0 copy-start.3
  47.6 0.7 copy-done.3
  48.3 0.2 pad_maximum_fusion.1
  48.5 0.0 copy-done.2
  48.5 1.3 %collective-permute-start.3 = (f32[5,70,3,128]{3,1,2,0:T(8,128)S(1)}, f32[5,70,3,128]{3,1,2,0:T(8,128)S(1)}, u32[]{:S(2)}, u32[]{:S(2)}) collective-permute-start(f32[5,70,3,128]{3,1,2,0:T(8,128)S(1)} %copy.20), channel_id=1, source_target_pairs={{1,0},{2,1},{3,2},{4,3},{5,4},{6,5},{7,6},{0,7},{9,8},{10,9},{11,1... | collective-permute-start | bytes 1612808 | tf_op jit(solution)/shard_map/ppermute | solution.py:414
  49.9 0.2 pad_maximum_fusion
  50.1 0.1 collective-permute-start.2
  50.1 0.0 all-to-all-done
  50.2 0.0 copy-start
  50.2 4.0 %all-to-all-start.1 = ((f32[32,32,128]{2,1,0:T(8,128)}), f32[32,32,128]{2,1,0:T(8,128)S(1)}, u32[]{:S(2)}, u32[]{:S(2)}) async-start(f32[32,32,128]{2,1,0:T(8,128)} %bitcast.72), calls=%async_computation.1 | async-start | bytes 1048576 | tf_op jit(solution)/shard_map/all_to_all | solution.py:386
  54.2 12.1 %collective-permute-done.3 = f32[5,70,3,128]{3,1,2,0:T(8,128)S(1)} collective-permute-done((f32[5,70,3,128]{3,1,2,0:T(8,128)S(1)}, f32[5,70,3,128]{3,1,2,0:T(8,128)S(1)}, u32[]{:S(2)}, u32[]{:S(2)}) %collective-permute-start.3) | collective-permute-done | bytes 537632 | tf_op jit(solution)/shard_map/ppermute | solution.py:414
  66.3 1.1 %copy.22.yhi = f32[5,70,3,128]{3,2,1,0:T(4,128)} copy(f32[5,70,3,128]{3,1,2,0:T(8,128)S(1)} %collective-permute-done.3) | data formatting | bytes 1075200 | tf_op jit(solution)/shard_map/ppermute | solution.py:414
  67.4 1.2 %collective-permute-done.2 = f32[5,70,3,128]{3,1,2,0:T(8,128)S(1)} collective-permute-done((f32[5,70,3,128]{3,1,2,0:T(8,128)S(1)}, f32[5,70,3,128]{3,1,2,0:T(8,128)S(1)}, u32[]{:S(2)}, u32[]{:S(2)}) %collective-permute-start.2) | collective-permute-done | bytes 537632 | tf_op jit(solution)/shard_map/ppermute | solution.py:413
  68.6 1.1 %copy.21.ylo = f32[5,70,3,128]{3,2,1,0:T(4,128)} copy(f32[5,70,3,128]{3,1,2,0:T(8,128)S(1)} %collective-permute-done.2) | data formatting | bytes 1075200 | tf_op jit(solution)/shard_map/ppermute | solution.py:413
  69.6 14.9 %advect.1 = (f32[64,32,128]{2,1,0:T(8,128)}, f32[64,32,128]{2,1,0:T(8,128)}) custom-call(f32[64,32,128]{2,1,0:T(8,128)} %bitcast.69, f32[64,32,128]{2,1,0:T(8,128)} %bitcast.71, f32[64,32,128]{2,1,0:T(8,128)} %uc.1, f32[64,32,128]{2,1,0:T(8,128)} %vw.1, f32[64,32,128]{2,1,0:T(8,128)} %wc.1, f32[5,3,32,128]{3,2,1,0:T(8,128)} %copy-done.3, ...), custom_call_target="tpu_custom_call" | custom-call | tf_op jit(solution)/shard_map/advect/pallas_call | solution.py:339
  84.6 0.0 copy-done
  84.6 0.2 fusion.8
  84.8 0.2 convert_reduce_fusion
  85.0 0.3 reduce-window.9
  85.3 0.1 slice.111
  85.4 0.1 slice_reduce_fusion
  85.5 0.1 add_bitcast_fusion
  85.6 1.1 %select_reduce_fusion.src = s32[512]{0:T(512)} fusion(s32[1024]{0:T(1024)S(1)} %add_bitcast_fusion, pred[1024]{0:T(1024)(128)(4,1)S(1)} %get-tuple-element.26), kind=kLoop, calls=%fused_computation | loop fusion | flops 2096640 | bytes 7168 | tf_op jit(solution)/shard_map/reduce_sum | solution.py:382
  86.7 0.0 all-to-all-done.1
  86.7 0.0 copy-start.1
  86.7 0.8 copy-done.1
  87.5 6.1 %receive.1 = (f32[512,128]{1,0:T(8,128)}, f32[512,128]{1,0:T(8,128)}) custom-call(s32[512]{0:T(512)} %select_reduce_fusion.src, f32[1024,128]{1,0:T(8,128)} %bitcast.61, f32[1024,128]{1,0:T(8,128)} %bitcast.67), custom_call_target="tpu_custom_call" | custom-call | tf_op jit(solution)/shard_map/receive/pallas_call | solution.py:368
  (9 shorter events, 0.2 us)
Async XLA Ops:
  4.9 45.3 %all-to-all-start = ((f32[32,32,128]{2,1,0:T(8,128)}), f32[32,32,128]{2,1,0:T(8,128)S(1)}, u32[]{:S(2)}, u32[]{:S(2)}) async-start(f32[32,32,128]{2,1,0:T(8,128)} %bitcast.66), calls=%async_computation | async-start | bytes 1048576 | tf_op jit(solution)/shard_map/all_to_all | solution.py:386
  32.2 10.1 %collective-permute-start.1 = (f32[5,3,32,128]{3,2,1,0:T(8,128)S(1)}, f32[5,3,32,128]{3,2,1,0:T(8,128)S(1)}, u32[]{:S(2)}, u32[]{:S(2)}) collective-permute-start(f32[5,3,32,128]{3,2,1,0:T(8,128)S(1)} %get-tuple-element.38), channel_id=1, source_target_pairs={{8,0},{16,8},{24,16},{0,24},{9,1},{17,9},{25,17},{1,25},{10,2},{18... | collective-permute-start | bytes 737288 | tf_op jit(solution)/shard_map/ppermute | solution.py:406
  35.9 11.7 %collective-permute-start = (f32[5,3,32,128]{3,2,1,0:T(8,128)S(1)}, f32[5,3,32,128]{3,2,1,0:T(8,128)S(1)}, u32[]{:S(2)}, u32[]{:S(2)}) collective-permute-start(f32[5,3,32,128]{3,2,1,0:T(8,128)S(1)} %get-tuple-element.39), channel_id=1, source_target_pairs={{0,8},{8,16},{16,24},{24,0},{1,9},{9,17},{17,25},{25,1},{2,10},{10... | collective-permute-start | bytes 737288 | tf_op jit(solution)/shard_map/ppermute | solution.py:405
  42.3 6.3 %copy-start.2 = (f32[5,3,32,128]{3,2,1,0:T(8,128)}, f32[5,3,32,128]{3,2,1,0:T(8,128)S(1)}, u32[]{:S(2)}) copy-start(f32[5,3,32,128]{3,2,1,0:T(8,128)S(1)} %collective-permute-done.1.xhi) | copy-start | bytes 737284
  47.6 0.7 copy-start.3
  48.5 17.8 %collective-permute-start.3 = (f32[5,70,3,128]{3,1,2,0:T(8,128)S(1)}, f32[5,70,3,128]{3,1,2,0:T(8,128)S(1)}, u32[]{:S(2)}, u32[]{:S(2)}) collective-permute-start(f32[5,70,3,128]{3,1,2,0:T(8,128)S(1)} %copy.20), channel_id=1, source_target_pairs={{1,0},{2,1},{3,2},{4,3},{5,4},{6,5},{7,6},{0,7},{9,8},{10,9},{11,1... | collective-permute-start | bytes 1612808 | tf_op jit(solution)/shard_map/ppermute | solution.py:414
  50.1 18.5 %collective-permute-start.2 = (f32[5,70,3,128]{3,1,2,0:T(8,128)S(1)}, f32[5,70,3,128]{3,1,2,0:T(8,128)S(1)}, u32[]{:S(2)}, u32[]{:S(2)}) collective-permute-start(f32[5,70,3,128]{3,1,2,0:T(8,128)S(1)} %copy.19), channel_id=1, source_target_pairs={{0,1},{1,2},{2,3},{3,4},{4,5},{5,6},{6,7},{7,0},{8,9},{9,10},{10,1... | collective-permute-start | bytes 1612808 | tf_op jit(solution)/shard_map/ppermute | solution.py:413
  50.2 34.5 %copy-start = (f32[32,32,128]{2,1,0:T(8,128)}, f32[32,32,128]{2,1,0:T(8,128)S(1)}, u32[]{:S(2)}) copy-start(f32[32,32,128]{2,1,0:T(8,128)S(1)} %all-to-all-done) | copy-start | bytes 1572868
  50.2 36.5 %all-to-all-start.1 = ((f32[32,32,128]{2,1,0:T(8,128)}), f32[32,32,128]{2,1,0:T(8,128)S(1)}, u32[]{:S(2)}, u32[]{:S(2)}) async-start(f32[32,32,128]{2,1,0:T(8,128)} %bitcast.72), calls=%async_computation.1 | async-start | bytes 1048576 | tf_op jit(solution)/shard_map/all_to_all | solution.py:386
  86.7 0.8 copy-start.1

commit v2 on v1

--- a/solution.py
+++ b/solution.py
@@ -15,6 +15,7 @@
 advect_step = 0.6
 clausius = 0.07; growth = 200.0 / 3.0; solute = 0.05; condense = 5e-07; latent = 10.0
 SMEM=lambda: pl.BlockSpec(memory_space=pltpu.SMEM)
+ANY=lambda: pl.BlockSpec(memory_space=pl.ANY)
 VM=lambda: pl.BlockSpec(memory_space=pltpu.VMEM)
 
 def row_loop(n, unroll, fn):
@@ -39,13 +40,19 @@
         in_specs=[SMEM(),VM()],out_specs=VM(),
         scratch_shapes=[pltpu.VMEM((n+SUB,LAN),jnp.float32)],name="place")(slot,mult)
 
-def home_kernel(slot,column,count,level,radius,floor,mult,tp,vp,send,ht,hv,ct,cv,rows_t,rows_v,buf):
+def home_kernel(slot,column,count,level,radius_,floor_,mult_,tp_,vp_,send,ht,hv,ct,cv,rows_t,rows_v,buf,radius,floor,mult,tp,vp,sem):
     n=radius.shape[0]
+    pairs_=((tp_,tp),(vp_,vp),(radius_,radius),(floor_,floor),(mult_,mult))
+    loads=[pltpu.make_async_copy(a,b,sem.at[i]) for i,(a,b) in enumerate(pairs_)]
+    for c in loads: c.start()
+    buf[...]=jnp.zeros_like(buf)
+    for c in loads[:2]: c.wait()
     def fetch(b):
         c=column[b]
         rows_t[pl.ds(b,1),:]=tp[pl.ds(c,1),:]
         rows_v[pl.ds(b,1),:]=vp[pl.ds(c,1),:]
     row_loop(n,32,fetch)
+    for c in loads[2:]: c.wait()
     depth=lax.broadcasted_iota(jnp.int32,(LAN,LAN),0)
     def tile(t,_):
         sl=pl.ds(pl.multiple_of(t*LAN,LAN),LAN)
@@ -72,7 +79,6 @@
         rows_t[sl,:]=jnp.transpose(jnp.where(alive,r2,0.0))
         return 0
     lax.fori_loop(0,n//LAN,tile,0)
-    buf[...]=jnp.zeros_like(buf)
     def put(b):
         buf[pl.ds(slot[b],1),:]=rows_t[pl.ds(b,1),:]
     row_loop(n,32,put)
@@ -84,13 +90,22 @@
     tab=jax.ShapeDtypeStruct((g,LAN),jnp.float32)
     return pl.pallas_call(home_kernel,
         out_shape=(jax.ShapeDtypeStruct(radius.shape,jnp.float32),tab,tab,tab,tab),
-        in_specs=[SMEM(),SMEM()]+[VM()]*7,out_specs=(VM(),)*5,
-        scratch_shapes=[pltpu.VMEM((n,LAN),jnp.float32),pltpu.VMEM((n,LAN),jnp.float32),pltpu.VMEM((n+SUB,LAN),jnp.float32)],
+        in_specs=[SMEM(),SMEM(),VM(),VM()]+[ANY()]*5,out_specs=(VM(),)*5,
+        scratch_shapes=[pltpu.VMEM((n,LAN),jnp.float32)]*2+[pltpu.VMEM((n+SUB,LAN),jnp.float32)]+[pltpu.VMEM((n,LAN),jnp.float32)]*3+[pltpu.VMEM((tp.size//levels,levels),jnp.float32)]*2+[pltpu.SemaphoreType.DMA((5,))],
         name="home")(slot,column,count.reshape(g,LAN),level.reshape(g,LAN),radius,floor,mult,
                      tp.reshape(-1,levels),vp.reshape(-1,levels))
 
-def scatter_kernel(column,level,cellv,ht,hv,ct,cv,tp,vp,ot,ov,vt,vv,acct,accv):
+def scatter_kernel(column,level,cellv,ht,hv,ct,cv,tp,vp,wu,wv,ww,ot,ov,xfirst,xlast,yfirst,ylast,vt,vv,acct,accv,wlo,whi,sem):
     g=cellv.shape[0]; n=g*LAN
+    nx,ny=tp.shape[:2]
+    winds=(wu,wv,ww)
+    loads=[pltpu.make_async_copy(tp,ot,sem.at[0]),pltpu.make_async_copy(vp,ov,sem.at[1])]
+    for i,w in enumerate(winds):
+        loads+=[pltpu.make_async_copy(w.at[:,pl.ds(0,SUB)],wlo.at[i],sem.at[2+i]),
+                pltpu.make_async_copy(w.at[:,pl.ds(ny-SUB,SUB)],whi.at[i],sem.at[5+i]),
+                pltpu.make_async_copy(w.at[pl.ds(0,W)],xfirst.at[2+i],sem.at[8+i]),
+                pltpu.make_async_copy(w.at[pl.ds(nx-W,W)],xlast.at[2+i],sem.at[11+i])]
+    for c in loads: c.start()
     spread=lambda ref,t: jnp.transpose(jnp.broadcast_to(ref[pl.ds(t,1),:],(LAN,LAN)))
     acct[...]=jnp.zeros_like(acct); accv[...]=jnp.zeros_like(accv)
     def source(t,_):
@@ -115,22 +130,34 @@
         vv[sl,:]=jnp.transpose(jnp.broadcast_to(nv,(LAN,LAN)))
         return 0
     lax.fori_loop(0,g,rows,0)
-    ot[...]=tp[...]; ov[...]=vp[...]
+    for c in loads: c.wait()
     lane=lax.broadcasted_iota(jnp.int32,(1,LAN),1)
+    flat_t=ot.reshape(nx*ny,LAN); flat_v=ov.reshape(nx*ny,LAN)
     def put(b):
         c=column[b]; hit=lane==level[b]
-        pltpu.store(ot.at[pl.ds(c,1),:],vt[pl.ds(b,1),:],mask=hit)
-        pltpu.store(ov.at[pl.ds(c,1),:],vv[pl.ds(b,1),:],mask=hit)
+        pltpu.store(flat_t.at[pl.ds(c,1),:],vt[pl.ds(b,1),:],mask=hit)
+        pltpu.store(flat_v.at[pl.ds(c,1),:],vv[pl.ds(b,1),:],mask=hit)
     row_loop(n,32,put)
-
-def scatter(column,level,cell,ht,hv,ct,cv,tp,vp):
+    for i,o in enumerate((ot,ov)):
+        xfirst[i]=o[0:W]; xlast[i]=o[nx-W:nx]
+    def side(x,_):
+        at=pl.ds(x*W,W)
+        for i,o in enumerate((ot,ov)):
+            yfirst[i,at,:]=o[x,0:W,:]; ylast[i,at,:]=o[x,ny-W:ny,:]
+        for i in range(3):
+            yfirst[2+i,at,:]=wlo[i,x,0:W,:]; ylast[2+i,at,:]=whi[i,x,SUB-W:SUB,:]
+        return 0
+    lax.fori_loop(0,nx,side,0,unroll=4)
+
+def scatter(column,level,cell,ht,hv,ct,cv,tp,vp,*winds):
     g=ht.shape[0]; n=g*LAN
-    t2=tp.reshape(-1,LAN); v2=vp.reshape(-1,LAN)
-    o=jax.ShapeDtypeStruct(t2.shape,jnp.float32)
-    a,b=pl.pallas_call(scatter_kernel,out_shape=(o,o),in_specs=[SMEM()]*2+[VM()]*7,out_specs=(VM(),VM()),
-        scratch_shapes=[pltpu.VMEM((n,LAN),jnp.float32)]*2+[pltpu.VMEM((g*SUB,LAN),jnp.float32)]*2,
-        name="scatter")(column,level,cell.reshape(g,LAN).astype(jnp.float32),ht,hv,ct,cv,t2,v2)
-    return a.reshape(tp.shape),b.reshape(vp.shape)
+    nx,ny,nz=tp.shape
+    S=lambda *d: jax.ShapeDtypeStruct(d,jnp.float32)
+    return pl.pallas_call(scatter_kernel,out_shape=(S(nx,ny,nz),)*2+(S(5,W,ny,nz),)*2+(S(5,nx*W,nz),)*2,
+        in_specs=[SMEM()]*2+[VM()]*5+[ANY()]*5,out_specs=(VM(),)*6,
+        scratch_shapes=[pltpu.VMEM((n,LAN),jnp.float32)]*2+[pltpu.VMEM((g*SUB,LAN),jnp.float32)]*2
+            +[pltpu.VMEM((3,nx,SUB,nz),jnp.float32)]*2+[pltpu.SemaphoreType.DMA((14,))],
+        name="scatter")(column,level,cell.reshape(g,LAN).astype(jnp.float32),ht,hv,ct,cv,tp,vp,*winds)
 
 
 def batcher(n):
@@ -242,21 +269,28 @@
 W=3
 UNROLL=8
 
-def advect_kernel(tc,vc,uc,vw,wc,xlo,xhi,ylo,yhi,ot,ov,f,ax,ay,az,ad,s1,s2,sem):
+def advect_kernel(tc,vc,uc,vw,wc,xlo_,xhi_,ylo_,yhi_,clo_,chi_,ot_,ov_,f,ax,ay,az,ad,s1,s2,ot,ov,xlo,xhi,ylo,yhi,clo,chi,sem,osem):
     nx,ny,_=tc.shape
     nt=ny//SUB+1
-    copies=[pltpu.make_async_copy(c,f.at[i,pl.ds(W,nx),pl.ds(0,ny)],sem.at[i]) for i,c in enumerate((tc,vc,uc,vw,wc))]
-    for c in copies: c.start()
-    def sides(x,_):
-        for i in range(5):
-            f[i,x,ny:ny+W,:]=yhi[i,x]
-            f[i,x,ny+SUB-W:ny+SUB,:]=ylo[i,x]
-        return 0
-    lax.fori_loop(0,nx+2*W,sides,0)
+    small=[pltpu.make_async_copy(a,b,sem.at[5+i]) for i,(a,b) in enumerate(zip((xlo_,xhi_,ylo_,yhi_,clo_,chi_),(xlo,xhi,ylo,yhi,clo,chi)))]
+    big=[pltpu.make_async_copy(c,f.at[i,pl.ds(W,nx),pl.ds(0,ny)],sem.at[i]) for i,c in enumerate((tc,vc,uc,vw,wc))]
+    for c in small: c.start()
+    for c in big[2:]+big[:2]: c.start()
+    for c in small: c.wait()
+    hi=slice(ny,ny+W); lo=slice(ny+SUB-W,ny+SUB)
     for i in range(5):
         f[i,0:W,0:ny,:]=xlo[i]
         f[i,W+nx:W+nx+W,0:ny,:]=xhi[i]
-    for c in copies: c.wait()
+        for x in range(W):
+            f[i,x,hi,:]=chi[0,i,x]; f[i,x,lo,:]=clo[0,i,x]
+            f[i,W+nx+x,hi,:]=chi[1,i,x]; f[i,W+nx+x,lo,:]=clo[1,i,x]
+    def sides(x,_):
+        for i in range(5):
+            f[i,W+x,hi,:]=yhi[i,pl.ds(x*W,W),:]
+            f[i,W+x,lo,:]=ylo[i,pl.ds(x*W,W),:]
+        return 0
+    lax.fori_loop(0,nx,sides,0,unroll=4)
+    for c in big[2:]: c.wait()
     scale=0.25*advect_step
     lane=lax.broadcasted_iota(jnp.int32,(SUB,LAN),1)
     first=lane==0; last=lane==LAN-1
@@ -293,7 +327,7 @@
                 ad[x,rows(t),:]=jnp.where(first,0.0,scale*dn)
         return 0
     lax.fori_loop(0,pl.cdiv(nx+2*W,UNROLL),coef,0)
-    def section(weight,src,dst,margin,count):
+    def section(weight,src,dst,margin,count,after=lambda g: None):
         edge=tuple(ax[margin-1,rows(t),:]*(src[i,margin-1,rows(t),:]+src[i,margin,rows(t),:]) for i in range(2) for t in range(count))
         def planes(g,prev):
             x0=margin+g*UNROLL
@@ -312,6 +346,7 @@
                         dst(i,x,t,f[i,x,rows(t),:]-weight*d)
                         nxt.append(gx)
                 prev=tuple(nxt)
+            after(g)
             return prev
         lax.fori_loop(0,pl.cdiv(nx+2*W-2*margin,UNROLL),planes,edge)
     def put(buf):
@@ -319,9 +354,17 @@
         return g
     def out(i,x,t,val):
         (ot,ov)[i][x-W,rows(t),:]=val
+    for c in big[:2]: c.wait()
     section(1.0/3.0,f,put(s1),1,nt)
     section(0.5,s1,put(s2),2,nt)
-    section(1.0,s2,out,3,nt-1)
+    def drain(g):
+        at=pl.ds(g*UNROLL,UNROLL)
+        return [pltpu.make_async_copy(a.at[at],b.at[at],osem.at[i]) for i,(a,b) in enumerate(((ot,ot_),(ov,ov_)))]
+    def flush(g):
+        for c in drain(g): c.start()
+    section(1.0,s2,out,3,nt-1,flush)
+    for g in range(nx//UNROLL):
+        for c in drain(g): c.wait()
 
 def pair_matrix():
     k=lax.broadcasted_iota(jnp.int32,(2*LAN,2*LAN),0)
@@ -331,14 +374,16 @@
     other=jnp.where(n>=LAN,o-1,o+1)
     return jnp.where((z==o)|(z==other),1.0,0.0).astype(jnp.bfloat16)
 
-def advect(t,v,u,w2,w3,xlo,xhi,ylo,yhi):
+def advect(t,v,u,w2,w3,*edges):
     nx,ny,nz=t.shape
     o=jax.ShapeDtypeStruct(t.shape,jnp.float32)
     ext=(pl.cdiv(nx+2*W,UNROLL)*UNROLL+SUB,ny+SUB,nz)
-    ANY=pl.BlockSpec(memory_space=pl.ANY); VM=pl.BlockSpec(memory_space=pltpu.VMEM)
-    return pl.pallas_call(advect_kernel,out_shape=(o,o),in_specs=[ANY]*5+[VM]*4,out_specs=(VM,VM),
-        scratch_shapes=[pltpu.VMEM((5,)+ext,jnp.float32)]+[pltpu.VMEM(ext,jnp.float32)]*4+[pltpu.VMEM((2,)+ext,jnp.float32)]*2+[pltpu.SemaphoreType.DMA((5,))],
-        name="advect")(t,v,u,w2,w3,xlo,xhi,ylo,yhi)
+    ANY=pl.BlockSpec(memory_space=pl.ANY)
+    return pl.pallas_call(advect_kernel,out_shape=(o,o),in_specs=[ANY]*11,out_specs=(ANY,ANY),
+        scratch_shapes=[pltpu.VMEM((5,)+ext,jnp.float32)]+[pltpu.VMEM(ext,jnp.float32)]*4+[pltpu.VMEM((2,)+ext,jnp.float32)]*2
+            +[pltpu.VMEM(t.shape,jnp.float32)]*2+[pltpu.VMEM(e.shape,jnp.float32) for e in edges]
+            +[pltpu.SemaphoreType.DMA((11,)),pltpu.SemaphoreType.DMA((2,))],
+        name="advect")(t,v,u,w2,w3,*edges)
 
 
 def receive_kernel(src, mults, r2s, ro_ref, mo_ref, mrow, rrow):
@@ -395,24 +440,18 @@
     return up, [(j, i) for i, j in up]
 
 
-def slabs(arrays, dim, start):
-    return jnp.stack([lax.slice_in_dim(a, start, start + W, axis=dim) for a in arrays])
-
-
-def halos(arrays):
-    nx, ny = arrays[0].shape[:2]
+def halos(xfirst, xlast, yfirst, ylast):
+    ny = xfirst.shape[2]
     up, down = shifts("gx")
-    xlo = lax.ppermute(slabs(arrays, 0, nx - W), "gx", up)
-    xhi = lax.ppermute(slabs(arrays, 0, 0), "gx", down)
+    xlo = lax.ppermute(xlast, "gx", up)
+    xhi = lax.ppermute(xfirst, "gx", down)
     up, down = shifts("gy")
-
-    def side(start):
-        ends = [x[:, :, start : start + W] for x in (xlo, xhi)]
-        return jnp.concatenate([ends[0], slabs(arrays, 1, start), ends[1]], axis=1)
-
-    ylo = lax.ppermute(side(ny - W), "gy", up)
-    yhi = lax.ppermute(side(0), "gy", down)
-    return xlo, xhi, ylo, yhi
+    ylo = lax.ppermute(ylast, "gy", up)
+    yhi = lax.ppermute(yfirst, "gy", down)
+    ends = jnp.stack([xlo, xhi])
+    clo = lax.ppermute(ends[:, :, :, ny - W :], "gy", up)
+    chi = lax.ppermute(ends[:, :, :, :W], "gy", down)
+    return xlo, xhi, ylo, yhi, clo, chi
 
 
 def body(
@@ -431,16 +470,18 @@
     devices = lax.axis_size("gx") * lax.axis_size("gy")
     levels = tprime.shape[2]
     slot = jnp.where(move_list >= 0, move_list, multiplicity.shape[0])
-    column = cell_index // levels
-    level = cell_index % levels
+    column = lax.shift_right_logical(cell_index, levels.bit_length() - 1)
+    level = cell_index & (levels - 1)
     mults = exchange(place(slot, multiplicity), devices)
     sent, ht, hv, ct, cv = home(
         slot, column, level, drop_counts, radius, min_radius, multiplicity, tprime, vapor
     )
     r2s = exchange(sent, devices)
-    heated_t, heated_v = scatter(column, level, cell_index, ht, hv, ct, cv, tprime, vapor)
-    fields = (heated_t, heated_v, wind_u, wind_v, wind_w)
-    temperature_out, vapor_out = advect(*fields, *halos(fields))
+    winds = (wind_u, wind_v, wind_w)
+    heated_t, heated_v, *edges = scatter(
+        column, level, cell_index, ht, hv, ct, cv, tprime, vapor, *winds
+    )
+    temperature_out, vapor_out = advect(heated_t, heated_v, *winds, *halos(*edges))
     radius_out, multiplicity_out = receive(sources(mults), mults, r2s)
     return (temperature_out, vapor_out, radius_out, multiplicity_out)
 

time: 94.4 us -> 75.2 us (0.80)
  local copies, waits for them, and re-layouts: 13.6 us -> 1.93 us
  waiting for transfers between devices: 19.6 us -> 13.1 us
  Pallas kernels: 39.7 us -> 38.1 us
  starting transfers between devices: 16.4 us -> 17.5 us
    ppermute x4 -> x6, waiting for transfers between devices: 19.6 us -> 13.1 us  [the longest x1 3.96 us: halos(): xhi = lax.ppermute(xfirst, 'gx', down)]
    unnamed x18 -> x16, local copies, waits for them, and re-layouts: 7.55 us -> 1.74 us
    ppermute x2 -> x0, local copies, waits for them, and re-layouts: 2.12 us -> none  [the longest x1 1.06 us: halos(): yhi = lax.ppermute(side(0), 'gy', down)]
    ppermute x4 -> x6, starting transfers between devices: 5.04 us -> 7.08 us  [the longest x1 2.39 us: halos(): yhi = lax.ppermute(yfirst, 'gy', down)]
    another operation x3 -> x1, local copies, waits for them, and re-layouts: 2.04 us -> 0.12 us  [the longest x2 1.93 us: slabs(): jnp.stack([lax.slice_in_dim(a, start, start + W, axis=dim) for a in arrays])]
    pallas_call x2, Pallas kernels: 21.6 us -> 19.7 us  [the longest x1 12.8 us: advect(): pl.pallas_call(advect_kernel, out_shape=(o, o), in_specs=[ANY] * 11, out_...]
    slice x5 -> x1, local copies, waits for them, and re-layouts: 1.76 us -> 0.07 us  [the longest x2 1.66 us: slabs(): lax.slice_in_dim(a, start, start + W, axis=dim)]
  transfers between devices with their start and end apart: 6 -> 8, of which waited for: 4 -> 4; matrix products, arithmetic and copies ran while one was open for 15% -> 3% of each run, Pallas kernels for 33% -> 39%
where the time goes in v2:
time: 75.2 us; the launch traced here: 74.6 us
  Pallas kernels  38.1 us (51%)
  starting transfers between devices  17.5 us (23%)
  waiting for transfers between devices  13.1 us (17%)
  other arithmetic  3.26 us (4%)
  local copies, waits for them, and re-layouts  1.93 us (3%)
    pallas_call x1, Pallas kernels, advect(): pl.pallas_call(advect_kernel, out_shape=(o, o), in_specs=[ANY] * 11, out_...  12.8 us
    all_to_all x2, starting transfers between devices, exchange(): lax.all_to_all(rows.reshape((devices, -1) + rows.shape[1:]), ('gx', 'gy')...  10.5 us
    pallas_call x1, Pallas kernels, home(): pl.pallas_call(home_kernel, out_shape=(jax.ShapeDtypeStruct(radius.shape,...  9.38 us
    pallas_call x1, Pallas kernels, scatter(): pl.pallas_call(scatter_kernel, out_shape=(S(nx, ny, nz),) * 2 + (S(5, W,...  6.95 us
    pallas_call x1, Pallas kernels, receive(): pl.pallas_call(receive_kernel, out_shape=(out, out), in_specs=[SMEM(), VM...  6.11 us
    ppermute x1, waiting for transfers between devices, halos(): xhi = lax.ppermute(xfirst, 'gx', down)  3.96 us
    ppermute x1, waiting for transfers between devices, halos(): xlo = lax.ppermute(xlast, 'gx', up)  3.91 us
    ppermute x1, waiting for transfers between devices, halos(): clo = lax.ppermute(ends[:, :, :, ny - W:], 'gy', up)  3.11 us
  transfers between devices with their start and end apart: 8, of which 4 were waited for; matrix products, arithmetic and copies ran while one was open for 3% of the time, Pallas kernels for 39%

profile of v2, /device:TPU:0, one launch (start us, length us, event | category | flops | bytes accessed | tf_op | source)
XLA Modules:
  0.0 74.6 jit_solution(5724711864140832646)
XLA Ops:
  0.6 1.4 %fusion.1 = (s32[8,128]{1,0:T(8,128)}, s32[1024]{0:T(1024)}, f32[8,128]{1,0:T(8,128)}, s32[1024]{0:T(1024)}, s32[1024]{0:T(1024)}) fusion(s32[1024]{0:T(1024)} %param.20, s32[1024]{0:T(1024)} %param.21), kind=kLoop, calls=%fused_computation.13 | loop fusion | flops 5120 | bytes 28672 | tf_op jit(solution)/shard_map/reshape | solution.py:95
  2.0 2.9 %place.1 = f32[1024,128]{1,0:T(8,128)} custom-call(s32[1024]{0:T(1024)} %get-tuple-element.42.slot, f32[1024,128]{1,0:T(8,128)} %mult.1), custom_call_target="tpu_custom_call" | custom-call | tf_op jit(solution)/shard_map/place/pallas_call | solution.py:39
  4.9 7.3 %all-to-all-start = ((f32[32,32,128]{2,1,0:T(8,128)}), f32[32,32,128]{2,1,0:T(8,128)S(1)}, u32[]{:S(2)}, u32[]{:S(2)}) async-start(f32[32,32,128]{2,1,0:T(8,128)} %bitcast.21), calls=%async_computation | async-start | bytes 1048576 | tf_op jit(solution)/shard_map/all_to_all | solution.py:431
  12.2 9.4 %home.1 = (f32[1024,128]{1,0:T(8,128)}, f32[8,128]{1,0:T(8,128)}, f32[8,128]{1,0:T(8,128)}, f32[8,128]{1,0:T(8,128)}, f32[8,128]{1,0:T(8,128)}) custom-call(s32[1024]{0:T(1024)} %get-tuple-element.42.slot, s32[1024]{0:T(1024)} %get-tuple-element.39.column, s32[8,128]{1,0:T(8,128)} %bitcast.25, s32[8,128]{1,0:T(8,128)} %get-tuple-element.38.level, ...), custom_call_target="tpu_custom_call" | custom-call | tf_op jit(solution)/shard_map/home/pallas_call | solution.py:91
  21.6 7.0 %scatter.1 = (f32[64,32,128]{2,1,0:T(8,128)}, f32[64,32,128]{2,1,0:T(8,128)}, f32[5,3,32,128]{3,2,1,0:T(8,128)}, f32[5,3,32,128]{3,2,1,0:T(8,128)}, f32[5,192,128]{2,1,0:T(8,128)}, /*index=5*/f32[5,192,128]{2,1,0:T(8,128)}) custom-call(s32[1024]{0:T(1024)} %get-tuple-element.39.column, s32[1024]{0:T(1024)} %get-tuple-element.41.level, ...), custom_call_target="tpu_custom_call" | custom-call | tf_op jit(solution)/shard_map/scatter/pallas_call | solution.py:156
  28.6 0.3 collective-permute-start.2
  28.9 2.4 %collective-permute-start.3 = (f32[5,192,128]{2,1,0:T(8,128)}, f32[5,192,128]{2,1,0:T(8,128)S(1)}, u32[]{:S(2)}, u32[]{:S(2)}) collective-permute-start(f32[5,192,128]{2,1,0:T(8,128)} %get-tuple-element.28), channel_id=1, source_target_pairs={{1,0},{2,1},{3,2},{4,3},{5,4},{6,5},{7,6},{0,7},{9,8},{10,9},{11,1... | collective-permute-start | bytes 1474568 | tf_op jit(solution)/shard_map/ppermute | solution.py:450
  31.3 1.8 %collective-permute-start = (f32[5,3,32,128]{3,2,1,0:T(8,128)}, f32[5,3,32,128]{3,2,1,0:T(8,128)S(1)}, u32[]{:S(2)}, u32[]{:S(2)}) collective-permute-start(f32[5,3,32,128]{3,2,1,0:T(8,128)} %get-tuple-element.25), channel_id=1, source_target_pairs={{0,8},{8,16},{16,24},{24,0},{1,9},{9,17},{17,25},{25,1},{2,10},{10... | collective-permute-start | bytes 737288 | tf_op jit(solution)/shard_map/ppermute | solution.py:446
  33.0 2.1 %collective-permute-start.1 = (f32[5,3,32,128]{3,2,1,0:T(8,128)}, f32[5,3,32,128]{3,2,1,0:T(8,128)S(1)}, u32[]{:S(2)}, u32[]{:S(2)}) collective-permute-start(f32[5,3,32,128]{3,2,1,0:T(8,128)} %get-tuple-element.26), channel_id=1, source_target_pairs={{8,0},{16,8},{24,16},{0,24},{9,1},{17,9},{25,17},{1,25},{10,2},{18... | collective-permute-start | bytes 737288 | tf_op jit(solution)/shard_map/ppermute | solution.py:447
  35.1 0.0 all-to-all-done
  35.1 0.0 copy-start
  35.1 3.1 %all-to-all-start.1 = ((f32[32,32,128]{2,1,0:T(8,128)}), f32[32,32,128]{2,1,0:T(8,128)S(1)}, u32[]{:S(2)}, u32[]{:S(2)}) async-start(f32[32,32,128]{2,1,0:T(8,128)} %bitcast.10), calls=%async_computation.1 | async-start | bytes 1048576 | tf_op jit(solution)/shard_map/all_to_all | solution.py:431
  38.2 3.9 %collective-permute-done.xlo_ = f32[5,3,32,128]{3,2,1,0:T(8,128)S(1)} collective-permute-done((f32[5,3,32,128]{3,2,1,0:T(8,128)}, f32[5,3,32,128]{3,2,1,0:T(8,128)S(1)}, u32[]{:S(2)}, u32[]{:S(2)}) %collective-permute-start) | collective-permute-done | bytes 245792 | tf_op jit(solution)/shard_map/ppermute | solution.py:446
  42.1 0.0 copy-start.2
  42.1 4.0 %collective-permute-done.1.xhi_ = f32[5,3,32,128]{3,2,1,0:T(8,128)S(1)} collective-permute-done((f32[5,3,32,128]{3,2,1,0:T(8,128)}, f32[5,3,32,128]{3,2,1,0:T(8,128)S(1)}, u32[]{:S(2)}, u32[]{:S(2)}) %collective-permute-start.1) | collective-permute-done | bytes 245792 | tf_op jit(solution)/shard_map/ppermute | solution.py:447
  46.1 0.0 copy-start.3
  46.1 0.1 collective-permute-start.5
  46.2 0.5 collective-permute-start.4
  46.7 2.1 %collective-permute-done.5.chi_ = f32[2,5,3,3,128]{4,3,2,1,0:T(4,128)S(1)} collective-permute-done((f32[2,5,3,3,128]{4,3,2,1,0:T(4,128)S(1)}, f32[2,5,3,3,128]{4,3,2,1,0:T(4,128)S(1)}, u32[]{:S(2)}, u32[]{:S(2)}) %collective-permute-start.5) | collective-permute-done | bytes 46112 | tf_op jit(solution)/shard_map/ppermute | solution.py:453
  48.8 0.0 copy-start.6
  48.8 3.1 %collective-permute-done.4.clo_ = f32[2,5,3,3,128]{4,3,2,1,0:T(4,128)S(1)} collective-permute-done((f32[2,5,3,3,128]{4,3,2,1,0:T(4,128)S(1)}, f32[2,5,3,3,128]{4,3,2,1,0:T(4,128)S(1)}, u32[]{:S(2)}, u32[]{:S(2)}) %collective-permute-start.4) | collective-permute-done | bytes 46112 | tf_op jit(solution)/shard_map/ppermute | solution.py:452
  51.9 0.0 copy-start.7
  51.9 0.0 collective-permute-done.2.ylo_
  51.9 0.0 copy-start.4
  51.9 0.0 collective-permute-done.3.yhi_
  51.9 0.0 copy-start.5
  51.9 0.0 copy-done.2
  51.9 0.0 copy-done.3
  51.9 0.0 copy-done.6
  51.9 0.6 copy-done.7
  52.5 0.2 copy-done.4
  52.7 0.2 copy-done.5
  52.9 12.8 %advect.1 = (f32[64,32,128]{2,1,0:T(8,128)}, f32[64,32,128]{2,1,0:T(8,128)}) custom-call(f32[64,32,128]{2,1,0:T(8,128)} %get-tuple-element.23.tc, f32[64,32,128]{2,1,0:T(8,128)} %get-tuple-element.24.vc, f32[64,32,128]{2,1,0:T(8,128)} %uc.1, f32[64,32,128]{2,1,0:T(8,128)} %vw.1, f32[64,32,128]{2,1,0:T(8,128)} %wc.1, f32[5,3,32,128]{3,2,1,0:T(8,128)} %copy-done.2, ...), custom_call_target="tpu_custom_call" | custom-call | tf_op jit(solution)/shard_map/advect/pallas_call | solution.py:382
  65.7 0.0 copy-done
  65.7 0.2 fusion.2
  65.9 0.2 convert_reduce_fusion
  66.1 0.3 reduce-window.9
  66.4 0.1 slice.19
  66.5 0.1 slice_reduce_fusion
  66.6 0.1 add_bitcast_fusion
  66.7 1.1 %select_reduce_fusion.src = s32[512]{0:T(512)} fusion(s32[1024]{0:T(1024)S(1)} %add_bitcast_fusion, pred[1024]{0:T(1024)(128)(4,1)S(1)} %get-tuple-element.34), kind=kLoop, calls=%fused_computation | loop fusion | flops 2096640 | bytes 7168 | tf_op jit(solution)/shard_map/reduce_sum | solution.py:427
  67.7 0.0 all-to-all-done.1
  67.7 0.0 copy-start.1
  67.7 0.8 %copy-done.1 = f32[32,32,128]{2,1,0:T(8,128)} copy-done((f32[32,32,128]{2,1,0:T(8,128)}, f32[32,32,128]{2,1,0:T(8,128)S(1)}, u32[]{:S(2)}) %copy-start.1) | copy-done | bytes 524312
  68.5 6.1 %receive.1 = (f32[512,128]{1,0:T(8,128)}, f32[512,128]{1,0:T(8,128)}) custom-call(s32[512]{0:T(512)} %select_reduce_fusion.src, f32[1024,128]{1,0:T(8,128)} %bitcast.17, f32[1024,128]{1,0:T(8,128)} %bitcast.20), custom_call_target="tpu_custom_call" | custom-call | tf_op jit(solution)/shard_map/receive/pallas_call | solution.py:413
  (2 shorter events, 0.0 us)
Async XLA Ops:
  4.9 30.2 %all-to-all-start = ((f32[32,32,128]{2,1,0:T(8,128)}), f32[32,32,128]{2,1,0:T(8,128)S(1)}, u32[]{:S(2)}, u32[]{:S(2)}) async-start(f32[32,32,128]{2,1,0:T(8,128)} %bitcast.21), calls=%async_computation | async-start | bytes 1048576 | tf_op jit(solution)/shard_map/all_to_all | solution.py:431
  28.6 23.3 %collective-permute-start.2 = (f32[5,192,128]{2,1,0:T(8,128)}, f32[5,192,128]{2,1,0:T(8,128)S(1)}, u32[]{:S(2)}, u32[]{:S(2)}) collective-permute-start(f32[5,192,128]{2,1,0:T(8,128)} %get-tuple-element.27), channel_id=1, source_target_pairs={{0,1},{1,2},{2,3},{3,4},{4,5},{5,6},{6,7},{7,0},{8,9},{9,10},{10,1... | collective-permute-start | bytes 1474568 | tf_op jit(solution)/shard_map/ppermute | solution.py:449
  28.9 23.0 %collective-permute-start.3 = (f32[5,192,128]{2,1,0:T(8,128)}, f32[5,192,128]{2,1,0:T(8,128)S(1)}, u32[]{:S(2)}, u32[]{:S(2)}) collective-permute-start(f32[5,192,128]{2,1,0:T(8,128)} %get-tuple-element.28), channel_id=1, source_target_pairs={{1,0},{2,1},{3,2},{4,3},{5,4},{6,5},{7,6},{0,7},{9,8},{10,9},{11,1... | collective-permute-start | bytes 1474568 | tf_op jit(solution)/shard_map/ppermute | solution.py:450
  31.3 10.9 %collective-permute-start = (f32[5,3,32,128]{3,2,1,0:T(8,128)}, f32[5,3,32,128]{3,2,1,0:T(8,128)S(1)}, u32[]{:S(2)}, u32[]{:S(2)}) collective-permute-start(f32[5,3,32,128]{3,2,1,0:T(8,128)} %get-tuple-element.25), channel_id=1, source_target_pairs={{0,8},{8,16},{16,24},{24,0},{1,9},{9,17},{17,25},{25,1},{2,10},{10... | collective-permute-start | bytes 737288 | tf_op jit(solution)/shard_map/ppermute | solution.py:446
  33.0 13.1 %collective-permute-start.1 = (f32[5,3,32,128]{3,2,1,0:T(8,128)}, f32[5,3,32,128]{3,2,1,0:T(8,128)S(1)}, u32[]{:S(2)}, u32[]{:S(2)}) collective-permute-start(f32[5,3,32,128]{3,2,1,0:T(8,128)} %get-tuple-element.26), channel_id=1, source_target_pairs={{8,0},{16,8},{24,16},{0,24},{9,1},{17,9},{25,17},{1,25},{10,2},{18... | collective-permute-start | bytes 737288 | tf_op jit(solution)/shard_map/ppermute | solution.py:447
  35.1 30.6 %copy-start = (f32[32,32,128]{2,1,0:T(8,128)}, f32[32,32,128]{2,1,0:T(8,128)S(1)}, u32[]{:S(2)}) copy-start(f32[32,32,128]{2,1,0:T(8,128)S(1)} %all-to-all-done) | copy-start | bytes 1572868
  35.1 32.7 %all-to-all-start.1 = ((f32[32,32,128]{2,1,0:T(8,128)}), f32[32,32,128]{2,1,0:T(8,128)S(1)}, u32[]{:S(2)}, u32[]{:S(2)}) async-start(f32[32,32,128]{2,1,0:T(8,128)} %bitcast.10), calls=%async_computation.1 | async-start | bytes 1048576 | tf_op jit(solution)/shard_map/all_to_all | solution.py:431
  42.1 9.8 %copy-start.2 = (f32[5,3,32,128]{3,2,1,0:T(8,128)}, f32[5,3,32,128]{3,2,1,0:T(8,128)S(1)}, u32[]{:S(2)}) copy-start(f32[5,3,32,128]{3,2,1,0:T(8,128)S(1)} %collective-permute-done.xlo_) | copy-start | bytes 737284
  46.1 5.8 %copy-start.3 = (f32[5,3,32,128]{3,2,1,0:T(8,128)}, f32[5,3,32,128]{3,2,1,0:T(8,128)S(1)}, u32[]{:S(2)}) copy-start(f32[5,3,32,128]{3,2,1,0:T(8,128)S(1)} %collective-permute-done.1.xhi_) | copy-start | bytes 737284
  46.1 2.6 %collective-permute-start.5 = (f32[2,5,3,3,128]{4,3,2,1,0:T(4,128)S(1)}, f32[2,5,3,3,128]{4,3,2,1,0:T(4,128)S(1)}, u32[]{:S(2)}, u32[]{:S(2)}) collective-permute-start(f32[2,5,3,3,128]{4,3,2,1,0:T(4,128)S(1)} %get-tuple-element.36), channel_id=1, source_target_pairs={{1,0},{2,1},{3,2},{4,3},{5,4},{6,5},{7,6},{0,7},{9,8},{10,9},{11,1... | collective-permute-start | bytes 138248 | tf_op jit(solution)/shard_map/ppermute | solution.py:453
  46.2 5.7 %collective-permute-start.4 = (f32[2,5,3,3,128]{4,3,2,1,0:T(4,128)S(1)}, f32[2,5,3,3,128]{4,3,2,1,0:T(4,128)S(1)}, u32[]{:S(2)}, u32[]{:S(2)}) collective-permute-start(f32[2,5,3,3,128]{4,3,2,1,0:T(4,128)S(1)} %get-tuple-element.37), channel_id=1, source_target_pairs={{0,1},{1,2},{2,3},{3,4},{4,5},{5,6},{6,7},{7,0},{8,9},{9,10},{10,1... | collective-permute-start | bytes 138248 | tf_op jit(solution)/shard_map/ppermute | solution.py:452
  48.8 3.2 %copy-start.6 = (f32[2,5,3,3,128]{4,3,2,1,0:T(4,128)}, f32[2,5,3,3,128]{4,3,2,1,0:T(4,128)S(1)}, u32[]{:S(2)}) copy-start(f32[2,5,3,3,128]{4,3,2,1,0:T(4,128)S(1)} %collective-permute-done.5.chi_) | copy-start | bytes 138244
  51.9 0.6 copy-start.7
  51.9 0.8 %copy-start.4 = (f32[5,192,128]{2,1,0:T(8,128)}, f32[5,192,128]{2,1,0:T(8,128)S(1)}, u32[]{:S(2)}) copy-start(f32[5,192,128]{2,1,0:T(8,128)S(1)} %collective-permute-done.2.ylo_) | copy-start | bytes 1474564
  51.9 1.0 %copy-start.5 = (f32[5,192,128]{2,1,0:T(8,128)}, f32[5,192,128]{2,1,0:T(8,128)S(1)}, u32[]{:S(2)}) copy-start(f32[5,192,128]{2,1,0:T(8,128)S(1)} %collective-permute-done.3.yhi_) | copy-start | bytes 1474564
  67.7 0.8 %copy-start.1 = (f32[32,32,128]{2,1,0:T(8,128)}, f32[32,32,128]{2,1,0:T(8,128)S(1)}, u32[]{:S(2)}) copy-start(f32[32,32,128]{2,1,0:T(8,128)S(1)} %all-to-all-done.1) | copy-start | bytes 1572868

commit v3 on v2

--- a/solution.py
+++ b/solution.py
@@ -1,3 +1,5 @@
+import functools
+
 import jax
 import jax.numpy as jnp
 from jax import lax
@@ -26,41 +28,68 @@
         return 0
     lax.fori_loop(0,n//unroll,group,0)
 
-def place_kernel(slot,mult,out,buf):
-    n=mult.shape[0]
-    buf[...]=jnp.zeros_like(buf)
-    def one(b):
-        buf[pl.ds(slot[b],1),:]=mult[pl.ds(b,1),:]
-    row_loop(n,32,one)
-    out[...]=buf[:n,:]
-
-def place(slot,mult):
-    n=mult.shape[0]
-    return pl.pallas_call(place_kernel,out_shape=jax.ShapeDtypeStruct(mult.shape,jnp.float32),
-        in_specs=[SMEM(),VM()],out_specs=VM(),
-        scratch_shapes=[pltpu.VMEM((n+SUB,LAN),jnp.float32)],name="place")(slot,mult)
-
-def home_kernel(slot,column,count,level,radius_,floor_,mult_,tp_,vp_,send,ht,hv,ct,cv,rows_t,rows_v,buf,radius,floor,mult,tp,vp,sem):
-    n=radius.shape[0]
-    pairs_=((tp_,tp),(vp_,vp),(radius_,radius),(floor_,floor),(mult_,mult))
-    loads=[pltpu.make_async_copy(a,b,sem.at[i]) for i,(a,b) in enumerate(pairs_)]
-    for c in loads: c.start()
-    buf[...]=jnp.zeros_like(buf)
-    for c in loads[:2]: c.wait()
+def staged(hbm, local, sem):
+    copies = [pltpu.make_async_copy(x, y, sem.at[i]) for i, (x, y) in enumerate(zip(hbm, local))]
+    for c in copies: c.start()
+    return copies
+
+def spare(n):
+    rows = 1 << (n - 1).bit_length()
+    return 2 * rows
+
+def merge_kernel(cap,move_,r2_,mult_,send,move,r2s,mult,rows_r,rows_m,buf,sem):
+    n=mult.shape[0]; wrap=spare(n)-1
+    copies=staged((move_,r2_,mult_),(move,r2s,mult),sem)
+    buf[:n,:]=jnp.zeros_like(mult); buf[n:2*n,:]=jnp.zeros_like(mult)
+    for c in copies: c.wait()
+    def tile(t,_):
+        sl=pl.ds(pl.multiple_of(t*LAN,LAN),LAN)
+        r2=jnp.transpose(r2s[sl,:])
+        a,b,rank=collect_tile(r2,jnp.where(r2>0.0,jnp.transpose(mult[sl,:]),0.0))
+        rank=jnp.transpose(rank).astype(jnp.int32)
+        rows_r[sl,:]=jnp.take_along_axis(jnp.transpose(a),rank,axis=1)
+        rows_m[sl,:]=jnp.take_along_axis(jnp.transpose(b),rank,axis=1)
+        return 0
+    lax.fori_loop(0,n//LAN,tile,0)
+    def put(b):
+        s=move[b]&wrap
+        if cap&(cap-1):
+            lead=lax.div(s,cap)
+        else:
+            lead=lax.shift_right_logical(s,cap.bit_length()-1)
+        at=s+lead*cap
+        buf[pl.ds(at,1),:]=rows_r[pl.ds(b,1),:]
+        buf[pl.ds(at+cap,1),:]=rows_m[pl.ds(b,1),:]
+    row_loop(n,32,put)
+    last=pltpu.make_async_copy(buf.at[pl.ds(0,2*n)],send,sem.at[0])
+    last.start(); last.wait()
+
+def merge(cap,move,r2,mult):
+    n=mult.shape[0]; F=lambda *d: pltpu.VMEM(d,jnp.float32)
+    return pl.pallas_call(functools.partial(merge_kernel,cap),out_shape=jax.ShapeDtypeStruct((2*n,LAN),jnp.float32),
+        in_specs=[ANY()]*3,out_specs=ANY(),
+        scratch_shapes=[pltpu.SMEM((n,),jnp.int32)]+[F(n,LAN)]*4+[F(2*spare(n),LAN),pltpu.SemaphoreType.DMA((3,))],
+        name="merge")(move,r2,mult)
+
+def home_kernel(cell_,cells_,counts_,tp_,vp_,radius_,floor_,mult_,send,heat_,cell,cells,counts,tp,vp,radius,floor,mult,rows_t,rows_v,heat,sem):
+    n=radius.shape[0]; g=n//LAN
+    depth_bits=LAN.bit_length()-1
+    copies=staged((cell_,tp_,vp_,cells_,counts_,radius_,floor_,mult_),(cell,tp,vp,cells,counts,radius,floor,mult),sem)
+    for c in copies[:3]: c.wait()
     def fetch(b):
-        c=column[b]
+        c=lax.shift_right_logical(cell[b],depth_bits)
         rows_t[pl.ds(b,1),:]=tp[pl.ds(c,1),:]
         rows_v[pl.ds(b,1),:]=vp[pl.ds(c,1),:]
     row_loop(n,32,fetch)
-    for c in loads[2:]: c.wait()
+    for c in copies[3:]: c.wait()
     depth=lax.broadcasted_iota(jnp.int32,(LAN,LAN),0)
     def tile(t,_):
         sl=pl.ds(pl.multiple_of(t*LAN,LAN),LAN)
-        here=depth==level[pl.ds(t,1),:]
+        here=depth==(cells[pl.ds(t,1),:]&(LAN-1))
         temp0=jnp.sum(jnp.where(here,jnp.transpose(rows_t[sl,:]),0.0),axis=0,keepdims=True)
         wet0=jnp.sum(jnp.where(here,jnp.transpose(rows_v[sl,:]),0.0),axis=0,keepdims=True)
         r=jnp.transpose(radius[sl,:]); fl=jnp.transpose(floor[sl,:])
-        alive=depth<count[pl.ds(t,1),:]
+        alive=depth<counts[pl.ds(t,1),:]
         m=jnp.where(alive,jnp.transpose(mult[sl,:]),0.0)
         r2=r*r; f2=fl*fl; g3=(growth*solute)*(f2*fl)
         inv=lax.rsqrt(r2); mass=r2*(r2*inv)
@@ -74,29 +103,28 @@
             wet=wet-condense*condensed
             temp=temp+latent*condense*condensed
             r2=grown; mass=new
-        ht[pl.ds(t,1),:]=temp-temp0; hv[pl.ds(t,1),:]=wet-wet0
-        ct[pl.ds(t,1),:]=temp0; cv[pl.ds(t,1),:]=wet0
+        heat[pl.ds(t,1),:]=temp-temp0; heat[pl.ds(g+t,1),:]=wet-wet0
+        heat[pl.ds(2*g+t,1),:]=temp0; heat[pl.ds(3*g+t,1),:]=wet0
         rows_t[sl,:]=jnp.transpose(jnp.where(alive,r2,0.0))
         return 0
-    lax.fori_loop(0,n//LAN,tile,0)
-    def put(b):
-        buf[pl.ds(slot[b],1),:]=rows_t[pl.ds(b,1),:]
-    row_loop(n,32,put)
-    send[...]=buf[:n,:]
-
-def home(slot,column,level,count,radius,floor,mult,tp,vp):
+    lax.fori_loop(0,g,tile,0)
+    first=pltpu.make_async_copy(heat,heat_,sem.at[1])
+    first.start()
+    last=pltpu.make_async_copy(rows_t,send,sem.at[0])
+    last.start(); last.wait(); first.wait()
+
+def home(cell,count,radius,floor,mult,tp,vp):
     n=radius.shape[0]; g=n//LAN
-    levels=tp.shape[-1]
-    tab=jax.ShapeDtypeStruct((g,LAN),jnp.float32)
+    cols=(tp.size//LAN,LAN); F=lambda *d: pltpu.VMEM(d,jnp.float32)
     return pl.pallas_call(home_kernel,
-        out_shape=(jax.ShapeDtypeStruct(radius.shape,jnp.float32),tab,tab,tab,tab),
-        in_specs=[SMEM(),SMEM(),VM(),VM()]+[ANY()]*5,out_specs=(VM(),)*5,
-        scratch_shapes=[pltpu.VMEM((n,LAN),jnp.float32)]*2+[pltpu.VMEM((n+SUB,LAN),jnp.float32)]+[pltpu.VMEM((n,LAN),jnp.float32)]*3+[pltpu.VMEM((tp.size//levels,levels),jnp.float32)]*2+[pltpu.SemaphoreType.DMA((5,))],
-        name="home")(slot,column,count.reshape(g,LAN),level.reshape(g,LAN),radius,floor,mult,
-                     tp.reshape(-1,levels),vp.reshape(-1,levels))
-
-def scatter_kernel(column,level,cellv,ht,hv,ct,cv,tp,vp,wu,wv,ww,ot,ov,xfirst,xlast,yfirst,ylast,vt,vv,acct,accv,wlo,whi,sem):
-    g=cellv.shape[0]; n=g*LAN
+        out_shape=(jax.ShapeDtypeStruct(radius.shape,jnp.float32),jax.ShapeDtypeStruct((4*g,LAN),jnp.float32)),
+        in_specs=[ANY()]*8,out_specs=(ANY(),)*2,
+        scratch_shapes=[pltpu.SMEM((n,),jnp.int32)]+[pltpu.VMEM((g,LAN),jnp.int32)]*2+[F(*cols)]*2+[F(n,LAN)]*5
+            +[F(4*g,LAN),pltpu.SemaphoreType.DMA((9,))],
+        name="home")(cell,cell.reshape(g,LAN),count.reshape(g,LAN),tp.reshape(cols),vp.reshape(cols),radius,floor,mult)
+
+def scatter_kernel(column,level,cells,heat,tp,vp,wu,wv,ww,ot,ov,xfirst,xlast,yfirst,ylast,vt,vv,acct,accv,spot,wlo,whi,sem):
+    g=cells.shape[0]; n=g*LAN
     nx,ny=tp.shape[:2]
     winds=(wu,wv,ww)
     loads=[pltpu.make_async_copy(tp,ot,sem.at[0]),pltpu.make_async_copy(vp,ov,sem.at[1])]
@@ -107,11 +135,12 @@
                 pltpu.make_async_copy(w.at[pl.ds(nx-W,W)],xlast.at[2+i],sem.at[11+i])]
     for c in loads: c.start()
     spread=lambda ref,t: jnp.transpose(jnp.broadcast_to(ref[pl.ds(t,1),:],(LAN,LAN)))
+    spot[...]=cells[...].astype(jnp.float32)
     acct[...]=jnp.zeros_like(acct); accv[...]=jnp.zeros_like(accv)
     def source(t,_):
-        c=spread(cellv,t); a=spread(ht,t); b=spread(hv,t)
+        c=spread(spot,t); a=spread(heat,t); b=spread(heat,g+t)
         for o in range(g):
-            mine=cellv[o:o+1,:]
+            mine=spot[o:o+1,:]
             st=jnp.zeros((SUB,LAN),jnp.float32); sv=st
             for k in range(LAN//SUB):
                 same=c[k*SUB:(k+1)*SUB,:]==mine
@@ -124,8 +153,8 @@
     def rows(t,_):
         sl=pl.ds(pl.multiple_of(t*LAN,LAN),LAN)
         s8=pl.ds(pl.multiple_of(t*SUB,SUB),SUB)
-        nt=ct[pl.ds(t,1),:]+jnp.sum(acct[s8,:],axis=0,keepdims=True)
-        nv=cv[pl.ds(t,1),:]+jnp.sum(accv[s8,:],axis=0,keepdims=True)
+        nt=heat[pl.ds(2*g+t,1),:]+jnp.sum(acct[s8,:],axis=0,keepdims=True)
+        nv=heat[pl.ds(3*g+t,1),:]+jnp.sum(accv[s8,:],axis=0,keepdims=True)
         vt[sl,:]=jnp.transpose(jnp.broadcast_to(nt,(LAN,LAN)))
         vv[sl,:]=jnp.transpose(jnp.broadcast_to(nv,(LAN,LAN)))
         return 0
@@ -149,15 +178,15 @@
         return 0
     lax.fori_loop(0,nx,side,0,unroll=4)
 
-def scatter(column,level,cell,ht,hv,ct,cv,tp,vp,*winds):
-    g=ht.shape[0]; n=g*LAN
+def scatter(column,level,cell,heat,tp,vp,*winds):
+    n=cell.shape[0]; g=n//LAN
     nx,ny,nz=tp.shape
     S=lambda *d: jax.ShapeDtypeStruct(d,jnp.float32)
     return pl.pallas_call(scatter_kernel,out_shape=(S(nx,ny,nz),)*2+(S(5,W,ny,nz),)*2+(S(5,nx*W,nz),)*2,
-        in_specs=[SMEM()]*2+[VM()]*5+[ANY()]*5,out_specs=(VM(),)*6,
-        scratch_shapes=[pltpu.VMEM((n,LAN),jnp.float32)]*2+[pltpu.VMEM((g*SUB,LAN),jnp.float32)]*2
+        in_specs=[SMEM()]*2+[VM()]*2+[ANY()]*5,out_specs=(VM(),)*6,
+        scratch_shapes=[pltpu.VMEM((n,LAN),jnp.float32)]*2+[pltpu.VMEM((g*SUB,LAN),jnp.float32)]*2+[pltpu.VMEM((g,LAN),jnp.float32)]
             +[pltpu.VMEM((3,nx,SUB,nz),jnp.float32)]*2+[pltpu.SemaphoreType.DMA((14,))],
-        name="scatter")(column,level,cell.reshape(g,LAN).astype(jnp.float32),ht,hv,ct,cv,tp,vp,*winds)
+        name="scatter")(column,level,cell.reshape(g,LAN),heat,tp,vp,*winds)
 
 
 def batcher(n):
@@ -386,45 +415,32 @@
         name="advect")(t,v,u,w2,w3,*edges)
 
 
-def receive_kernel(src, mults, r2s, ro_ref, mo_ref, mrow, rrow):
-    blocks = ro_ref.shape[0]
-
+def receive_kernel(cap, src, rows, ro_ref, mo_ref):
     def pull(b):
         s = src[b]
-        mrow[pl.ds(b, 1), :] = mults[pl.ds(s, 1), :]
-        rrow[pl.ds(b, 1), :] = r2s[pl.ds(s, 1), :]
-
-    row_loop(blocks, 32, pull)
-
-    def tile(t, _):
-        sl = pl.ds(pl.multiple_of(t * LAN, LAN), LAN)
-        r2 = jnp.transpose(rrow[sl, :])
-        a, b, rank = collect_tile(r2, jnp.where(r2 > 0.0, jnp.transpose(mrow[sl, :]), 0.0))
-        rank = jnp.transpose(rank).astype(jnp.int32)
-        ro_ref[sl, :] = jnp.take_along_axis(jnp.transpose(a), rank, axis=1)
-        mo_ref[sl, :] = jnp.take_along_axis(jnp.transpose(b), rank, axis=1)
-        return 0
-
-    lax.fori_loop(0, blocks // LAN, tile, 0)
-
-
-def receive(src, mults, r2s):
+        ro_ref[pl.ds(b, 1), :] = rows[pl.ds(s, 1), :]
+        mo_ref[pl.ds(b, 1), :] = rows[pl.ds(s + cap, 1), :]
+
+    row_loop(ro_ref.shape[0], 32, pull)
+
+
+def receive(cap, src, rows):
     out = jax.ShapeDtypeStruct((BLK_DEV, LAN), jnp.float32)
     return pl.pallas_call(
-        receive_kernel,
+        functools.partial(receive_kernel, cap),
         out_shape=(out, out),
-        in_specs=[SMEM(), VM(), VM()],
+        in_specs=[SMEM(), VM()],
         out_specs=(VM(), VM()),
-        scratch_shapes=[pltpu.VMEM((BLK_DEV, LAN), jnp.float32)] * 2,
         name="receive",
-    )(src, mults, r2s)
-
-
-def sources(mults):
-    taken = mults[:, 0] > 0.0
+    )(src, rows)
+
+
+def sources(rows, devices, cap):
+    taken = rows.reshape(devices, 2, cap, LAN)[:, 0, :, 0].reshape(-1) > 0.0
     position = jnp.cumsum(taken.astype(jnp.int32)) - 1
     hit = (position[None, :] == jnp.arange(BLK_DEV, dtype=jnp.int32)[:, None]) & taken[None, :]
-    return jnp.sum(jnp.where(hit, jnp.arange(mults.shape[0], dtype=jnp.int32)[None, :], 0), axis=1)
+    slots = jnp.arange(devices * cap, dtype=jnp.int32)
+    return jnp.sum(jnp.where(hit, (slots + slots // cap * cap)[None, :], 0), axis=1)
 
 
 def exchange(rows, devices):
@@ -440,18 +456,21 @@
     return up, [(j, i) for i, j in up]
 
 
-def halos(xfirst, xlast, yfirst, ylast):
-    ny = xfirst.shape[2]
+def edge_halos(xfirst, xlast, yfirst, ylast):
     up, down = shifts("gx")
     xlo = lax.ppermute(xlast, "gx", up)
     xhi = lax.ppermute(xfirst, "gx", down)
     up, down = shifts("gy")
-    ylo = lax.ppermute(ylast, "gy", up)
-    yhi = lax.ppermute(yfirst, "gy", down)
+    return xlo, xhi, lax.ppermute(ylast, "gy", up), lax.ppermute(yfirst, "gy", down)
+
+
+def corner_halos(xlo, xhi):
+    ny = xlo.shape[2]
+    up, down = shifts("gy")
     ends = jnp.stack([xlo, xhi])
     clo = lax.ppermute(ends[:, :, :, ny - W :], "gy", up)
     chi = lax.ppermute(ends[:, :, :, :W], "gy", down)
-    return xlo, xhi, ylo, yhi, clo, chi
+    return clo, chi
 
 
 def body(
@@ -469,20 +488,26 @@
 ):
     devices = lax.axis_size("gx") * lax.axis_size("gy")
     levels = tprime.shape[2]
-    slot = jnp.where(move_list >= 0, move_list, multiplicity.shape[0])
     column = lax.shift_right_logical(cell_index, levels.bit_length() - 1)
     level = cell_index & (levels - 1)
-    mults = exchange(place(slot, multiplicity), devices)
-    sent, ht, hv, ct, cv = home(
-        slot, column, level, drop_counts, radius, min_radius, multiplicity, tprime, vapor
+    winds = (wind_u, wind_v, wind_w)
+    cap = (radius.shape[0] + devices - 1) // devices
+    r2, heat = home(
+        cell_index, drop_counts, radius, min_radius, multiplicity, tprime, vapor
     )
-    r2s = exchange(sent, devices)
-    winds = (wind_u, wind_v, wind_w)
-    heated_t, heated_v, *edges = scatter(
-        column, level, cell_index, ht, hv, ct, cv, tprime, vapor, *winds
+    heated_t, heated_v, *edges = scatter(column, level, cell_index, heat, tprime, vapor, *winds)
+    edges, r2 = lax.optimization_barrier((edges, r2))
+    xlo, xhi, ylo, yhi = edge_halos(*edges)
+    xlo, xhi, ylo, yhi, sent = lax.optimization_barrier(
+        (xlo, xhi, ylo, yhi, merge(cap, move_list, r2, multiplicity))
     )
-    temperature_out, vapor_out = advect(heated_t, heated_v, *winds, *halos(*edges))
-    radius_out, multiplicity_out = receive(sources(mults), mults, r2s)
+    moved = exchange(sent, devices)
+    clo, chi = corner_halos(xlo, xhi)
+    temperature_out, vapor_out = advect(
+        heated_t, heated_v, *winds, xlo, xhi, ylo, yhi, clo, chi
+    )
+    moved, temperature_out = lax.optimization_barrier((moved, temperature_out))
+    radius_out, multiplicity_out = receive(cap, sources(moved, devices, cap), moved)
     return (temperature_out, vapor_out, radius_out, multiplicity_out)
 
 

time: 75.2 us -> 71.7 us (0.953)
  starting transfers between devices: 17.5 us -> 13.8 us
  Pallas kernels: 38.1 us -> 41.6 us
  waiting for transfers between devices: 13.1 us -> 10 us
    all_to_all x2 -> x1, starting transfers between devices: 10.5 us -> 3.37 us  [exchange(): lax.all_to_all(rows.reshape((devices, -1) + rows.shape[1:]), ('gx', 'gy')...]
    ppermute x6, waiting for transfers between devices: 13.1 us -> 8.12 us  [the longest x1 8.11 us: corner_halos(): clo = lax.ppermute(ends[:, :, :, ny - W:], 'gy', up)]
    pallas_call x2, Pallas kernels: 8.98 us -> 13.8 us  [the longest x1 11.2 us: merge(): pl.pallas_call(functools.partial(merge_kernel, cap), out_shape=jax.ShapeD...]
    ppermute x6, starting transfers between devices: 7.08 us -> 10.5 us  [the longest x1 2.93 us: edge_halos(): lax.ppermute(yfirst, 'gy', down)]
    all_to_all x2 -> x1, waiting for transfers between devices: 0.01 us -> 1.9 us  [exchange(): lax.all_to_all(rows.reshape((devices, -1) + rows.shape[1:]), ('gx', 'gy')...]
    pallas_call x1, Pallas kernels: 9.38 us -> 7.93 us  [home(): pl.pallas_call(home_kernel, out_shape=(jax.ShapeDtypeStruct(radius.shape,...]
    reshape x1 -> x0, other arithmetic: 1.38 us -> none  [home(): level.reshape(g, LAN)]
    and x0 -> x1, other arithmetic: none -> 1.28 us  [body(): level = cell_index & levels - 1]
  transfers between devices with their start and end apart: 8 -> 7, of which waited for: 4 -> 2; matrix products, arithmetic and copies ran while one was open for 3% -> 0% of each run, Pallas kernels for 39% -> 34%
where the time goes in v3:
time: 71.7 us; the launch traced here: 71.3 us
  Pallas kernels  41.6 us (58%)
  starting transfers between devices  13.8 us (19%)
  waiting for transfers between devices  10 us (14%)
  other arithmetic  2.8 us (4%)
  local copies, waits for them, and re-layouts  2.28 us (3%)
  between operations  0.78 us (1%)
    pallas_call x1, Pallas kernels, advect(): pl.pallas_call(advect_kernel, out_shape=(o, o), in_specs=[ANY] * 11, out_...  12.8 us
    pallas_call x1, Pallas kernels, merge(): pl.pallas_call(functools.partial(merge_kernel, cap), out_shape=jax.ShapeD...  11.2 us
    ppermute x1, waiting for transfers between devices, corner_halos(): clo = lax.ppermute(ends[:, :, :, ny - W:], 'gy', up)  8.11 us
    pallas_call x1, Pallas kernels, home(): pl.pallas_call(home_kernel, out_shape=(jax.ShapeDtypeStruct(radius.shape,...  7.93 us
    pallas_call x1, Pallas kernels, scatter(): pl.pallas_call(scatter_kernel, out_shape=(S(nx, ny, nz),) * 2 + (S(5, W,...  7.04 us
    all_to_all x1, starting transfers between devices, exchange(): lax.all_to_all(rows.reshape((devices, -1) + rows.shape[1:]), ('gx', 'gy')...  3.37 us
    ppermute x1, starting transfers between devices, edge_halos(): lax.ppermute(yfirst, 'gy', down)  2.93 us
    pallas_call x1, Pallas kernels, receive(): pl.pallas_call(functools.partial(receive_kernel, cap), out_shape=(out, ou...  2.64 us
  transfers between devices with their start and end apart: 7, of which 2 were waited for; matrix products, arithmetic and copies ran while one was open for 0% of the time, Pallas kernels for 34%

profile of v3, /device:TPU:0, one launch (start us, length us, event | category | flops | bytes accessed | tf_op | source)
XLA Modules:
  0.0 71.3 jit_solution(15574540784906379854)
XLA Ops:
  0.6 1.3 %broadcast_and_fusion = (s32[1024]{0:T(1024)}, s32[1024]{0:T(1024)}) fusion(s32[1024]{0:T(1024)} %cell_.1), kind=kLoop, calls=%fused_computation.17 | loop fusion | flops 2048 | bytes 12288 | tf_op jit(solution)/shard_map/and | solution.py:492
  1.9 7.9 %home.1 = (f32[1024,128]{1,0:T(8,128)}, f32[32,128]{1,0:T(8,128)}) custom-call(s32[1024]{0:T(1024)} %cell_.1, s32[8,128]{1,0:T(8,128)} %bitcast.26, s32[8,128]{1,0:T(8,128)} %bitcast.28, f32[2048,128]{1,0:T(8,128)} %bitcast.22, f32[2048,128]{1,0:T(8,128)} %bitcast.23, f32[1024,128]{1,0:T(8,128)} %radius_.1, f32[1024,128]{1,0:T(8,128)} %floor_.1, ...), custom_call_target="tpu_custom_call" | custom-call | tf_op jit(solution)/shard_map/home/pallas_call | solution.py:119
  9.8 7.0 %scatter.1 = (f32[64,32,128]{2,1,0:T(8,128)}, f32[64,32,128]{2,1,0:T(8,128)}, f32[5,3,32,128]{3,2,1,0:T(8,128)}, f32[5,3,32,128]{3,2,1,0:T(8,128)}, f32[5,192,128]{2,1,0:T(8,128)}, /*index=5*/f32[5,192,128]{2,1,0:T(8,128)}) custom-call(s32[1024]{0:T(1024)} %get-tuple-element.57.column, s32[1024]{0:T(1024)} %get-tuple-element.56.level, s32[8,128]{1,0:T(8,128)} %bitcast.27, ...), custom_call_target="tpu_custom_call" | custom-call | tf_op jit(solution)/shard_map/scatter/pallas_call | solution.py:185
  16.9 0.5 collective-permute-start.2
  17.4 2.9 %collective-permute-start.3 = (f32[5,192,128]{2,1,0:T(8,128)}, f32[5,192,128]{2,1,0:T(8,128)S(1)}, u32[]{:S(2)}, u32[]{:S(2)}) collective-permute-start(f32[5,192,128]{2,1,0:T(8,128)} %get-tuple-element.37), channel_id=1, source_target_pairs={{1,0},{2,1},{3,2},{4,3},{5,4},{6,5},{7,6},{0,7},{9,8},{10,9},{11,1... | collective-permute-start | bytes 1474568 | tf_op jit(solution)/shard_map/ppermute | solution.py:464
  20.4 2.3 %collective-permute-start = (f32[5,3,32,128]{3,2,1,0:T(8,128)}, f32[5,3,32,128]{3,2,1,0:T(8,128)S(1)}, u32[]{:S(2)}, u32[]{:S(2)}) collective-permute-start(f32[5,3,32,128]{3,2,1,0:T(8,128)} %get-tuple-element.34), channel_id=1, source_target_pairs={{0,8},{8,16},{16,24},{24,0},{1,9},{9,17},{17,25},{25,1},{2,10},{10... | collective-permute-start | bytes 737288 | tf_op jit(solution)/shard_map/ppermute | solution.py:461
  22.6 2.0 %collective-permute-start.1 = (f32[5,3,32,128]{3,2,1,0:T(8,128)}, f32[5,3,32,128]{3,2,1,0:T(8,128)S(1)}, u32[]{:S(2)}, u32[]{:S(2)}) collective-permute-start(f32[5,3,32,128]{3,2,1,0:T(8,128)} %get-tuple-element.35), channel_id=1, source_target_pairs={{8,0},{16,8},{24,16},{0,24},{9,1},{17,9},{25,17},{1,25},{10,2},{18... | collective-permute-start | bytes 737288 | tf_op jit(solution)/shard_map/ppermute | solution.py:462
  24.7 11.2 %merge.1 = f32[2048,128]{1,0:T(8,128)} custom-call(s32[1024]{0:T(1024)} %move_.1, f32[1024,128]{1,0:T(8,128)} %get-tuple-element.38.r2_, f32[1024,128]{1,0:T(8,128)} %mult_.3), custom_call_target="tpu_custom_call" | custom-call | tf_op jit(solution)/shard_map/merge/pallas_call | solution.py:69
  35.9 0.0 collective-permute-done.xlo_
  35.9 0.0 copy-start.1
  35.9 0.0 collective-permute-done.1.xhi_
  35.9 0.0 copy-start.2
  35.9 0.0 collective-permute-done.2.ylo_
  35.9 0.0 copy-start.3
  35.9 0.0 collective-permute-done.3.yhi_
  35.9 0.0 copy-start.4
  35.9 0.8 %copy-done.3 = f32[5,192,128]{2,1,0:T(8,128)} copy-done((f32[5,192,128]{2,1,0:T(8,128)}, f32[5,192,128]{2,1,0:T(8,128)S(1)}, u32[]{:S(2)}) %copy-start.3) | copy-done | bytes 491544
  36.7 0.2 copy-done.4
  36.9 3.4 %all-to-all-start = ((f32[32,64,128]{2,1,0:T(8,128)}), f32[32,64,128]{2,1,0:T(8,128)S(1)}, u32[]{:S(2)}, u32[]{:S(2)}) async-start(f32[32,64,128]{2,1,0:T(8,128)} %bitcast.21), calls=%async_computation | async-start | bytes 2097152 | tf_op jit(solution)/shard_map/all_to_all | solution.py:447
  40.3 0.0 copy-done.1
  40.3 0.0 copy-done.2
  40.4 0.3 collective-permute-start.4
  40.7 2.4 %collective-permute-start.5 = (f32[2,5,3,3,128]{4,3,2,1,0:T(4,128)S(1)}, f32[2,5,3,3,128]{4,3,2,1,0:T(4,128)S(1)}, u32[]{:S(2)}, u32[]{:S(2)}) collective-permute-start(f32[2,5,3,3,128]{4,3,2,1,0:T(4,128)S(1)} %get-tuple-element.54), channel_id=1, source_target_pairs={{1,0},{2,1},{3,2},{4,3},{5,4},{6,5},{7,6},{0,7},{9,8},{10,9},{11,1... | collective-permute-start | bytes 138248 | tf_op jit(solution)/shard_map/ppermute | solution.py:472
  43.1 8.1 %collective-permute-done.4.clo_ = f32[2,5,3,3,128]{4,3,2,1,0:T(4,128)S(1)} collective-permute-done((f32[2,5,3,3,128]{4,3,2,1,0:T(4,128)S(1)}, f32[2,5,3,3,128]{4,3,2,1,0:T(4,128)S(1)}, u32[]{:S(2)}, u32[]{:S(2)}) %collective-permute-start.4) | collective-permute-done | bytes 46112 | tf_op jit(solution)/shard_map/ppermute | solution.py:471
  51.2 0.0 copy-start.5
  51.2 0.0 collective-permute-done.5.chi_
  51.2 0.0 copy-start.6
  51.2 0.6 copy-done.5
  51.8 0.0 copy-done.6
  51.8 12.8 %advect.1 = (f32[64,32,128]{2,1,0:T(8,128)}, f32[64,32,128]{2,1,0:T(8,128)}) custom-call(f32[64,32,128]{2,1,0:T(8,128)} %get-tuple-element.40.tc, f32[64,32,128]{2,1,0:T(8,128)} %get-tuple-element.41.vc, f32[64,32,128]{2,1,0:T(8,128)} %uc.1, f32[64,32,128]{2,1,0:T(8,128)} %vw.1, f32[64,32,128]{2,1,0:T(8,128)} %wc.1, f32[5,3,32,128]{3,2,1,0:T(8,128)} %copy-done.1, ...), custom_call_target="tpu_custom_call" | custom-call | tf_op jit(solution)/shard_map/advect/pallas_call | solution.py:411
  64.6 1.9 %all-to-all-done = f32[32,64,128]{2,1,0:T(8,128)S(1)} async-done(((f32[32,64,128]{2,1,0:T(8,128)}), f32[32,64,128]{2,1,0:T(8,128)S(1)}, u32[]{:S(2)}, u32[]{:S(2)}) %all-to-all-start) | async-done | bytes 1048608 | tf_op jit(solution)/shard_map/all_to_all | solution.py:447
  66.5 0.0 copy-start
  66.6 0.2 copy.17
  66.8 0.1 reshape.91
  66.9 0.3 reduce-window.9
  67.2 0.1 slice.19
  67.3 0.1 slice_reduce_fusion
  67.4 0.1 add_bitcast_fusion
  67.5 0.1 gt.17
  67.6 1.1 %select_reduce_fusion.src = s32[512]{0:T(512)} fusion(s32[1024]{0:T(1024)S(1)} %iota_add_fusion, s32[1024]{0:T(1024)S(1)} %add_bitcast_fusion, pred[1024]{0:T(1024)(128)(4,1)S(1)} %gt.17), kind=kLoop, calls=%fused_computation | loop fusion | flops 2096640 | bytes 11264 | tf_op jit(solution)/shard_map/reduce_sum | solution.py:443
  68.7 0.0 copy-done
  68.7 2.6 %receive.1 = (f32[512,128]{1,0:T(8,128)}, f32[512,128]{1,0:T(8,128)}) custom-call(s32[512]{0:T(512)} %select_reduce_fusion.src, f32[2048,128]{1,0:T(8,128)} %bitcast.20), custom_call_target="tpu_custom_call" | custom-call | tf_op jit(solution)/shard_map/receive/pallas_call | solution.py:429
  (5 shorter events, 0.1 us)
Async XLA Ops:
  16.9 19.0 %collective-permute-start.2 = (f32[5,192,128]{2,1,0:T(8,128)}, f32[5,192,128]{2,1,0:T(8,128)S(1)}, u32[]{:S(2)}, u32[]{:S(2)}) collective-permute-start(f32[5,192,128]{2,1,0:T(8,128)} %get-tuple-element.36), channel_id=1, source_target_pairs={{0,1},{1,2},{2,3},{3,4},{4,5},{5,6},{6,7},{7,0},{8,9},{9,10},{10,1... | collective-permute-start | bytes 1474568 | tf_op jit(solution)/shard_map/ppermute | solution.py:464
  17.4 18.5 %collective-permute-start.3 = (f32[5,192,128]{2,1,0:T(8,128)}, f32[5,192,128]{2,1,0:T(8,128)S(1)}, u32[]{:S(2)}, u32[]{:S(2)}) collective-permute-start(f32[5,192,128]{2,1,0:T(8,128)} %get-tuple-element.37), channel_id=1, source_target_pairs={{1,0},{2,1},{3,2},{4,3},{5,4},{6,5},{7,6},{0,7},{9,8},{10,9},{11,1... | collective-permute-start | bytes 1474568 | tf_op jit(solution)/shard_map/ppermute | solution.py:464
  20.4 15.5 %collective-permute-start = (f32[5,3,32,128]{3,2,1,0:T(8,128)}, f32[5,3,32,128]{3,2,1,0:T(8,128)S(1)}, u32[]{:S(2)}, u32[]{:S(2)}) collective-permute-start(f32[5,3,32,128]{3,2,1,0:T(8,128)} %get-tuple-element.34), channel_id=1, source_target_pairs={{0,8},{8,16},{16,24},{24,0},{1,9},{9,17},{17,25},{25,1},{2,10},{10... | collective-permute-start | bytes 737288 | tf_op jit(solution)/shard_map/ppermute | solution.py:461
  22.6 13.2 %collective-permute-start.1 = (f32[5,3,32,128]{3,2,1,0:T(8,128)}, f32[5,3,32,128]{3,2,1,0:T(8,128)S(1)}, u32[]{:S(2)}, u32[]{:S(2)}) collective-permute-start(f32[5,3,32,128]{3,2,1,0:T(8,128)} %get-tuple-element.35), channel_id=1, source_target_pairs={{8,0},{16,8},{24,16},{0,24},{9,1},{17,9},{25,17},{1,25},{10,2},{18... | collective-permute-start | bytes 737288 | tf_op jit(solution)/shard_map/ppermute | solution.py:462
  35.9 4.4 %copy-start.1 = (f32[5,3,32,128]{3,2,1,0:T(8,128)}, f32[5,3,32,128]{3,2,1,0:T(8,128)S(1)}, u32[]{:S(2)}) copy-start(f32[5,3,32,128]{3,2,1,0:T(8,128)S(1)} %collective-permute-done.xlo_) | copy-start | bytes 737284
  35.9 4.4 %copy-start.2 = (f32[5,3,32,128]{3,2,1,0:T(8,128)}, f32[5,3,32,128]{3,2,1,0:T(8,128)S(1)}, u32[]{:S(2)}) copy-start(f32[5,3,32,128]{3,2,1,0:T(8,128)S(1)} %collective-permute-done.1.xhi_) | copy-start | bytes 737284
  35.9 0.8 %copy-start.3 = (f32[5,192,128]{2,1,0:T(8,128)}, f32[5,192,128]{2,1,0:T(8,128)S(1)}, u32[]{:S(2)}) copy-start(f32[5,192,128]{2,1,0:T(8,128)S(1)} %collective-permute-done.2.ylo_) | copy-start | bytes 1474564
  35.9 1.0 %copy-start.4 = (f32[5,192,128]{2,1,0:T(8,128)}, f32[5,192,128]{2,1,0:T(8,128)S(1)}, u32[]{:S(2)}) copy-start(f32[5,192,128]{2,1,0:T(8,128)S(1)} %collective-permute-done.3.yhi_) | copy-start | bytes 1474564
  36.9 29.6 %all-to-all-start = ((f32[32,64,128]{2,1,0:T(8,128)}), f32[32,64,128]{2,1,0:T(8,128)S(1)}, u32[]{:S(2)}, u32[]{:S(2)}) async-start(f32[32,64,128]{2,1,0:T(8,128)} %bitcast.21), calls=%async_computation | async-start | bytes 2097152 | tf_op jit(solution)/shard_map/all_to_all | solution.py:447
  40.4 10.8 %collective-permute-start.4 = (f32[2,5,3,3,128]{4,3,2,1,0:T(4,128)S(1)}, f32[2,5,3,3,128]{4,3,2,1,0:T(4,128)S(1)}, u32[]{:S(2)}, u32[]{:S(2)}) collective-permute-start(f32[2,5,3,3,128]{4,3,2,1,0:T(4,128)S(1)} %get-tuple-element.55), channel_id=1, source_target_pairs={{0,1},{1,2},{2,3},{3,4},{4,5},{5,6},{6,7},{7,0},{8,9},{9,10},{10,1... | collective-permute-start | bytes 138248 | tf_op jit(solution)/shard_map/ppermute | solution.py:471
  40.7 10.5 %collective-permute-start.5 = (f32[2,5,3,3,128]{4,3,2,1,0:T(4,128)S(1)}, f32[2,5,3,3,128]{4,3,2,1,0:T(4,128)S(1)}, u32[]{:S(2)}, u32[]{:S(2)}) collective-permute-start(f32[2,5,3,3,128]{4,3,2,1,0:T(4,128)S(1)} %get-tuple-element.54), channel_id=1, source_target_pairs={{1,0},{2,1},{3,2},{4,3},{5,4},{6,5},{7,6},{0,7},{9,8},{10,9},{11,1... | collective-permute-start | bytes 138248 | tf_op jit(solution)/shard_map/ppermute | solution.py:472
  51.2 0.6 copy-start.5
  51.2 0.6 copy-start.6
  66.5 2.2 %copy-start = (f32[32,64,128]{2,1,0:T(8,128)}, f32[32,64,128]{2,1,0:T(8,128)S(1)}, u32[]{:S(2)}) copy-start(f32[32,64,128]{2,1,0:T(8,128)S(1)} %all-to-all-done) | copy-start | bytes 3145732

commit v4 on v3

--- a/solution.py
+++ b/solution.py
@@ -41,16 +41,8 @@
     n=mult.shape[0]; wrap=spare(n)-1
     copies=staged((move_,r2_,mult_),(move,r2s,mult),sem)
     buf[:n,:]=jnp.zeros_like(mult); buf[n:2*n,:]=jnp.zeros_like(mult)
+    rows_r[:LAN,:]=jnp.zeros((LAN,LAN),jnp.float32); rows_m[:LAN,:]=jnp.zeros((LAN,LAN),jnp.float32)
     for c in copies: c.wait()
-    def tile(t,_):
-        sl=pl.ds(pl.multiple_of(t*LAN,LAN),LAN)
-        r2=jnp.transpose(r2s[sl,:])
-        a,b,rank=collect_tile(r2,jnp.where(r2>0.0,jnp.transpose(mult[sl,:]),0.0))
-        rank=jnp.transpose(rank).astype(jnp.int32)
-        rows_r[sl,:]=jnp.take_along_axis(jnp.transpose(a),rank,axis=1)
-        rows_m[sl,:]=jnp.take_along_axis(jnp.transpose(b),rank,axis=1)
-        return 0
-    lax.fori_loop(0,n//LAN,tile,0)
     def put(b):
         s=move[b]&wrap
         if cap&(cap-1):
@@ -60,7 +52,20 @@
         at=s+lead*cap
         buf[pl.ds(at,1),:]=rows_r[pl.ds(b,1),:]
         buf[pl.ds(at+cap,1),:]=rows_m[pl.ds(b,1),:]
-    row_loop(n,32,put)
+    def tile(t,_):
+        sl=pl.ds(pl.multiple_of(t*LAN,LAN),LAN)
+        done=pl.multiple_of(jnp.maximum(t-1,0)*LAN,LAN)
+        for u in range(LAN):
+            put(done+u)
+        r2=jnp.transpose(r2s[sl,:])
+        a,b,rank=collect_tile(r2,jnp.where(r2>0.0,jnp.transpose(mult[sl,:]),0.0))
+        rank=jnp.transpose(rank).astype(jnp.int32)
+        rows_r[sl,:]=jnp.take_along_axis(jnp.transpose(a),rank,axis=1)
+        rows_m[sl,:]=jnp.take_along_axis(jnp.transpose(b),rank,axis=1)
+        return 0
+    lax.fori_loop(0,n//LAN,tile,0)
+    for u in range(LAN):
+        put(n-LAN+u)
     last=pltpu.make_async_copy(buf.at[pl.ds(0,2*n)],send,sem.at[0])
     last.start(); last.wait()
 
@@ -71,23 +76,35 @@
         scratch_shapes=[pltpu.SMEM((n,),jnp.int32)]+[F(n,LAN)]*4+[F(2*spare(n),LAN),pltpu.SemaphoreType.DMA((3,))],
         name="merge")(move,r2,mult)
 
-def home_kernel(cell_,cells_,counts_,tp_,vp_,radius_,floor_,mult_,send,heat_,cell,cells,counts,tp,vp,radius,floor,mult,rows_t,rows_v,heat,sem):
+def home_kernel(cell_,cells_,counts_,tp_,vp_,radius_,floor_,mult_,wu,wv,ww,send,ot_,ov_,xfirst,xlast,yfirst,ylast,cell,cells,counts,tp,vp,radius,floor,mult,rows_t,rows_v,heat,acct,accv,spot,wlo,whi,sem,wsem):
     n=radius.shape[0]; g=n//LAN
     depth_bits=LAN.bit_length()-1
     copies=staged((cell_,tp_,vp_,cells_,counts_,radius_,floor_,mult_),(cell,tp,vp,cells,counts,radius,floor,mult),sem)
+    nx,ny=wu.shape[:2]
+    loads=[]
+    for i,w in enumerate((wu,wv,ww)):
+        loads+=[pltpu.make_async_copy(w.at[:,pl.ds(0,SUB)],wlo.at[i],wsem.at[i]),
+                pltpu.make_async_copy(w.at[:,pl.ds(ny-SUB,SUB)],whi.at[i],wsem.at[3+i]),
+                pltpu.make_async_copy(w.at[pl.ds(0,W)],xfirst.at[2+i],wsem.at[6+i]),
+                pltpu.make_async_copy(w.at[pl.ds(nx-W,W)],xlast.at[2+i],wsem.at[9+i])]
     for c in copies[:3]: c.wait()
     def fetch(b):
         c=lax.shift_right_logical(cell[b],depth_bits)
         rows_t[pl.ds(b,1),:]=tp[pl.ds(c,1),:]
         rows_v[pl.ds(b,1),:]=vp[pl.ds(c,1),:]
-    row_loop(n,32,fetch)
+    row_loop(LAN,32,fetch)
     for c in copies[3:]: c.wait()
+    for c in loads: c.start()
     depth=lax.broadcasted_iota(jnp.int32,(LAN,LAN),0)
     def tile(t,_):
         sl=pl.ds(pl.multiple_of(t*LAN,LAN),LAN)
         here=depth==(cells[pl.ds(t,1),:]&(LAN-1))
-        temp0=jnp.sum(jnp.where(here,jnp.transpose(rows_t[sl,:]),0.0),axis=0,keepdims=True)
-        wet0=jnp.sum(jnp.where(here,jnp.transpose(rows_v[sl,:]),0.0),axis=0,keepdims=True)
+        near_t=rows_t[sl,:]; near_v=rows_v[sl,:]
+        ahead=pl.multiple_of(jnp.minimum(t+1,g-1)*LAN,LAN)
+        for u in range(LAN):
+            fetch(ahead+u)
+        temp0=jnp.sum(jnp.where(here,jnp.transpose(near_t),0.0),axis=0,keepdims=True)
+        wet0=jnp.sum(jnp.where(here,jnp.transpose(near_v),0.0),axis=0,keepdims=True)
         r=jnp.transpose(radius[sl,:]); fl=jnp.transpose(floor[sl,:])
         alive=depth<counts[pl.ds(t,1),:]
         m=jnp.where(alive,jnp.transpose(mult[sl,:]),0.0)
@@ -105,35 +122,11 @@
             r2=grown; mass=new
         heat[pl.ds(t,1),:]=temp-temp0; heat[pl.ds(g+t,1),:]=wet-wet0
         heat[pl.ds(2*g+t,1),:]=temp0; heat[pl.ds(3*g+t,1),:]=wet0
-        rows_t[sl,:]=jnp.transpose(jnp.where(alive,r2,0.0))
+        radius[sl,:]=jnp.transpose(jnp.where(alive,r2,0.0))
         return 0
     lax.fori_loop(0,g,tile,0)
-    first=pltpu.make_async_copy(heat,heat_,sem.at[1])
-    first.start()
-    last=pltpu.make_async_copy(rows_t,send,sem.at[0])
-    last.start(); last.wait(); first.wait()
-
-def home(cell,count,radius,floor,mult,tp,vp):
-    n=radius.shape[0]; g=n//LAN
-    cols=(tp.size//LAN,LAN); F=lambda *d: pltpu.VMEM(d,jnp.float32)
-    return pl.pallas_call(home_kernel,
-        out_shape=(jax.ShapeDtypeStruct(radius.shape,jnp.float32),jax.ShapeDtypeStruct((4*g,LAN),jnp.float32)),
-        in_specs=[ANY()]*8,out_specs=(ANY(),)*2,
-        scratch_shapes=[pltpu.SMEM((n,),jnp.int32)]+[pltpu.VMEM((g,LAN),jnp.int32)]*2+[F(*cols)]*2+[F(n,LAN)]*5
-            +[F(4*g,LAN),pltpu.SemaphoreType.DMA((9,))],
-        name="home")(cell,cell.reshape(g,LAN),count.reshape(g,LAN),tp.reshape(cols),vp.reshape(cols),radius,floor,mult)
-
-def scatter_kernel(column,level,cells,heat,tp,vp,wu,wv,ww,ot,ov,xfirst,xlast,yfirst,ylast,vt,vv,acct,accv,spot,wlo,whi,sem):
-    g=cells.shape[0]; n=g*LAN
-    nx,ny=tp.shape[:2]
-    winds=(wu,wv,ww)
-    loads=[pltpu.make_async_copy(tp,ot,sem.at[0]),pltpu.make_async_copy(vp,ov,sem.at[1])]
-    for i,w in enumerate(winds):
-        loads+=[pltpu.make_async_copy(w.at[:,pl.ds(0,SUB)],wlo.at[i],sem.at[2+i]),
-                pltpu.make_async_copy(w.at[:,pl.ds(ny-SUB,SUB)],whi.at[i],sem.at[5+i]),
-                pltpu.make_async_copy(w.at[pl.ds(0,W)],xfirst.at[2+i],sem.at[8+i]),
-                pltpu.make_async_copy(w.at[pl.ds(nx-W,W)],xlast.at[2+i],sem.at[11+i])]
-    for c in loads: c.start()
+    last=pltpu.make_async_copy(radius,send,sem.at[0])
+    last.start()
     spread=lambda ref,t: jnp.transpose(jnp.broadcast_to(ref[pl.ds(t,1),:],(LAN,LAN)))
     spot[...]=cells[...].astype(jnp.float32)
     acct[...]=jnp.zeros_like(acct); accv[...]=jnp.zeros_like(accv)
@@ -155,18 +148,20 @@
         s8=pl.ds(pl.multiple_of(t*SUB,SUB),SUB)
         nt=heat[pl.ds(2*g+t,1),:]+jnp.sum(acct[s8,:],axis=0,keepdims=True)
         nv=heat[pl.ds(3*g+t,1),:]+jnp.sum(accv[s8,:],axis=0,keepdims=True)
-        vt[sl,:]=jnp.transpose(jnp.broadcast_to(nt,(LAN,LAN)))
-        vv[sl,:]=jnp.transpose(jnp.broadcast_to(nv,(LAN,LAN)))
+        rows_t[sl,:]=jnp.transpose(jnp.broadcast_to(nt,(LAN,LAN)))
+        rows_v[sl,:]=jnp.transpose(jnp.broadcast_to(nv,(LAN,LAN)))
         return 0
     lax.fori_loop(0,g,rows,0)
     for c in loads: c.wait()
     lane=lax.broadcasted_iota(jnp.int32,(1,LAN),1)
-    flat_t=ot.reshape(nx*ny,LAN); flat_v=ov.reshape(nx*ny,LAN)
     def put(b):
-        c=column[b]; hit=lane==level[b]
-        pltpu.store(flat_t.at[pl.ds(c,1),:],vt[pl.ds(b,1),:],mask=hit)
-        pltpu.store(flat_v.at[pl.ds(c,1),:],vv[pl.ds(b,1),:],mask=hit)
+        x=cell[b]
+        c=lax.shift_right_logical(x,LAN.bit_length()-1); hit=lane==(x&(LAN-1))
+        pltpu.store(tp.at[pl.ds(c,1),:],rows_t[pl.ds(b,1),:],mask=hit)
+        pltpu.store(vp.at[pl.ds(c,1),:],rows_v[pl.ds(b,1),:],mask=hit)
     row_loop(n,32,put)
+    outs=staged((tp,vp),(ot_,ov_),wsem)
+    ot=tp.reshape(nx,ny,LAN); ov=vp.reshape(nx,ny,LAN)
     for i,o in enumerate((ot,ov)):
         xfirst[i]=o[0:W]; xlast[i]=o[nx-W:nx]
     def side(x,_):
@@ -177,16 +172,21 @@
             yfirst[2+i,at,:]=wlo[i,x,0:W,:]; ylast[2+i,at,:]=whi[i,x,SUB-W:SUB,:]
         return 0
     lax.fori_loop(0,nx,side,0,unroll=4)
-
-def scatter(column,level,cell,heat,tp,vp,*winds):
-    n=cell.shape[0]; g=n//LAN
+    last.wait()
+    for c in outs: c.wait()
+
+def home(cell,count,radius,floor,mult,tp,vp,*winds):
+    n=radius.shape[0]; g=n//LAN
     nx,ny,nz=tp.shape
+    cols=(nx*ny,nz); F=lambda *d: pltpu.VMEM(d,jnp.float32)
     S=lambda *d: jax.ShapeDtypeStruct(d,jnp.float32)
-    return pl.pallas_call(scatter_kernel,out_shape=(S(nx,ny,nz),)*2+(S(5,W,ny,nz),)*2+(S(5,nx*W,nz),)*2,
-        in_specs=[SMEM()]*2+[VM()]*2+[ANY()]*5,out_specs=(VM(),)*6,
-        scratch_shapes=[pltpu.VMEM((n,LAN),jnp.float32)]*2+[pltpu.VMEM((g*SUB,LAN),jnp.float32)]*2+[pltpu.VMEM((g,LAN),jnp.float32)]
-            +[pltpu.VMEM((3,nx,SUB,nz),jnp.float32)]*2+[pltpu.SemaphoreType.DMA((14,))],
-        name="scatter")(column,level,cell.reshape(g,LAN),heat,tp,vp,*winds)
+    r2,t,v,*edges=pl.pallas_call(home_kernel,
+        out_shape=(S(n,LAN),S(*cols),S(*cols))+(S(5,W,ny,nz),)*2+(S(5,nx*W,nz),)*2,
+        in_specs=[ANY()]*11,out_specs=(ANY(),)*3+(VM(),)*4,
+        scratch_shapes=[pltpu.SMEM((n,),jnp.int32)]+[pltpu.VMEM((g,LAN),jnp.int32)]*2+[F(*cols)]*2+[F(n,LAN)]*5
+            +[F(4*g,LAN)]+[F(g*SUB,LAN)]*2+[F(g,LAN)]+[F(3,nx,SUB,nz)]*2+[pltpu.SemaphoreType.DMA((8,)),pltpu.SemaphoreType.DMA((12,))],
+        name="home")(cell,cell.reshape(g,LAN),count.reshape(g,LAN),tp.reshape(cols),vp.reshape(cols),radius,floor,mult,*winds)
+    return r2,t.reshape(tp.shape),v.reshape(vp.shape),edges
 
 
 def batcher(n):
@@ -415,32 +415,38 @@
         name="advect")(t,v,u,w2,w3,*edges)
 
 
-def receive_kernel(cap, src, rows, ro_ref, mo_ref):
-    def pull(b):
-        s = src[b]
-        ro_ref[pl.ds(b, 1), :] = rows[pl.ds(s, 1), :]
-        mo_ref[pl.ds(b, 1), :] = rows[pl.ds(s + cap, 1), :]
-
-    row_loop(ro_ref.shape[0], 32, pull)
-
-
-def receive(cap, src, rows):
+def receive_kernel(cap, place, rows, ro_ref, mo_ref, rbuf, mbuf):
+    blocks = ro_ref.shape[0]
+    slots = place.shape[0]
+
+    def group(d, _):
+        at = pl.multiple_of(d * cap, cap)
+        for u in range(cap):
+            to = place[at + u]
+            rbuf[pl.ds(to, 1), :] = rows[pl.ds(2 * at + u, 1), :]
+            mbuf[pl.ds(to, 1), :] = rows[pl.ds(2 * at + cap + u, 1), :]
+        return 0
+
+    lax.fori_loop(0, slots // cap, group, 0)
+    ro_ref[...] = rbuf[:blocks, :]
+    mo_ref[...] = mbuf[:blocks, :]
+
+
+def receive(cap, place, rows):
     out = jax.ShapeDtypeStruct((BLK_DEV, LAN), jnp.float32)
     return pl.pallas_call(
         functools.partial(receive_kernel, cap),
         out_shape=(out, out),
         in_specs=[SMEM(), VM()],
         out_specs=(VM(), VM()),
+        scratch_shapes=[pltpu.VMEM((BLK_DEV + SUB, LAN), jnp.float32)] * 2,
         name="receive",
-    )(src, rows)
-
-
-def sources(rows, devices, cap):
+    )(place, rows)
+
+
+def places(rows, devices, cap):
     taken = rows.reshape(devices, 2, cap, LAN)[:, 0, :, 0].reshape(-1) > 0.0
-    position = jnp.cumsum(taken.astype(jnp.int32)) - 1
-    hit = (position[None, :] == jnp.arange(BLK_DEV, dtype=jnp.int32)[:, None]) & taken[None, :]
-    slots = jnp.arange(devices * cap, dtype=jnp.int32)
-    return jnp.sum(jnp.where(hit, (slots + slots // cap * cap)[None, :], 0), axis=1)
+    return jnp.where(taken, jnp.cumsum(taken.astype(jnp.int32)) - 1, BLK_DEV)
 
 
 def exchange(rows, devices):
@@ -487,15 +493,11 @@
     move_list,
 ):
     devices = lax.axis_size("gx") * lax.axis_size("gy")
-    levels = tprime.shape[2]
-    column = lax.shift_right_logical(cell_index, levels.bit_length() - 1)
-    level = cell_index & (levels - 1)
     winds = (wind_u, wind_v, wind_w)
     cap = (radius.shape[0] + devices - 1) // devices
-    r2, heat = home(
-        cell_index, drop_counts, radius, min_radius, multiplicity, tprime, vapor
+    r2, heated_t, heated_v, edges = home(
+        cell_index, drop_counts, radius, min_radius, multiplicity, tprime, vapor, *winds
     )
-    heated_t, heated_v, *edges = scatter(column, level, cell_index, heat, tprime, vapor, *winds)
     edges, r2 = lax.optimization_barrier((edges, r2))
     xlo, xhi, ylo, yhi = edge_halos(*edges)
     xlo, xhi, ylo, yhi, sent = lax.optimization_barrier(
@@ -507,7 +509,7 @@
         heated_t, heated_v, *winds, xlo, xhi, ylo, yhi, clo, chi
     )
     moved, temperature_out = lax.optimization_barrier((moved, temperature_out))
-    radius_out, multiplicity_out = receive(cap, sources(moved, devices, cap), moved)
+    radius_out, multiplicity_out = receive(cap, places(moved, devices, cap), moved)
     return (temperature_out, vapor_out, radius_out, multiplicity_out)
 
 

time: 71.7 us -> 68.3 us (0.953)
  Pallas kernels: 41.6 us -> 39.3 us
  other arithmetic: 2.8 us -> 1.02 us
  waiting for transfers between devices: 10 us -> 10.9 us
    ppermute x1, waiting for transfers between devices: 0.01 us -> 6.33 us  [corner_halos(): chi = lax.ppermute(ends[:, :, :, :W], 'gy', down)]
    ppermute x1, waiting for transfers between devices: 8.11 us -> 2.19 us  [corner_halos(): clo = lax.ppermute(ends[:, :, :, ny - W:], 'gy', up)]
    pallas_call x1, Pallas kernels: 11.2 us -> 9.4 us  [merge(): pl.pallas_call(functools.partial(merge_kernel, cap), out_shape=jax.ShapeD...]
    and x1 -> x0, other arithmetic: 1.28 us -> none  [body(): level = cell_index & levels - 1]
    pallas_call x2 -> x1, Pallas kernels: 15 us -> 13.8 us  [home(): pl.pallas_call(home_kernel, out_shape=(S(n, LAN), S(*cols), S(*cols)) + (...]
    reduce_sum x1 -> x0, other arithmetic: 1.1 us -> none  [sources(): jnp.sum(jnp.where(hit, (slots + slots // cap * cap)[None, :], 0), axis=1)]
  transfers between devices with their start and end apart: 7 -> 7, of which waited for: 2 -> 4; matrix products, arithmetic and copies ran while one was open for 0% -> 0% of each run, Pallas kernels for 34% -> 33%
where the time goes in v4:
time: 68.3 us; the launch traced here: 68 us
  Pallas kernels  39.3 us (58%)
  starting transfers between devices  13.9 us (20%)
  waiting for transfers between devices  10.9 us (16%)
  local copies, waits for them, and re-layouts  2.24 us (3%)
  other arithmetic  1.02 us (1%)
  between operations  0.74 us (1%)
    pallas_call x1, Pallas kernels, home(): pl.pallas_call(home_kernel, out_shape=(S(n, LAN), S(*cols), S(*cols)) + (...  13.8 us
    pallas_call x1, Pallas kernels, advect(): pl.pallas_call(advect_kernel, out_shape=(o, o), in_specs=[ANY] * 11, out_...  12.8 us
    pallas_call x1, Pallas kernels, merge(): pl.pallas_call(functools.partial(merge_kernel, cap), out_shape=jax.ShapeD...  9.4 us
    ppermute x1, waiting for transfers between devices, corner_halos(): chi = lax.ppermute(ends[:, :, :, :W], 'gy', down)  6.33 us
    all_to_all x1, starting transfers between devices, exchange(): lax.all_to_all(rows.reshape((devices, -1) + rows.shape[1:]), ('gx', 'gy')...  3.63 us
    pallas_call x1, Pallas kernels, receive(): pl.pallas_call(functools.partial(receive_kernel, cap), out_shape=(out, ou...  3.3 us
    ppermute x1, starting transfers between devices, edge_halos(): lax.ppermute(yfirst, 'gy', down)  2.93 us
    ppermute x1, starting transfers between devices, corner_halos(): chi = lax.ppermute(ends[:, :, :, :W], 'gy', down)  2.44 us
  transfers between devices with their start and end apart: 7, of which 4 were waited for; matrix products, arithmetic and copies ran while one was open for 0% of the time, Pallas kernels for 33%

profile of v4, /device:TPU:0, one launch (start us, length us, event | category | flops | bytes accessed | tf_op | source)
XLA Modules:
  0.0 68.0 jit_solution(6312688037152224420)
XLA Ops:
  0.6 13.8 %home.1 = (f32[1024,128]{1,0:T(8,128)}, f32[2048,128]{1,0:T(8,128)}, f32[2048,128]{1,0:T(8,128)}, f32[5,3,32,128]{3,2,1,0:T(8,128)}, f32[5,3,32,128]{3,2,1,0:T(8...) custom-call(s32[1024]{0:T(1024)} %cell_.1, s32[8,128]{1,0:T(8,128)} %bitcast.30, s32[8,128]{1,0:T(8,128)} %bitcast.31, ...), custom_call_target="tpu_custom_call" | custom-call | tf_op jit(solution)/shard_map/home/pallas_call | solution.py:183
  14.4 0.5 collective-permute-start.2
  15.0 2.9 %collective-permute-start.3 = (f32[5,192,128]{2,1,0:T(8,128)}, f32[5,192,128]{2,1,0:T(8,128)S(1)}, u32[]{:S(2)}, u32[]{:S(2)}) collective-permute-start(f32[5,192,128]{2,1,0:T(8,128)} %get-tuple-element.35), channel_id=1, source_target_pairs={{1,0},{2,1},{3,2},{4,3},{5,4},{6,5},{7,6},{0,7},{9,8},{10,9},{11,1... | collective-permute-start | bytes 1474568 | tf_op jit(solution)/shard_map/ppermute | solution.py:470
  17.9 2.3 %collective-permute-start = (f32[5,3,32,128]{3,2,1,0:T(8,128)}, f32[5,3,32,128]{3,2,1,0:T(8,128)S(1)}, u32[]{:S(2)}, u32[]{:S(2)}) collective-permute-start(f32[5,3,32,128]{3,2,1,0:T(8,128)} %get-tuple-element.32), channel_id=1, source_target_pairs={{0,8},{8,16},{16,24},{24,0},{1,9},{9,17},{17,25},{25,1},{2,10},{10... | collective-permute-start | bytes 737288 | tf_op jit(solution)/shard_map/ppermute | solution.py:467
  20.2 2.0 %collective-permute-start.1 = (f32[5,3,32,128]{3,2,1,0:T(8,128)}, f32[5,3,32,128]{3,2,1,0:T(8,128)S(1)}, u32[]{:S(2)}, u32[]{:S(2)}) collective-permute-start(f32[5,3,32,128]{3,2,1,0:T(8,128)} %get-tuple-element.33), channel_id=1, source_target_pairs={{8,0},{16,8},{24,16},{0,24},{9,1},{17,9},{25,17},{1,25},{10,2},{18... | collective-permute-start | bytes 737288 | tf_op jit(solution)/shard_map/ppermute | solution.py:468
  22.2 9.4 %merge.1 = f32[2048,128]{1,0:T(8,128)} custom-call(s32[1024]{0:T(1024)} %move_.1, f32[1024,128]{1,0:T(8,128)} %get-tuple-element.36.r2_, f32[1024,128]{1,0:T(8,128)} %mult_.3), custom_call_target="tpu_custom_call" | custom-call | tf_op jit(solution)/shard_map/merge/pallas_call | solution.py:74
  31.6 0.0 collective-permute-done.xlo_
  31.6 0.0 copy-start.1
  31.7 0.6 collective-permute-done.1.xhi_
  32.2 0.0 copy-start.2
  32.2 0.0 collective-permute-done.2.ylo_
  32.2 0.0 copy-start.3
  32.2 0.0 collective-permute-done.3.yhi_
  32.2 0.0 copy-start.4
  32.2 0.8 %copy-done.3 = f32[5,192,128]{2,1,0:T(8,128)} copy-done((f32[5,192,128]{2,1,0:T(8,128)}, f32[5,192,128]{2,1,0:T(8,128)S(1)}, u32[]{:S(2)}) %copy-start.3) | copy-done | bytes 491544
  33.0 0.2 copy-done.4
  33.2 3.6 %all-to-all-start = ((f32[32,64,128]{2,1,0:T(8,128)}), f32[32,64,128]{2,1,0:T(8,128)S(1)}, u32[]{:S(2)}, u32[]{:S(2)}) async-start(f32[32,64,128]{2,1,0:T(8,128)} %bitcast.23), calls=%async_computation | async-start | bytes 2097152 | tf_op jit(solution)/shard_map/all_to_all | solution.py:453
  36.9 0.0 copy-done.1
  36.9 0.0 copy-done.2
  36.9 2.4 %collective-permute-start.5 = (f32[2,5,3,3,128]{4,3,2,1,0:T(4,128)S(1)}, f32[2,5,3,3,128]{4,3,2,1,0:T(4,128)S(1)}, u32[]{:S(2)}, u32[]{:S(2)}) collective-permute-start(f32[2,5,3,3,128]{4,3,2,1,0:T(4,128)S(1)} %get-tuple-element.52), channel_id=1, source_target_pairs={{1,0},{2,1},{3,2},{4,3},{5,4},{6,5},{7,6},{0,7},{9,8},{10,9},{11,1... | collective-permute-start | bytes 138248 | tf_op jit(solution)/shard_map/ppermute | solution.py:478
  39.4 0.0 collective-permute-start.4
  39.4 6.3 %collective-permute-done.5.chi_ = f32[2,5,3,3,128]{4,3,2,1,0:T(4,128)S(1)} collective-permute-done((f32[2,5,3,3,128]{4,3,2,1,0:T(4,128)S(1)}, f32[2,5,3,3,128]{4,3,2,1,0:T(4,128)S(1)}, u32[]{:S(2)}, u32[]{:S(2)}) %collective-permute-start.5) | collective-permute-done | bytes 46112 | tf_op jit(solution)/shard_map/ppermute | solution.py:478
  45.7 0.0 copy-start.5
  45.7 2.2 %collective-permute-done.4.clo_ = f32[2,5,3,3,128]{4,3,2,1,0:T(4,128)S(1)} collective-permute-done((f32[2,5,3,3,128]{4,3,2,1,0:T(4,128)S(1)}, f32[2,5,3,3,128]{4,3,2,1,0:T(4,128)S(1)}, u32[]{:S(2)}, u32[]{:S(2)}) %collective-permute-start.4) | collective-permute-done | bytes 46112 | tf_op jit(solution)/shard_map/ppermute | solution.py:477
  47.9 0.0 copy-start.6
  47.9 0.0 copy-done.5
  47.9 0.6 copy-done.6
  48.5 12.8 %advect.1 = (f32[64,32,128]{2,1,0:T(8,128)}, f32[64,32,128]{2,1,0:T(8,128)}) custom-call(f32[64,32,128]{2,1,0:T(8,128)} %bitcast.26, f32[64,32,128]{2,1,0:T(8,128)} %bitcast.27, f32[64,32,128]{2,1,0:T(8,128)} %uc.1, f32[64,32,128]{2,1,0:T(8,128)} %vw.1, f32[64,32,128]{2,1,0:T(8,128)} %wc.1, f32[5,3,32,128]{3,2,1,0:T(8,128)} %copy-done.1, ...), custom_call_target="tpu_custom_call" | custom-call | tf_op jit(solution)/shard_map/advect/pallas_call | solution.py:411
  61.3 1.8 %all-to-all-done = f32[32,64,128]{2,1,0:T(8,128)S(1)} async-done(((f32[32,64,128]{2,1,0:T(8,128)}), f32[32,64,128]{2,1,0:T(8,128)S(1)}, u32[]{:S(2)}, u32[]{:S(2)}) %all-to-all-start) | async-done | bytes 1048608 | tf_op jit(solution)/shard_map/all_to_all | solution.py:453
  63.1 0.0 copy-start
  63.1 0.2 copy.16
  63.4 0.1 reshape.67
  63.4 0.1 gt.13
  63.5 0.3 reduce-window.9
  63.8 0.1 slice.19
  63.9 0.1 slice_reduce_fusion
  64.0 0.7 bitcast_select_fusion.place
  64.7 0.0 copy-done
  64.7 3.3 %receive.1 = (f32[512,128]{1,0:T(8,128)}, f32[512,128]{1,0:T(8,128)}) custom-call(s32[1024]{0:T(1024)} %bitcast_select_fusion.place, f32[2048,128]{1,0:T(8,128)} %bitcast.22), custom_call_target="tpu_custom_call" | custom-call | tf_op jit(solution)/shard_map/receive/pallas_call | solution.py:437
  (4 shorter events, 0.1 us)
Async XLA Ops:
  14.4 17.8 %collective-permute-start.2 = (f32[5,192,128]{2,1,0:T(8,128)}, f32[5,192,128]{2,1,0:T(8,128)S(1)}, u32[]{:S(2)}, u32[]{:S(2)}) collective-permute-start(f32[5,192,128]{2,1,0:T(8,128)} %get-tuple-element.34), channel_id=1, source_target_pairs={{0,1},{1,2},{2,3},{3,4},{4,5},{5,6},{6,7},{7,0},{8,9},{9,10},{10,1... | collective-permute-start | bytes 1474568 | tf_op jit(solution)/shard_map/ppermute | solution.py:470
  15.0 17.2 %collective-permute-start.3 = (f32[5,192,128]{2,1,0:T(8,128)}, f32[5,192,128]{2,1,0:T(8,128)S(1)}, u32[]{:S(2)}, u32[]{:S(2)}) collective-permute-start(f32[5,192,128]{2,1,0:T(8,128)} %get-tuple-element.35), channel_id=1, source_target_pairs={{1,0},{2,1},{3,2},{4,3},{5,4},{6,5},{7,6},{0,7},{9,8},{10,9},{11,1... | collective-permute-start | bytes 1474568 | tf_op jit(solution)/shard_map/ppermute | solution.py:470
  17.9 13.7 %collective-permute-start = (f32[5,3,32,128]{3,2,1,0:T(8,128)}, f32[5,3,32,128]{3,2,1,0:T(8,128)S(1)}, u32[]{:S(2)}, u32[]{:S(2)}) collective-permute-start(f32[5,3,32,128]{3,2,1,0:T(8,128)} %get-tuple-element.32), channel_id=1, source_target_pairs={{0,8},{8,16},{16,24},{24,0},{1,9},{9,17},{17,25},{25,1},{2,10},{10... | collective-permute-start | bytes 737288 | tf_op jit(solution)/shard_map/ppermute | solution.py:467
  20.2 12.0 %collective-permute-start.1 = (f32[5,3,32,128]{3,2,1,0:T(8,128)}, f32[5,3,32,128]{3,2,1,0:T(8,128)S(1)}, u32[]{:S(2)}, u32[]{:S(2)}) collective-permute-start(f32[5,3,32,128]{3,2,1,0:T(8,128)} %get-tuple-element.33), channel_id=1, source_target_pairs={{8,0},{16,8},{24,16},{0,24},{9,1},{17,9},{25,17},{1,25},{10,2},{18... | collective-permute-start | bytes 737288 | tf_op jit(solution)/shard_map/ppermute | solution.py:468
  31.6 5.2 %copy-start.1 = (f32[5,3,32,128]{3,2,1,0:T(8,128)}, f32[5,3,32,128]{3,2,1,0:T(8,128)S(1)}, u32[]{:S(2)}) copy-start(f32[5,3,32,128]{3,2,1,0:T(8,128)S(1)} %collective-permute-done.xlo_) | copy-start | bytes 737284
  32.2 4.6 %copy-start.2 = (f32[5,3,32,128]{3,2,1,0:T(8,128)}, f32[5,3,32,128]{3,2,1,0:T(8,128)S(1)}, u32[]{:S(2)}) copy-start(f32[5,3,32,128]{3,2,1,0:T(8,128)S(1)} %collective-permute-done.1.xhi_) | copy-start | bytes 737284
  32.2 0.8 %copy-start.3 = (f32[5,192,128]{2,1,0:T(8,128)}, f32[5,192,128]{2,1,0:T(8,128)S(1)}, u32[]{:S(2)}) copy-start(f32[5,192,128]{2,1,0:T(8,128)S(1)} %collective-permute-done.2.ylo_) | copy-start | bytes 1474564
  32.2 1.0 %copy-start.4 = (f32[5,192,128]{2,1,0:T(8,128)}, f32[5,192,128]{2,1,0:T(8,128)S(1)}, u32[]{:S(2)}) copy-start(f32[5,192,128]{2,1,0:T(8,128)S(1)} %collective-permute-done.3.yhi_) | copy-start | bytes 1474564
  33.2 29.8 %all-to-all-start = ((f32[32,64,128]{2,1,0:T(8,128)}), f32[32,64,128]{2,1,0:T(8,128)S(1)}, u32[]{:S(2)}, u32[]{:S(2)}) async-start(f32[32,64,128]{2,1,0:T(8,128)} %bitcast.23), calls=%async_computation | async-start | bytes 2097152 | tf_op jit(solution)/shard_map/all_to_all | solution.py:453
  36.9 8.8 %collective-permute-start.5 = (f32[2,5,3,3,128]{4,3,2,1,0:T(4,128)S(1)}, f32[2,5,3,3,128]{4,3,2,1,0:T(4,128)S(1)}, u32[]{:S(2)}, u32[]{:S(2)}) collective-permute-start(f32[2,5,3,3,128]{4,3,2,1,0:T(4,128)S(1)} %get-tuple-element.52), channel_id=1, source_target_pairs={{1,0},{2,1},{3,2},{4,3},{5,4},{6,5},{7,6},{0,7},{9,8},{10,9},{11,1... | collective-permute-start | bytes 138248 | tf_op jit(solution)/shard_map/ppermute | solution.py:478
  39.4 8.5 %collective-permute-start.4 = (f32[2,5,3,3,128]{4,3,2,1,0:T(4,128)S(1)}, f32[2,5,3,3,128]{4,3,2,1,0:T(4,128)S(1)}, u32[]{:S(2)}, u32[]{:S(2)}) collective-permute-start(f32[2,5,3,3,128]{4,3,2,1,0:T(4,128)S(1)} %get-tuple-element.53), channel_id=1, source_target_pairs={{0,1},{1,2},{2,3},{3,4},{4,5},{5,6},{6,7},{7,0},{8,9},{9,10},{10,1... | collective-permute-start | bytes 138248 | tf_op jit(solution)/shard_map/ppermute | solution.py:477
  45.7 2.2 %copy-start.5 = (f32[2,5,3,3,128]{4,3,2,1,0:T(4,128)}, f32[2,5,3,3,128]{4,3,2,1,0:T(4,128)S(1)}, u32[]{:S(2)}) copy-start(f32[2,5,3,3,128]{4,3,2,1,0:T(4,128)S(1)} %collective-permute-done.5.chi_) | copy-start | bytes 138244
  47.9 0.6 copy-start.6
  63.1 1.7 %copy-start = (f32[32,64,128]{2,1,0:T(8,128)}, f32[32,64,128]{2,1,0:T(8,128)S(1)}, u32[]{:S(2)}) copy-start(f32[32,64,128]{2,1,0:T(8,128)S(1)} %all-to-all-done) | copy-start | bytes 3145732

commit v5 on v4

--- a/solution.py
+++ b/solution.py
@@ -415,9 +415,22 @@
         name="advect")(t,v,u,w2,w3,*edges)
 
 
-def receive_kernel(cap, place, rows, ro_ref, mo_ref, rbuf, mbuf):
+def receive_kernel(cap, place_, rows_, ro_ref, mo_ref, place, rows, rbuf, mbuf, sem, psem):
     blocks = ro_ref.shape[0]
-    slots = place.shape[0]
+    groups = place.shape[0] // cap
+    parts = 4 if groups % 4 == 0 else 1
+    size = rows.shape[0] // parts
+    first = pltpu.make_async_copy(place_, place, psem)
+    first.start()
+    loads = [
+        pltpu.make_async_copy(
+            rows_.at[pl.ds(i * size, size)], rows.at[pl.ds(i * size, size)], sem.at[i]
+        )
+        for i in range(parts)
+    ]
+    for c in loads:
+        c.start()
+    first.wait()
 
     def group(d, _):
         at = pl.multiple_of(d * cap, cap)
@@ -427,7 +440,9 @@
             mbuf[pl.ds(to, 1), :] = rows[pl.ds(2 * at + cap + u, 1), :]
         return 0
 
-    lax.fori_loop(0, slots // cap, group, 0)
+    for i, c in enumerate(loads):
+        c.wait()
+        lax.fori_loop(i * groups // parts, (i + 1) * groups // parts, group, 0)
     ro_ref[...] = rbuf[:blocks, :]
     mo_ref[...] = mbuf[:blocks, :]
 
@@ -437,9 +452,11 @@
     return pl.pallas_call(
         functools.partial(receive_kernel, cap),
         out_shape=(out, out),
-        in_specs=[SMEM(), VM()],
+        in_specs=[ANY(), ANY()],
         out_specs=(VM(), VM()),
-        scratch_shapes=[pltpu.VMEM((BLK_DEV + SUB, LAN), jnp.float32)] * 2,
+        scratch_shapes=[pltpu.SMEM(place.shape, jnp.int32), pltpu.VMEM(rows.shape, jnp.float32)]
+        + [pltpu.VMEM((BLK_DEV + SUB, LAN), jnp.float32)] * 2
+        + [pltpu.SemaphoreType.DMA((4,)), pltpu.SemaphoreType.DMA(())],
         name="receive",
     )(place, rows)
 

time: 68.3 us -> 68 us (level)
  no operation moved by 1% of the time
where the time goes in v5:
time: 68 us; the launch traced here: 67.8 us
  Pallas kernels  39 us (57%)
  starting transfers between devices  13.9 us (20%)
  waiting for transfers between devices  10.9 us (16%)
  local copies, waits for them, and re-layouts  2.24 us (3%)
  other arithmetic  1.02 us (2%)
  between operations  0.74 us (1%)
    pallas_call x1, Pallas kernels, home(): pl.pallas_call(home_kernel, out_shape=(S(n, LAN), S(*cols), S(*cols)) + (...  13.8 us
    pallas_call x1, Pallas kernels, advect(): pl.pallas_call(advect_kernel, out_shape=(o, o), in_specs=[ANY] * 11, out_...  12.8 us
    pallas_call x1, Pallas kernels, merge(): pl.pallas_call(functools.partial(merge_kernel, cap), out_shape=jax.ShapeD...  9.4 us
    ppermute x1, waiting for transfers between devices, corner_halos(): chi = lax.ppermute(ends[:, :, :, :W], 'gy', down)  6.33 us
    all_to_all x1, starting transfers between devices, exchange(): lax.all_to_all(rows.reshape((devices, -1) + rows.shape[1:]), ('gx', 'gy')...  3.64 us
    pallas_call x1, Pallas kernels, receive(): pl.pallas_call(functools.partial(receive_kernel, cap), out_shape=(out, ou...  3.05 us
    ppermute x1, starting transfers between devices, edge_halos(): lax.ppermute(yfirst, 'gy', down)  2.93 us
    ppermute x1, starting transfers between devices, corner_halos(): chi = lax.ppermute(ends[:, :, :, :W], 'gy', down)  2.44 us
  transfers between devices with their start and end apart: 7, of which 4 were waited for; matrix products, arithmetic and copies ran while one was open for 0% of the time, Pallas kernels for 33%

profile of v5, /device:TPU:0, one launch (start us, length us, event | category | flops | bytes accessed | tf_op | source)
XLA Modules:
  0.0 67.8 jit_solution(17946306126339295801)
XLA Ops:
  0.6 13.8 %home.1 = (f32[1024,128]{1,0:T(8,128)}, f32[2048,128]{1,0:T(8,128)}, f32[2048,128]{1,0:T(8,128)}, f32[5,3,32,128]{3,2,1,0:T(8,128)}, f32[5,3,32,128]{3,2,1,0:T(8...) custom-call(s32[1024]{0:T(1024)} %cell_.1, s32[8,128]{1,0:T(8,128)} %bitcast.30, s32[8,128]{1,0:T(8,128)} %bitcast.31, ...), custom_call_target="tpu_custom_call" | custom-call | tf_op jit(solution)/shard_map/home/pallas_call | solution.py:183
  14.4 0.5 collective-permute-start.2
  15.0 2.9 %collective-permute-start.3 = (f32[5,192,128]{2,1,0:T(8,128)}, f32[5,192,128]{2,1,0:T(8,128)S(1)}, u32[]{:S(2)}, u32[]{:S(2)}) collective-permute-start(f32[5,192,128]{2,1,0:T(8,128)} %get-tuple-element.35), channel_id=1, source_target_pairs={{1,0},{2,1},{3,2},{4,3},{5,4},{6,5},{7,6},{0,7},{9,8},{10,9},{11,1... | collective-permute-start | bytes 1474568 | tf_op jit(solution)/shard_map/ppermute | solution.py:487
  17.9 2.3 %collective-permute-start = (f32[5,3,32,128]{3,2,1,0:T(8,128)}, f32[5,3,32,128]{3,2,1,0:T(8,128)S(1)}, u32[]{:S(2)}, u32[]{:S(2)}) collective-permute-start(f32[5,3,32,128]{3,2,1,0:T(8,128)} %get-tuple-element.32), channel_id=1, source_target_pairs={{0,8},{8,16},{16,24},{24,0},{1,9},{9,17},{17,25},{25,1},{2,10},{10... | collective-permute-start | bytes 737288 | tf_op jit(solution)/shard_map/ppermute | solution.py:484
  20.2 2.0 %collective-permute-start.1 = (f32[5,3,32,128]{3,2,1,0:T(8,128)}, f32[5,3,32,128]{3,2,1,0:T(8,128)S(1)}, u32[]{:S(2)}, u32[]{:S(2)}) collective-permute-start(f32[5,3,32,128]{3,2,1,0:T(8,128)} %get-tuple-element.33), channel_id=1, source_target_pairs={{8,0},{16,8},{24,16},{0,24},{9,1},{17,9},{25,17},{1,25},{10,2},{18... | collective-permute-start | bytes 737288 | tf_op jit(solution)/shard_map/ppermute | solution.py:485
  22.2 9.4 %merge.1 = f32[2048,128]{1,0:T(8,128)} custom-call(s32[1024]{0:T(1024)} %move_.1, f32[1024,128]{1,0:T(8,128)} %get-tuple-element.36.r2_, f32[1024,128]{1,0:T(8,128)} %mult_.3), custom_call_target="tpu_custom_call" | custom-call | tf_op jit(solution)/shard_map/merge/pallas_call | solution.py:74
  31.6 0.0 collective-permute-done.xlo_
  31.6 0.0 copy-start.1
  31.7 0.6 collective-permute-done.1.xhi_
  32.2 0.0 copy-start.2
  32.2 0.0 collective-permute-done.2.ylo_
  32.2 0.0 copy-start.3
  32.2 0.0 collective-permute-done.3.yhi_
  32.2 0.0 copy-start.4
  32.2 0.8 %copy-done.3 = f32[5,192,128]{2,1,0:T(8,128)} copy-done((f32[5,192,128]{2,1,0:T(8,128)}, f32[5,192,128]{2,1,0:T(8,128)S(1)}, u32[]{:S(2)}) %copy-start.3) | copy-done | bytes 491544
  33.0 0.2 copy-done.4
  33.2 3.6 %all-to-all-start = ((f32[32,64,128]{2,1,0:T(8,128)}), f32[32,64,128]{2,1,0:T(8,128)S(1)}, u32[]{:S(2)}, u32[]{:S(2)}) async-start(f32[32,64,128]{2,1,0:T(8,128)} %bitcast.23), calls=%async_computation | async-start | bytes 2097152 | tf_op jit(solution)/shard_map/all_to_all | solution.py:470
  36.9 0.0 copy-done.1
  36.9 0.0 copy-done.2
  36.9 2.4 %collective-permute-start.5 = (f32[2,5,3,3,128]{4,3,2,1,0:T(4,128)S(1)}, f32[2,5,3,3,128]{4,3,2,1,0:T(4,128)S(1)}, u32[]{:S(2)}, u32[]{:S(2)}) collective-permute-start(f32[2,5,3,3,128]{4,3,2,1,0:T(4,128)S(1)} %get-tuple-element.52), channel_id=1, source_target_pairs={{1,0},{2,1},{3,2},{4,3},{5,4},{6,5},{7,6},{0,7},{9,8},{10,9},{11,1... | collective-permute-start | bytes 138248 | tf_op jit(solution)/shard_map/ppermute | solution.py:495
  39.4 0.0 collective-permute-start.4
  39.4 6.3 %collective-permute-done.5.chi_ = f32[2,5,3,3,128]{4,3,2,1,0:T(4,128)S(1)} collective-permute-done((f32[2,5,3,3,128]{4,3,2,1,0:T(4,128)S(1)}, f32[2,5,3,3,128]{4,3,2,1,0:T(4,128)S(1)}, u32[]{:S(2)}, u32[]{:S(2)}) %collective-permute-start.5) | collective-permute-done | bytes 46112 | tf_op jit(solution)/shard_map/ppermute | solution.py:495
  45.7 0.0 copy-start.5
  45.7 2.2 %collective-permute-done.4.clo_ = f32[2,5,3,3,128]{4,3,2,1,0:T(4,128)S(1)} collective-permute-done((f32[2,5,3,3,128]{4,3,2,1,0:T(4,128)S(1)}, f32[2,5,3,3,128]{4,3,2,1,0:T(4,128)S(1)}, u32[]{:S(2)}, u32[]{:S(2)}) %collective-permute-start.4) | collective-permute-done | bytes 46112 | tf_op jit(solution)/shard_map/ppermute | solution.py:494
  47.9 0.0 copy-start.6
  47.9 0.0 copy-done.5
  47.9 0.6 copy-done.6
  48.5 12.8 %advect.1 = (f32[64,32,128]{2,1,0:T(8,128)}, f32[64,32,128]{2,1,0:T(8,128)}) custom-call(f32[64,32,128]{2,1,0:T(8,128)} %bitcast.26, f32[64,32,128]{2,1,0:T(8,128)} %bitcast.27, f32[64,32,128]{2,1,0:T(8,128)} %uc.1, f32[64,32,128]{2,1,0:T(8,128)} %vw.1, f32[64,32,128]{2,1,0:T(8,128)} %wc.1, f32[5,3,32,128]{3,2,1,0:T(8,128)} %copy-done.1, ...), custom_call_target="tpu_custom_call" | custom-call | tf_op jit(solution)/shard_map/advect/pallas_call | solution.py:411
  61.3 1.8 %all-to-all-done = f32[32,64,128]{2,1,0:T(8,128)S(1)} async-done(((f32[32,64,128]{2,1,0:T(8,128)}), f32[32,64,128]{2,1,0:T(8,128)S(1)}, u32[]{:S(2)}, u32[]{:S(2)}) %all-to-all-start) | async-done | bytes 1048608 | tf_op jit(solution)/shard_map/all_to_all | solution.py:470
  63.1 0.0 copy-start
  63.1 0.2 copy.16
  63.4 0.1 reshape.67
  63.5 0.1 gt.13
  63.5 0.3 reduce-window.9
  63.8 0.1 slice.19
  63.9 0.1 slice_reduce_fusion
  64.0 0.7 %bitcast_select_fusion.place_ = s32[1024]{0:T(1024)} fusion(pred[1024]{0:T(1024)(128)(4,1)S(1)} %gt.13, s32[8,128]{1,0:T(8,128)S(1)} %reduce-window.9, s32[8]{0:T(128)S(1)} %slice_reduce_fusion), kind=kLoop, calls=%fused_computation.4 | loop fusion | flops 3072 | bytes 9248 | tf_op jit(solution)/shard_map/jit(_where)/select_n | solution.py:466
  64.7 0.0 copy-done
  64.7 3.0 %receive.1 = (f32[512,128]{1,0:T(8,128)}, f32[512,128]{1,0:T(8,128)}) custom-call(s32[1024]{0:T(1024)} %bitcast_select_fusion.place_, f32[2048,128]{1,0:T(8,128)} %bitcast.22), custom_call_target="tpu_custom_call" | custom-call | tf_op jit(solution)/shard_map/receive/pallas_call | solution.py:452
  (4 shorter events, 0.1 us)
Async XLA Ops:
  14.4 17.8 %collective-permute-start.2 = (f32[5,192,128]{2,1,0:T(8,128)}, f32[5,192,128]{2,1,0:T(8,128)S(1)}, u32[]{:S(2)}, u32[]{:S(2)}) collective-permute-start(f32[5,192,128]{2,1,0:T(8,128)} %get-tuple-element.34), channel_id=1, source_target_pairs={{0,1},{1,2},{2,3},{3,4},{4,5},{5,6},{6,7},{7,0},{8,9},{9,10},{10,1... | collective-permute-start | bytes 1474568 | tf_op jit(solution)/shard_map/ppermute | solution.py:487
  15.0 17.2 %collective-permute-start.3 = (f32[5,192,128]{2,1,0:T(8,128)}, f32[5,192,128]{2,1,0:T(8,128)S(1)}, u32[]{:S(2)}, u32[]{:S(2)}) collective-permute-start(f32[5,192,128]{2,1,0:T(8,128)} %get-tuple-element.35), channel_id=1, source_target_pairs={{1,0},{2,1},{3,2},{4,3},{5,4},{6,5},{7,6},{0,7},{9,8},{10,9},{11,1... | collective-permute-start | bytes 1474568 | tf_op jit(solution)/shard_map/ppermute | solution.py:487
  17.9 13.7 %collective-permute-start = (f32[5,3,32,128]{3,2,1,0:T(8,128)}, f32[5,3,32,128]{3,2,1,0:T(8,128)S(1)}, u32[]{:S(2)}, u32[]{:S(2)}) collective-permute-start(f32[5,3,32,128]{3,2,1,0:T(8,128)} %get-tuple-element.32), channel_id=1, source_target_pairs={{0,8},{8,16},{16,24},{24,0},{1,9},{9,17},{17,25},{25,1},{2,10},{10... | collective-permute-start | bytes 737288 | tf_op jit(solution)/shard_map/ppermute | solution.py:484
  20.2 12.0 %collective-permute-start.1 = (f32[5,3,32,128]{3,2,1,0:T(8,128)}, f32[5,3,32,128]{3,2,1,0:T(8,128)S(1)}, u32[]{:S(2)}, u32[]{:S(2)}) collective-permute-start(f32[5,3,32,128]{3,2,1,0:T(8,128)} %get-tuple-element.33), channel_id=1, source_target_pairs={{8,0},{16,8},{24,16},{0,24},{9,1},{17,9},{25,17},{1,25},{10,2},{18... | collective-permute-start | bytes 737288 | tf_op jit(solution)/shard_map/ppermute | solution.py:485
  31.6 5.2 %copy-start.1 = (f32[5,3,32,128]{3,2,1,0:T(8,128)}, f32[5,3,32,128]{3,2,1,0:T(8,128)S(1)}, u32[]{:S(2)}) copy-start(f32[5,3,32,128]{3,2,1,0:T(8,128)S(1)} %collective-permute-done.xlo_) | copy-start | bytes 737284
  32.2 4.7 %copy-start.2 = (f32[5,3,32,128]{3,2,1,0:T(8,128)}, f32[5,3,32,128]{3,2,1,0:T(8,128)S(1)}, u32[]{:S(2)}) copy-start(f32[5,3,32,128]{3,2,1,0:T(8,128)S(1)} %collective-permute-done.1.xhi_) | copy-start | bytes 737284
  32.2 0.8 %copy-start.3 = (f32[5,192,128]{2,1,0:T(8,128)}, f32[5,192,128]{2,1,0:T(8,128)S(1)}, u32[]{:S(2)}) copy-start(f32[5,192,128]{2,1,0:T(8,128)S(1)} %collective-permute-done.2.ylo_) | copy-start | bytes 1474564
  32.2 1.0 %copy-start.4 = (f32[5,192,128]{2,1,0:T(8,128)}, f32[5,192,128]{2,1,0:T(8,128)S(1)}, u32[]{:S(2)}) copy-start(f32[5,192,128]{2,1,0:T(8,128)S(1)} %collective-permute-done.3.yhi_) | copy-start | bytes 1474564
  33.2 29.9 %all-to-all-start = ((f32[32,64,128]{2,1,0:T(8,128)}), f32[32,64,128]{2,1,0:T(8,128)S(1)}, u32[]{:S(2)}, u32[]{:S(2)}) async-start(f32[32,64,128]{2,1,0:T(8,128)} %bitcast.23), calls=%async_computation | async-start | bytes 2097152 | tf_op jit(solution)/shard_map/all_to_all | solution.py:470
  36.9 8.8 %collective-permute-start.5 = (f32[2,5,3,3,128]{4,3,2,1,0:T(4,128)S(1)}, f32[2,5,3,3,128]{4,3,2,1,0:T(4,128)S(1)}, u32[]{:S(2)}, u32[]{:S(2)}) collective-permute-start(f32[2,5,3,3,128]{4,3,2,1,0:T(4,128)S(1)} %get-tuple-element.52), channel_id=1, source_target_pairs={{1,0},{2,1},{3,2},{4,3},{5,4},{6,5},{7,6},{0,7},{9,8},{10,9},{11,1... | collective-permute-start | bytes 138248 | tf_op jit(solution)/shard_map/ppermute | solution.py:495
  39.4 8.5 %collective-permute-start.4 = (f32[2,5,3,3,128]{4,3,2,1,0:T(4,128)S(1)}, f32[2,5,3,3,128]{4,3,2,1,0:T(4,128)S(1)}, u32[]{:S(2)}, u32[]{:S(2)}) collective-permute-start(f32[2,5,3,3,128]{4,3,2,1,0:T(4,128)S(1)} %get-tuple-element.53), channel_id=1, source_target_pairs={{0,1},{1,2},{2,3},{3,4},{4,5},{5,6},{6,7},{7,0},{8,9},{9,10},{10,1... | collective-permute-start | bytes 138248 | tf_op jit(solution)/shard_map/ppermute | solution.py:494
  45.7 2.2 %copy-start.5 = (f32[2,5,3,3,128]{4,3,2,1,0:T(4,128)}, f32[2,5,3,3,128]{4,3,2,1,0:T(4,128)S(1)}, u32[]{:S(2)}) copy-start(f32[2,5,3,3,128]{4,3,2,1,0:T(4,128)S(1)} %collective-permute-done.5.chi_) | copy-start | bytes 138244
  47.9 0.6 copy-start.6
  63.1 1.7 %copy-start = (f32[32,64,128]{2,1,0:T(8,128)}, f32[32,64,128]{2,1,0:T(8,128)S(1)}, u32[]{:S(2)}) copy-start(f32[32,64,128]{2,1,0:T(8,128)S(1)} %all-to-all-done) | copy-start | bytes 3145732
